TPU v7x, 256 devices: a whole 4x4x8 slice. The times are simulated.
256 devices in a mesh: gx: 32 (over z, y), gy: 8 (over x, core).
Axes of the slice: x: 4, y: 4, z: 8, core: 2. Of those that a mesh axis runs over, the one named last changes fastest.
Arguments:
- spins: bfloat16 [16, 128, 512, 256], P(None, 'gx', 'gy'), may hold values from -1 to 1
- couplings: int32 [6, 128, 512, 256], P(None, 'gx', 'gy'), may hold values from -1 to 1, as said below
- betas: float32 [16], replicated, may hold values from 0.25 to 1.5
- metro_uniform: bfloat16 [2, 16, 128, 512, 256], P(None, None, 'gx', 'gy'), may hold values from 0 to 1
- swap_uniform: float32 [8], replicated, may hold values from 0.8 to 1
Outputs:
- spins_out: bfloat16 [16, 128, 512, 256], P(None, 'gx', 'gy')
- energies: float32 [16], replicated
Inputs may be any that keep to these rules, and one draw needn't show every extreme that they name: Every entry is -1 or 1; couplings[3 + d] at a cell equals couplings[d] at the cell one step lower along lattice dimension d, with periodic wrap.
All inputs are finite; a program needn't handle non-finite values.
Results may differ from a plain program's by a relative error of at most 0.0085.
Values may be sent and summed in bfloat16 or wider, within the bound.
No kernel may reach another device: no remote copies, remote signals or barrier semaphores. Data moves between devices by JAX's collectives and lax.ppermute only.
A program may use at most 128 MiB of HBM per device.

v0:
```python
import functools

import jax
import jax.numpy as jnp
from jax import lax
from jax.sharding import Mesh
from jax.sharding import PartitionSpec as P

SWEEPS = 2
GX_GY = ("gx_0", "gx_1", "gy_0", "gy_1")
GX = ("gx_0", "gx_1")
GY = ("gy_0", "gy_1")


soft_width = 0.1
swap_width = 0.25
swap_gain = 64.0


def padded_2(x, sides, width):
    edges = {}
    for axis, dim in sides:
        count, length = (lax.axis_size(axis), x.shape[dim])
        up = [(i, (i + 1) % count) for i in range(count)]
        last = lax.slice_in_dim(x, length - width, length, axis=dim)
        initial = lax.slice_in_dim(x, 0, width, axis=dim)
        edges[dim] = (
            lax.ppermute(last, axis, up),
            lax.ppermute(initial, axis, [(b, a) for a, b in up]),
        )
    done = []
    for _, dim in sides:
        low, high = edges[dim]
        around = [(width, width) if d in done else (0, 0) for d in range(x.ndim)]
        x = jnp.concatenate([jnp.pad(low, around), x, jnp.pad(high, around)], axis=dim)
        done.append(dim)
    return x


def one_axis_at_a_time(x, axes):
    return functools.reduce(lax.psum, axes, x)


def full_neighbours(state):
    padded = padded_2(state, ((GX, 1), (GY, 2)), 1)
    return (padded[:, 2:, 1:-1], padded[:, :-2, 1:-1], padded[:, 1:-1, 2:], padded[:, 1:-1, :-2])


def neighbour_field(bonds, near, current):
    up_x, down_x, up_y, down_y = near
    field = bonds[0] * up_x.astype(jnp.float32) + bonds[3] * down_x.astype(jnp.float32)
    field = field + bonds[1] * up_y.astype(jnp.float32) + bonds[4] * down_y.astype(jnp.float32)
    field = field + bonds[2] * jnp.roll(current, -1, 3) + bonds[5] * jnp.roll(current, 1, 3)
    return field


def body(spins, couplings, betas, metro_uniform, swap_uniform):
    bonds = couplings.astype(jnp.float32)[:, None]
    replicas, cells_x, cells_y, cells_z = spins.shape
    shape = (cells_x, cells_y, cells_z)
    xstart = lax.axis_index(GX) * cells_x
    ystart = lax.axis_index(GY) * cells_y
    xcoord = xstart + lax.broadcasted_iota(jnp.int32, shape, 0)
    ycoord = ystart + lax.broadcasted_iota(jnp.int32, shape, 1)
    parity = (xcoord + ycoord + lax.broadcasted_iota(jnp.int32, shape, 2)) % 2
    inverse = betas[:, None, None, None]
    state = spins
    field = None
    for sweep in range(SWEEPS):
        uniform = metro_uniform[sweep].astype(jnp.float32)
        for colour in (0, 1):
            near = full_neighbours(state)
            current = state.astype(jnp.float32)
            field = neighbour_field(bonds, near, current)
            accept = jnp.exp(-inverse * jnp.maximum(2.0 * current * field, 0.0))
            weight = jax.nn.sigmoid((accept - uniform) / soft_width)
            flipped = current * (1.0 - 2.0 * weight)
            state = jnp.where(parity == colour, flipped, current).astype(jnp.bfloat16)
    current = state.astype(jnp.float32)
    partial_sum = jnp.sum(jnp.where(parity == 1, current * field, 0.0), axis=(1, 2, 3))
    total = one_axis_at_a_time(partial_sum, GX_GY)
    cell_count = cells_x * lax.axis_size(GX) * cells_y * lax.axis_size(GY) * cells_z
    energies = -total / jnp.float32(cell_count)
    delta = swap_gain * (betas[0::2] - betas[1::2]) * (energies[0::2] - energies[1::2])
    mix = jax.nn.sigmoid((jnp.minimum(delta, 0.0) - jnp.log(swap_uniform)) / swap_width)
    paired = current.reshape(replicas // 2, 2, cells_x, cells_y, cells_z)
    weight = mix[:, None, None, None]
    upper = paired[:, 0]
    lower = paired[:, 1]
    new_upper = (1.0 - weight) * upper + weight * lower
    new_lower = (1.0 - weight) * lower + weight * upper
    mixed = jnp.stack([new_upper, new_lower], axis=1).astype(jnp.bfloat16)
    return (mixed.reshape(replicas, cells_x, cells_y, cells_z), energies)


def solution(mesh):
    split = Mesh(mesh.devices.reshape(8, 4, 4, 2), ("gx_0", "gx_1", "gy_0", "gy_1"))
    return jax.shard_map(
        body,
        mesh=split,
        in_specs=(
            P(None, GX, GY, None),
            P(None, GX, GY, None),
            P(),
            P(None, None, GX, GY, None),
            P(),
        ),
        out_specs=(P(None, GX, GY, None), P()),
        check_vma=False,
    )
```

profile of v0, /device:TPU:1, one launch (start us, length us, event | category | flops | bytes accessed | tf_op | source)
XLA Modules:
  0.0 167.4 jit_solution(12810217923258802604)
XLA Ops:
  0.6 2.5 %fusion.86 = (bf16[16,1,64,256]{3,2,1,0:T(8,128)(2,1)}, bf16[16,1,64,256]{3,2,1,0:T(8,128)(2,1)}) fusion(bf16[16,4,64,256]{3,2,1,0:T(8,128)(2,1)} %param.5), kind=kLoop, calls=%fused_computation.144 | loop fusion | bytes 2097152 | tf_op jit(solution)/shard_map/slice | solution.py:26
  3.1 2.1 %collective-permute-start.1 = (bf16[16,1,64,256]{3,2,1,0:T(8,128)(2,1)}, bf16[16,1,64,256]{3,2,1,0:T(8,128)(2,1)}, u32[]{:S(2)}, u32[]{:S(2)}) collective-permute-start(bf16[16,1,64,256]{3,2,1,0:T(8,128)(2,1)} %get-tuple-element.35), channel_id=1, source_target_pairs={{0,8},{8,16},{16,24},{24,32},{32,40},{40,48},{48,56},{56,64},{64,7... | collective-permute-start | bytes 1572872 | tf_op jit(solution)/shard_map/ppermute | solution.py:28
  5.2 6.7 %collective-permute-start = (bf16[16,1,64,256]{3,2,1,0:T(8,128)(2,1)}, bf16[16,1,64,256]{3,2,1,0:T(8,128)(2,1)}, u32[]{:S(2)}, u32[]{:S(2)}) collective-permute-start(bf16[16,1,64,256]{3,2,1,0:T(8,128)(2,1)} %get-tuple-element.34), channel_id=1, source_target_pairs={{8,0},{16,8},{24,16},{32,24},{40,32},{48,40},{56,48},{64,56},{72,6... | collective-permute-start | bytes 1572872 | tf_op jit(solution)/shard_map/ppermute | solution.py:29
  12.0 1.8 %fusion.85 = (bf16[16,4,1,256]{3,2,1,0:T(2,128)(2,1)}, bf16[16,4,1,256]{3,2,1,0:T(2,128)(2,1)}) fusion(bf16[16,4,64,256]{3,2,1,0:T(8,128)(2,1)} %param.5), kind=kLoop, calls=%fused_computation.143 | loop fusion | bytes 131072 | tf_op jit(solution)/shard_map/slice | solution.py:26
  15.8 4.3 %fusion.87 = (f32[16,4,64,255]{3,2,1,0:T(8,128)}, f32[16,4,64,255]{3,2,1,0:T(8,128)}) fusion(bf16[16,4,64,256]{3,2,1,0:T(8,128)(2,1)S(1)} %copy-done), kind=kLoop, calls=%fused_computation.145 | loop fusion | bytes 16711680 | tf_op jit(solution)/shard_map/jit(_roll_static)/slice | solution.py:53
  20.1 2.4 %fusion.88 = (f32[16,4,64,1]{3,2,1,0:T(8,128)}, f32[16,4,64,1]{3,2,1,0:T(8,128)}) fusion(bf16[16,4,64,256]{3,2,1,0:T(8,128)(2,1)S(1)} %copy-done), kind=kLoop, calls=%fused_computation.146 | loop fusion | bytes 65536 | tf_op jit(solution)/shard_map/jit(_roll_static)/slice | solution.py:53
  28.8 10.7 %fusion.57 = bf16[16,4,64,256]{3,2,1,0:T(8,128)(2,1)S(1)} fusion(f32[16,4,64,255]{3,2,1,0:T(8,128)} %get-tuple-element.37, f32[16,4,64,1]{3,2,1,0:T(8,128)} %get-tuple-element.39, f32[16,4,64,1]{3,2,1,0:T(8,128)S(1)} %copy-done.2, f32[16,4,64,255]{3,2,1,0:T(8,128)} %get-tuple-element.36, bf16[16,6,64,256]{3,2,1,0:T(8,128)(2,1)S(1)} %constant_dynamic-update-slice_fusion, ...), kind=kLoop, calls=%fused_computation.76 | loop fusion | flops 53477376 | bytes 20578368 | tf_op jit(solution)/shard_map/convert_element_type | solution.py:78
  41.0 1.8 %collective-permute-start.4 = (bf16[16,1,64,256]{3,2,1,0:T(8,128)(2,1)S(1)}, bf16[16,1,64,256]{3,2,1,0:T(8,128)(2,1)S(1)}, u32[]{:S(2)}, u32[]{:S(2)}) collective-permute-start(bf16[16,1,64,256]{3,2,1,0:T(8,128)(2,1)S(1)} %get-tuple-element.27), channel_id=1, source_target_pairs={{8,0},{16,8},{24,16},{32,24},{40,32},{48,40},{56,48},{64,56},{72,6... | collective-permute-start | bytes 1572872 | tf_op jit(solution)/shard_map/ppermute | solution.py:29
  47.2 6.5 %collective-permute-done.4 = bf16[16,1,64,256]{3,2,1,0:T(8,128)(2,1)S(1)} collective-permute-done((bf16[16,1,64,256]{3,2,1,0:T(8,128)(2,1)S(1)}, bf16[16,1,64,256]{3,2,1,0:T(8,128)(2,1)S(1)}, u32[]{:S(2)}, u32[]{:S(2)}) %collective-permute-start.4) | collective-permute-done | bytes 524320 | tf_op jit(solution)/shard_map/ppermute | solution.py:29
  53.7 5.1 %collective-permute-done.5 = bf16[16,1,64,256]{3,2,1,0:T(8,128)(2,1)S(1)} collective-permute-done((bf16[16,1,64,256]{3,2,1,0:T(8,128)(2,1)S(1)}, bf16[16,1,64,256]{3,2,1,0:T(8,128)(2,1)S(1)}, u32[]{:S(2)}, u32[]{:S(2)}) %collective-permute-start.5) | collective-permute-done | bytes 524320 | tf_op jit(solution)/shard_map/ppermute | solution.py:28
  58.8 9.6 %fusion.58 = bf16[16,4,64,256]{3,2,1,0:T(8,128)(2,1)S(1)} fusion(f32[16,4,64,255]{3,2,1,0:T(8,128)S(1)} %get-tuple-element.29, f32[16,4,64,1]{3,2,1,0:T(8,128)S(1)} %get-tuple-element.31, f32[16,4,64,1]{3,2,1,0:T(8,128)S(1)} %get-tuple-element.30, f32[16,4,64,255]{3,2,1,0:T(8,128)S(1)} %get-tuple-element.28, ...), kind=kLoop, calls=%fused_computation.77 | loop fusion | flops 61865984 | bytes 17432640 | tf_op jit(solution)/shard_map/convert_element_type | solution.py:78
  71.4 2.2 %collective-permute-start.10 = (bf16[16,4,1,256]{3,2,1,0:T(2,128)(2,1)S(1)}, bf16[16,4,1,256]{3,2,1,0:T(2,128)(2,1)S(1)}, u32[]{:S(2)}, u32[]{:S(2)}) collective-permute-start(bf16[16,4,1,256]{3,2,1,0:T(2,128)(2,1)S(1)} %get-tuple-element.16), channel_id=1, source_target_pairs={{1,0},{2,1},{3,2},{4,3},{5,4},{6,5},{7,6},{0,7},{9,8},{10,9},{11,1... | collective-permute-start | bytes 98312 | tf_op jit(solution)/shard_map/ppermute | solution.py:29
  77.0 4.6 %collective-permute-done.8 = bf16[16,1,64,256]{3,2,1,0:T(8,128)(2,1)S(1)} collective-permute-done((bf16[16,1,64,256]{3,2,1,0:T(8,128)(2,1)S(1)}, bf16[16,1,64,256]{3,2,1,0:T(8,128)(2,1)S(1)}, u32[]{:S(2)}, u32[]{:S(2)}) %collective-permute-start.8) | collective-permute-done | bytes 524320 | tf_op jit(solution)/shard_map/ppermute | solution.py:29
  81.7 3.6 %collective-permute-done.9 = bf16[16,1,64,256]{3,2,1,0:T(8,128)(2,1)S(1)} collective-permute-done((bf16[16,1,64,256]{3,2,1,0:T(8,128)(2,1)S(1)}, bf16[16,1,64,256]{3,2,1,0:T(8,128)(2,1)S(1)}, u32[]{:S(2)}, u32[]{:S(2)}) %collective-permute-start.9) | collective-permute-done | bytes 524320 | tf_op jit(solution)/shard_map/ppermute | solution.py:28
  85.3 9.5 %fusion.59 = bf16[16,4,64,256]{3,2,1,0:T(8,128)(2,1)S(1)} fusion(f32[16,4,64,255]{3,2,1,0:T(8,128)S(1)} %get-tuple-element.21, f32[16,4,64,1]{3,2,1,0:T(8,128)S(1)} %get-tuple-element.23, f32[16,4,64,1]{3,2,1,0:T(8,128)S(1)} %get-tuple-element.22, f32[16,4,64,255]{3,2,1,0:T(8,128)S(1)} %get-tuple-element.20, ...), kind=kLoop, calls=%fused_computation.78 | loop fusion | flops 61865984 | bytes 17432640 | tf_op jit(solution)/shard_map/convert_element_type | solution.py:78
  97.9 3.1 %collective-permute-start.14 = (bf16[16,4,1,256]{3,2,1,0:T(2,128)(2,1)S(1)}, bf16[16,4,1,256]{3,2,1,0:T(2,128)(2,1)S(1)}, u32[]{:S(2)}, u32[]{:S(2)}) collective-permute-start(bf16[16,4,1,256]{3,2,1,0:T(2,128)(2,1)S(1)} %get-tuple-element.8), channel_id=1, source_target_pairs={{1,0},{2,1},{3,2},{4,3},{5,4},{6,5},{7,6},{0,7},{9,8},{10,9},{11,1... | collective-permute-start | bytes 98312 | tf_op jit(solution)/shard_map/ppermute | solution.py:29
  104.4 2.9 %collective-permute-done.12 = bf16[16,1,64,256]{3,2,1,0:T(8,128)(2,1)S(1)} collective-permute-done((bf16[16,1,64,256]{3,2,1,0:T(8,128)(2,1)S(1)}, bf16[16,1,64,256]{3,2,1,0:T(8,128)(2,1)S(1)}, u32[]{:S(2)}, u32[]{:S(2)}) %collective-permute-start.12) | collective-permute-done | bytes 524320 | tf_op jit(solution)/shard_map/ppermute | solution.py:29
  107.3 3.6 %collective-permute-done.13 = bf16[16,1,64,256]{3,2,1,0:T(8,128)(2,1)S(1)} collective-permute-done((bf16[16,1,64,256]{3,2,1,0:T(8,128)(2,1)S(1)}, bf16[16,1,64,256]{3,2,1,0:T(8,128)(2,1)S(1)}, u32[]{:S(2)}, u32[]{:S(2)}) %collective-permute-start.13) | collective-permute-done | bytes 524320 | tf_op jit(solution)/shard_map/ppermute | solution.py:28
  110.9 11.2 %select_reduce_fusion = (f32[16]{0:T(128)S(1)}, f32[16,4,64,256]{3,2,1,0:T(8,128)}) fusion(pred[4,64,256]{2,1,0:T(8,128)(4,1)S(1)} %get-tuple-element.46, bf16[2,16,4,64,256]{4,3,2,1,0:T(8,128)(2,1)S(1)} %copy-done.1, f32[16]{0:T(128)S(1)} %neg.25, bf16[16,4,64,256]{3,2,1,0:T(8,128)(2,1)S(1)} %fusion.59, f32[16,4,64,255]{3,2,1,0:T(8,128)S(1)} %get-tuple-element.14, ...), kind=kLoop, calls=%fused_computation.74 | loop fusion | flops 66060272 | bytes 19529856 | tf_op jit(solution)/shard_map/reduce_sum | solution.py:80
  122.2 10.7 %psum.28 = f32[16]{0:T(128)S(1)} all-reduce(f32[16]{0:T(128)S(1)} %get-tuple-element.4), channel_id=1, replica_groups=mesh['gx_0'=8,'gx_1'=4,'gy_0'=4,'gy_1'=2] {'gx_0'}, use_global_device_ids=true, to_apply=%region_1.2 | all-reduce | flops 16 | bytes 128 | tf_op jit(solution)/shard_map/psum | solution.py:41
  132.9 6.5 %psum.29 = f32[16]{0:T(128)S(1)} all-reduce(f32[16]{0:T(128)S(1)} %psum.28), channel_id=1, replica_groups=mesh['gx_0'=8,'gx_1'=4,'gy_0'=4,'gy_1'=2] {'gx_1'}, use_global_device_ids=true, to_apply=%region_2.3 | all-reduce | flops 16 | bytes 128 | tf_op jit(solution)/shard_map/psum | solution.py:41
  139.5 11.3 %psum.30 = f32[16]{0:T(128)S(1)} all-reduce(f32[16]{0:T(128)S(1)} %psum.29), channel_id=1, replica_groups=mesh['gx_0'=8,'gx_1'=4,'gy_0'=4,'gy_1'=2] {'gy_0'}, use_global_device_ids=true, to_apply=%region_3.4 | all-reduce | flops 16 | bytes 128 | tf_op jit(solution)/shard_map/psum | solution.py:41
  150.8 11.9 %psum.31 = f32[16]{0:T(128)S(1)} all-reduce(f32[16]{0:T(128)S(1)} %psum.30), channel_id=1, replica_groups=mesh['gx_0'=8,'gx_1'=4,'gy_0'=4,'gy_1'=2] {'gy_1'}, use_global_device_ids=true, to_apply=%region_4.5 | all-reduce | flops 16 | bytes 128 | tf_op jit(solution)/shard_map/psum | solution.py:41
  163.0 2.9 %add_convert_fusion.1 = (bf16[8,1,4,64,256]{4,3,2,1,0:T(8,128)(2,1)S(1)}, bf16[8,1,4,64,256]{4,3,2,1,0:T(8,128)(2,1)S(1)}) fusion(f32[8,2,4,64,256]{4,3,2,1,0:T(8,128)} %bitcast.25, f32[8]{0:T(128)S(1)} %get-tuple-element.3, f32[8]{0:T(128)S(1)} %get-tuple-element.2), kind=kLoop, calls=%fused_computation.109 | loop fusion | flops 4194304 | bytes 6291520 | tf_op jit(solution)/shard_map/convert.2
  (67 shorter events, 28.6 us)
Async XLA Ops:
  0.6 15.2 %copy-start = (bf16[16,4,64,256]{3,2,1,0:T(8,128)(2,1)S(1)}, bf16[16,4,64,256]{3,2,1,0:T(8,128)(2,1)}, u32[]{:S(2)}) copy-start(bf16[16,4,64,256]{3,2,1,0:T(8,128)(2,1)} %param.5) | copy-start | bytes 6291460
  3.1 22.8 %collective-permute-start.1 = (bf16[16,1,64,256]{3,2,1,0:T(8,128)(2,1)}, bf16[16,1,64,256]{3,2,1,0:T(8,128)(2,1)}, u32[]{:S(2)}, u32[]{:S(2)}) collective-permute-start(bf16[16,1,64,256]{3,2,1,0:T(8,128)(2,1)} %get-tuple-element.35), channel_id=1, source_target_pairs={{0,8},{8,16},{16,24},{24,32},{32,40},{40,48},{48,56},{56,64},{64,7... | collective-permute-start | bytes 1572872 | tf_op jit(solution)/shard_map/ppermute | solution.py:28
  5.2 22.1 %collective-permute-start = (bf16[16,1,64,256]{3,2,1,0:T(8,128)(2,1)}, bf16[16,1,64,256]{3,2,1,0:T(8,128)(2,1)}, u32[]{:S(2)}, u32[]{:S(2)}) collective-permute-start(bf16[16,1,64,256]{3,2,1,0:T(8,128)(2,1)} %get-tuple-element.34), channel_id=1, source_target_pairs={{8,0},{16,8},{24,16},{32,24},{40,32},{48,40},{56,48},{64,56},{72,6... | collective-permute-start | bytes 1572872 | tf_op jit(solution)/shard_map/ppermute | solution.py:29
  13.7 15.0 %collective-permute-start.2 = (bf16[16,4,1,256]{3,2,1,0:T(2,128)(2,1)}, bf16[16,4,1,256]{3,2,1,0:T(2,128)(2,1)S(1)}, u32[]{:S(2)}, u32[]{:S(2)}) collective-permute-start(bf16[16,4,1,256]{3,2,1,0:T(2,128)(2,1)} %get-tuple-element.32), channel_id=1, source_target_pairs={{1,0},{2,1},{3,2},{4,3},{5,4},{6,5},{7,6},{0,7},{9,8},{10,9},{11,1... | collective-permute-start | bytes 98312 | tf_op jit(solution)/shard_map/ppermute | solution.py:29
  14.7 14.0 %collective-permute-start.3 = (bf16[16,4,1,256]{3,2,1,0:T(2,128)(2,1)}, bf16[16,4,1,256]{3,2,1,0:T(2,128)(2,1)S(1)}, u32[]{:S(2)}, u32[]{:S(2)}) collective-permute-start(bf16[16,4,1,256]{3,2,1,0:T(2,128)(2,1)} %get-tuple-element.33), channel_id=1, source_target_pairs={{0,1},{1,2},{2,3},{3,4},{4,5},{5,6},{6,7},{7,0},{8,9},{9,10},{10,1... | collective-permute-start | bytes 98312 | tf_op jit(solution)/shard_map/ppermute | solution.py:28
  20.1 2.4 %copy-start.4 = (s32[6,4,64,256]{3,2,1,0:T(8,128)S(1)}, s32[6,4,64,256]{3,2,1,0:T(8,128)}, u32[]{:S(2)}) copy-start(s32[6,4,64,256]{3,2,1,0:T(8,128)} %param.6) | copy-start | bytes 4718596
  25.6 3.1 %copy-start.1 = (bf16[2,16,4,64,256]{4,3,2,1,0:T(8,128)(2,1)S(1)}, bf16[2,16,4,64,256]{4,3,2,1,0:T(8,128)(2,1)}, u32[]{:S(2)}) copy-start(bf16[2,16,4,64,256]{4,3,2,1,0:T(8,128)(2,1)} %param.8) | copy-start | bytes 12582916
  25.6 3.1 %copy-start.2 = (f32[16,4,64,1]{3,2,1,0:T(8,128)S(1)}, f32[16,4,64,1]{3,2,1,0:T(8,128)}, u32[]{:S(2)}) copy-start(f32[16,4,64,1]{3,2,1,0:T(8,128)} %get-tuple-element.38) | copy-start | bytes 49156
  41.0 12.7 %collective-permute-start.4 = (bf16[16,1,64,256]{3,2,1,0:T(8,128)(2,1)S(1)}, bf16[16,1,64,256]{3,2,1,0:T(8,128)(2,1)S(1)}, u32[]{:S(2)}, u32[]{:S(2)}) collective-permute-start(bf16[16,1,64,256]{3,2,1,0:T(8,128)(2,1)S(1)} %get-tuple-element.27), channel_id=1, source_target_pairs={{8,0},{16,8},{24,16},{32,24},{40,32},{48,40},{56,48},{64,56},{72,6... | collective-permute-start | bytes 1572872 | tf_op jit(solution)/shard_map/ppermute | solution.py:29
  42.8 16.0 %collective-permute-start.5 = (bf16[16,1,64,256]{3,2,1,0:T(8,128)(2,1)S(1)}, bf16[16,1,64,256]{3,2,1,0:T(8,128)(2,1)S(1)}, u32[]{:S(2)}, u32[]{:S(2)}) collective-permute-start(bf16[16,1,64,256]{3,2,1,0:T(8,128)(2,1)S(1)} %get-tuple-element.26), channel_id=1, source_target_pairs={{0,8},{8,16},{16,24},{24,32},{32,40},{40,48},{48,56},{56,64},{64,7... | collective-permute-start | bytes 1572872 | tf_op jit(solution)/shard_map/ppermute | solution.py:28
  42.9 4.2 %collective-permute-start.6 = (bf16[16,4,1,256]{3,2,1,0:T(2,128)(2,1)S(1)}, bf16[16,4,1,256]{3,2,1,0:T(2,128)(2,1)S(1)}, u32[]{:S(2)}, u32[]{:S(2)}) collective-permute-start(bf16[16,4,1,256]{3,2,1,0:T(2,128)(2,1)S(1)} %get-tuple-element.24), channel_id=1, source_target_pairs={{1,0},{2,1},{3,2},{4,3},{5,4},{6,5},{7,6},{0,7},{9,8},{10,9},{11,1... | collective-permute-start | bytes 98312 | tf_op jit(solution)/shard_map/ppermute | solution.py:29
  44.0 14.8 %copy-start.3 = (f32[4,64,256]{2,1,0:T(8,128)S(1)}, f32[4,64,256]{2,1,0:T(8,128)}, u32[]{:S(2)}) copy-start(f32[4,64,256]{2,1,0:T(8,128)} %get-tuple-element.45) | copy-start | bytes 786436
  44.0 3.1 %collective-permute-start.7 = (bf16[16,4,1,256]{3,2,1,0:T(2,128)(2,1)S(1)}, bf16[16,4,1,256]{3,2,1,0:T(2,128)(2,1)S(1)}, u32[]{:S(2)}, u32[]{:S(2)}) collective-permute-start(bf16[16,4,1,256]{3,2,1,0:T(2,128)(2,1)S(1)} %get-tuple-element.25), channel_id=1, source_target_pairs={{0,1},{1,2},{2,3},{3,4},{4,5},{5,6},{6,7},{7,0},{8,9},{9,10},{10,1... | collective-permute-start | bytes 98312 | tf_op jit(solution)/shard_map/ppermute | solution.py:28
  69.8 11.9 %collective-permute-start.8 = (bf16[16,1,64,256]{3,2,1,0:T(8,128)(2,1)S(1)}, bf16[16,1,64,256]{3,2,1,0:T(8,128)(2,1)S(1)}, u32[]{:S(2)}, u32[]{:S(2)}) collective-permute-start(bf16[16,1,64,256]{3,2,1,0:T(8,128)(2,1)S(1)} %get-tuple-element.19), channel_id=1, source_target_pairs={{8,0},{16,8},{24,16},{32,24},{40,32},{48,40},{56,48},{64,56},{72,6... | collective-permute-start | bytes 1572872 | tf_op jit(solution)/shard_map/ppermute | solution.py:29
  70.1 15.1 %collective-permute-start.9 = (bf16[16,1,64,256]{3,2,1,0:T(8,128)(2,1)S(1)}, bf16[16,1,64,256]{3,2,1,0:T(8,128)(2,1)S(1)}, u32[]{:S(2)}, u32[]{:S(2)}) collective-permute-start(bf16[16,1,64,256]{3,2,1,0:T(8,128)(2,1)S(1)} %get-tuple-element.18), channel_id=1, source_target_pairs={{0,8},{8,16},{16,24},{24,32},{32,40},{40,48},{48,56},{56,64},{64,7... | collective-permute-start | bytes 1572872 | tf_op jit(solution)/shard_map/ppermute | solution.py:28
  71.4 5.6 %collective-permute-start.10 = (bf16[16,4,1,256]{3,2,1,0:T(2,128)(2,1)S(1)}, bf16[16,4,1,256]{3,2,1,0:T(2,128)(2,1)S(1)}, u32[]{:S(2)}, u32[]{:S(2)}) collective-permute-start(bf16[16,4,1,256]{3,2,1,0:T(2,128)(2,1)S(1)} %get-tuple-element.16), channel_id=1, source_target_pairs={{1,0},{2,1},{3,2},{4,3},{5,4},{6,5},{7,6},{0,7},{9,8},{10,9},{11,1... | collective-permute-start | bytes 98312 | tf_op jit(solution)/shard_map/ppermute | solution.py:29
  73.7 3.3 %collective-permute-start.11 = (bf16[16,4,1,256]{3,2,1,0:T(2,128)(2,1)S(1)}, bf16[16,4,1,256]{3,2,1,0:T(2,128)(2,1)S(1)}, u32[]{:S(2)}, u32[]{:S(2)}) collective-permute-start(bf16[16,4,1,256]{3,2,1,0:T(2,128)(2,1)S(1)} %get-tuple-element.17), channel_id=1, source_target_pairs={{0,1},{1,2},{2,3},{3,4},{4,5},{5,6},{6,7},{7,0},{8,9},{9,10},{10,1... | collective-permute-start | bytes 98312 | tf_op jit(solution)/shard_map/ppermute | solution.py:28
  96.3 11.0 %collective-permute-start.12 = (bf16[16,1,64,256]{3,2,1,0:T(8,128)(2,1)S(1)}, bf16[16,1,64,256]{3,2,1,0:T(8,128)(2,1)S(1)}, u32[]{:S(2)}, u32[]{:S(2)}) collective-permute-start(bf16[16,1,64,256]{3,2,1,0:T(8,128)(2,1)S(1)} %get-tuple-element.11), channel_id=1, source_target_pairs={{8,0},{16,8},{24,16},{32,24},{40,32},{48,40},{56,48},{64,56},{72,6... | collective-permute-start | bytes 1572872 | tf_op jit(solution)/shard_map/ppermute | solution.py:29
  96.6 14.3 %collective-permute-start.13 = (bf16[16,1,64,256]{3,2,1,0:T(8,128)(2,1)S(1)}, bf16[16,1,64,256]{3,2,1,0:T(8,128)(2,1)S(1)}, u32[]{:S(2)}, u32[]{:S(2)}) collective-permute-start(bf16[16,1,64,256]{3,2,1,0:T(8,128)(2,1)S(1)} %get-tuple-element.10), channel_id=1, source_target_pairs={{0,8},{8,16},{16,24},{24,32},{32,40},{40,48},{48,56},{56,64},{64,7... | collective-permute-start | bytes 1572872 | tf_op jit(solution)/shard_map/ppermute | solution.py:28
  97.9 6.5 %collective-permute-start.14 = (bf16[16,4,1,256]{3,2,1,0:T(2,128)(2,1)S(1)}, bf16[16,4,1,256]{3,2,1,0:T(2,128)(2,1)S(1)}, u32[]{:S(2)}, u32[]{:S(2)}) collective-permute-start(bf16[16,4,1,256]{3,2,1,0:T(2,128)(2,1)S(1)} %get-tuple-element.8), channel_id=1, source_target_pairs={{1,0},{2,1},{3,2},{4,3},{5,4},{6,5},{7,6},{0,7},{9,8},{10,9},{11,1... | collective-permute-start | bytes 98312 | tf_op jit(solution)/shard_map/ppermute | solution.py:29
  101.0 3.4 %collective-permute-start.15 = (bf16[16,4,1,256]{3,2,1,0:T(2,128)(2,1)S(1)}, bf16[16,4,1,256]{3,2,1,0:T(2,128)(2,1)S(1)}, u32[]{:S(2)}, u32[]{:S(2)}) collective-permute-start(bf16[16,4,1,256]{3,2,1,0:T(2,128)(2,1)S(1)} %get-tuple-element.9), channel_id=1, source_target_pairs={{0,1},{1,2},{2,3},{3,4},{4,5},{5,6},{6,7},{7,0},{8,9},{9,10},{10,1... | collective-permute-start | bytes 98312 | tf_op jit(solution)/shard_map/ppermute | solution.py:28
  110.9 52.0 %copy-start.5 = (f32[8]{0:T(128)S(1)}, f32[8]{0:T(128)}, u32[]{:S(2)}) copy-start(f32[8]{0:T(128)} %param.9) | copy-start | bytes 100
  110.9 52.0 %copy-start.6 = (f32[8]{0:T(128)S(1)}, f32[8]{0:T(128)}, u32[]{:S(2)}) copy-start(f32[8]{0:T(128)} %slice.231) | copy-start | bytes 100
  162.7 4.7 %copy-start.8 = (f32[16]{0:T(128)}, f32[16]{0:T(128)S(1)}, u32[]{:S(2)}) copy-start(f32[16]{0:T(128)S(1)} %negate_multiply_fusion) | copy-start | bytes 196
  (1 other events, 1.1 us)
where the time goes:
time: 168 us; the launch traced here: 167 us
  other arithmetic  45.9 us (27%)
  blocking collectives  40.5 us (24%)
  waiting for transfers between devices  31.4 us (19%)
  starting transfers between devices  25.4 us (15%)
  local copies, waits for them, and re-layouts  23.3 us (14%)
    psum x4, blocking collectives, one_axis_at_a_time(): return functools.reduce(lax.psum, axes, x)  40.5 us
    convert_element_type x3, other arithmetic, body(): state = jnp.where(parity == colour, flipped, current).astype(jnp.bfloat16)  29.8 us
    ppermute x8, waiting for transfers between devices, padded_2(): lax.ppermute(initial, axis, [(b, a) for a, b in up])  19 us
    ppermute x8, starting transfers between devices, padded_2(): lax.ppermute(initial, axis, [(b, a) for a, b in up])  16.7 us
    ppermute x8, waiting for transfers between devices, padded_2(): lax.ppermute(last, axis, up)  12.4 us
    reduce_sum x1, other arithmetic, body(): jnp.sum(jnp.where(parity == 1, current * field, 0.0), axis=(1, 2, 3))  11.2 us
    slice x6, local copies, waits for them, and re-layouts, neighbour_field(): jnp.roll(current, -1, 3)  10.5 us
    ppermute x8, starting transfers between devices, padded_2(): lax.ppermute(last, axis, up)  8.67 us
  transfers between devices with their start and end apart: 16, of which 10 were waited for; matrix products, arithmetic and copies ran while one was open for 10% of the time, Pallas kernels for 0%

commit v1 on v0

v1 whole, which is shorter than its diff:
```python
import functools
import math

import jax
import jax.numpy as jnp
from jax import lax
from jax.experimental import pallas as pl
from jax.experimental.pallas import tpu as pltpu
from jax.sharding import PartitionSpec as P

R = 16
CX, CY, NZ = 4, 64, 256
HALF = NZ // 2
PAD = 8
GROUPS = 2
RG = R // GROUPS
LOG2E = math.log2(math.e)
F32 = jnp.float32
BF16 = jnp.bfloat16
VMEM_LIMIT = 24 * 1024 * 1024

swap_width = 0.25
swap_gain = 64.0

VM = pl.BlockSpec(memory_space=pltpu.VMEM)
SM = pl.BlockSpec(memory_space=pltpu.SMEM)
HB = pl.BlockSpec(memory_space=pl.ANY)


def vm(shape, dtype):
    return pltpu.VMEM(shape, dtype)


def params(limit=VMEM_LIMIT):
    return pltpu.CompilerParams(vmem_limit_bytes=limit)


def cost(ops, moved):
    return pl.CostEstimate(flops=ops, bytes_accessed=moved, transcendentals=0)


def split_matrix():
    row = lax.broadcasted_iota(jnp.int32, (NZ, NZ), 0)
    col = lax.broadcasted_iota(jnp.int32, (NZ, NZ), 1)
    wanted = jnp.where(col < HALF, 2 * col, 2 * (col - HALF) + 1)
    return (row == wanted).astype(F32).astype(BF16)


def join_matrix():
    row = lax.broadcasted_iota(jnp.int32, (NZ, NZ), 0)
    col = lax.broadcasted_iota(jnp.int32, (NZ, NZ), 1)
    wanted = jnp.where(row < HALF, 2 * row, 2 * (row - HALF) + 1)
    return (col == wanted).astype(F32).astype(BF16)


def odd_rows(rows=CY):
    return lax.broadcasted_iota(jnp.int32, (rows, HALF), 0) % 2 == 1


def by_colour(even, odd, x, odd_row):
    if x % 2 == 0:
        return jnp.where(odd_row, odd, even), jnp.where(odd_row, even, odd)
    return jnp.where(odd_row, even, odd), jnp.where(odd_row, odd, even)


def split_spins(spins_ref, *refs):
    a0s, a1s = refs[:GROUPS], refs[GROUPS : 2 * GROUPS]
    sends = refs[2 * GROUPS : 6 * GROUPS]
    buf, sems = refs[6 * GROUPS :]
    copies = []
    for g in range(GROUPS):
        copies.append(
            pltpu.make_async_copy(spins_ref.at[pl.ds(g * RG, RG)], buf.at[pl.ds(g * RG, RG)], sems.at[g])
        )
        copies[-1].start()
    matrix = split_matrix()
    odd_row = odd_rows()
    for g in range(GROUPS):
        copies[g].wait()
        a0, a1 = a0s[g], a1s[g]
        xlo, xhi, ylo, yhi = sends[4 * g : 4 * g + 4]

        @pl.loop(0, RG)
        def _(r):
            cells = buf[g * RG + r].reshape(CX * CY, NZ)
            parts = jnp.dot(cells, matrix, preferred_element_type=F32)
            for x in range(CX):
                rows = parts[x * CY : (x + 1) * CY]
                c0, c1 = by_colour(rows[:, :HALF], rows[:, HALF:], x, odd_row)
                a0[r, x, PAD : PAD + CY, :] = c0
                a1[r, x, PAD : PAD + CY, :] = c1
                ylo[r, x : x + 1, :] = c1[:1]
                yhi[r, x : x + 1, :] = c1[CY - 1 :]
                if x == 0:
                    xlo[r] = c1.astype(BF16)
                if x == CX - 1:
                    xhi[r] = c1.astype(BF16)


def send_shapes():
    return [
        jax.ShapeDtypeStruct((RG, CY, HALF), BF16),
        jax.ShapeDtypeStruct((RG, CY, HALF), BF16),
        jax.ShapeDtypeStruct((RG, CX, HALF), F32),
        jax.ShapeDtypeStruct((RG, CX, HALF), F32),
    ]


def state_shape():
    return vm((RG, CX, CY + 2 * PAD, HALF), F32)


def run_split_spins(spins):
    out = pl.pallas_call(
        split_spins,
        out_shape=[state_shape()] * (2 * GROUPS) + send_shapes() * GROUPS,
        in_specs=[HB],
        out_specs=[VM] * (6 * GROUPS),
        scratch_shapes=[pltpu.VMEM((R, CX, CY, NZ), BF16), pltpu.SemaphoreType.DMA((GROUPS,))],
        compiler_params=params(),
        cost_estimate=cost(10**8, 2 * 2**20),
        name="split_spins",
    )(spins)
    a0 = list(out[:GROUPS])
    a1 = list(out[GROUPS : 2 * GROUPS])
    sends = [list(out[2 * GROUPS + 4 * g : 2 * GROUPS + 4 * g + 4]) for g in range(GROUPS)]
    return a0, a1, sends


def split_draws(sweep, with_bonds, *refs):
    refs = list(refs)
    bonds_ref = refs.pop(0) if with_bonds else None
    uniform_ref = refs.pop(0)
    u0s, u1s = refs[:GROUPS], refs[GROUPS : 2 * GROUPS]
    del refs[: 2 * GROUPS]
    outs = [refs.pop(0), refs.pop(0)] if with_bonds else None
    bond_buf = refs.pop(0) if with_bonds else None
    buf, sems = refs
    copies = []
    if with_bonds:
        bond_copy = pltpu.make_async_copy(bonds_ref, bond_buf, sems.at[GROUPS])
        bond_copy.start()
    for g in range(GROUPS):
        copies.append(
            pltpu.make_async_copy(uniform_ref.at[sweep, pl.ds(g * RG, RG)], buf.at[pl.ds(g * RG, RG)], sems.at[g])
        )
        copies[-1].start()
    matrix = split_matrix()
    odd_row = odd_rows()
    if with_bonds:
        bond_copy.wait()
        for x in range(CX):
            halves = []
            for k in range(6):
                cells = bond_buf[k, x].astype(F32).astype(BF16)
                parts = jnp.dot(cells, matrix, preferred_element_type=F32)
                halves.append((parts[:, :HALF], parts[:, HALF:]))
            for place, k in enumerate((0, 3, 1, 4)):
                c0, c1 = by_colour(*halves[k], x, odd_row)
                outs[0][place, x] = c0
                outs[1][place, x] = c1
            for place, (k, m) in enumerate(((2, 5), (5, 2))):
                c0, c1 = by_colour(halves[k][0], halves[m][1], x, odd_row)
                outs[0][4 + place, x] = c0
                outs[1][4 + place, x] = c1
    for g in range(GROUPS):
        copies[g].wait()
        u0, u1 = u0s[g], u1s[g]

        @pl.loop(0, RG)
        def _(r):
            cells = buf[g * RG + r].reshape(CX * CY, NZ)
            parts = jnp.dot(cells, matrix, preferred_element_type=F32) * 5.0
            for x in range(CX):
                rows = parts[x * CY : (x + 1) * CY]
                c0, c1 = by_colour(rows[:, :HALF], rows[:, HALF:], x, odd_row)
                u0[r, x] = c0
                u1[r, x] = c1


def run_split_draws(sweep, couplings, uniform):
    with_bonds = couplings is not None
    bond_out = [vm((6, CX, CY, HALF), F32)] * 2 if with_bonds else []
    bond_scratch = [pltpu.VMEM((6, CX, CY, NZ), jnp.int32)] if with_bonds else []
    out = pl.pallas_call(
        functools.partial(split_draws, sweep, with_bonds),
        out_shape=[vm((RG, CX, CY, HALF), F32)] * (2 * GROUPS) + bond_out,
        in_specs=[HB] * (2 if with_bonds else 1),
        out_specs=[VM] * (2 * GROUPS + len(bond_out)),
        scratch_shapes=bond_scratch
        + [pltpu.VMEM((R, CX, CY, NZ), BF16), pltpu.SemaphoreType.DMA((GROUPS + 1,))],
        compiler_params=params(),
        cost_estimate=cost(10**8, 2 * 2**20),
        name=f"split_draws_{sweep}",
    )(*([couplings] if with_bonds else []), uniform)
    return list(out[:GROUPS]), list(out[GROUPS : 2 * GROUPS]), list(out[2 * GROUPS :])


def half_sweep(colour, last, scale_ref, own_in, other_in, u_ref, bonds_ref, xlo_ref, xhi_ref, ylo_ref, yhi_ref, *outs):
    own, other = outs[:2]
    if last:
        energy = outs[2]
    else:
        sxlo, sxhi, sylo, syhi = outs[2:]

    @pl.loop(0, RG)
    def _(r):
        for x in range(CX):
            other[r, x, PAD - 1 : PAD, :] = ylo_ref[r, x : x + 1, :]
            other[r, x, PAD + CY : PAD + CY + 1, :] = yhi_ref[r, x : x + 1, :]

    tile = 16
    odd_row = odd_rows(tile)

    @pl.loop(0, RG // 2)
    def _(pair):
        sums = [jnp.zeros((tile, HALF), F32) for _ in range(2)]
        for x in range(CX):
            for y in range(0, CY, tile):
                bonds = [bonds_ref[k, x, y : y + tile, :] for k in range(6)]
                for i in range(2):
                    r = pair * 2 + i

                    def near(dx, dy):
                        at = x + dx
                        if at < 0:
                            return xlo_ref[r, y : y + tile, :].astype(F32)
                        if at >= CX:
                            return xhi_ref[r, y : y + tile, :].astype(F32)
                        return other[r, at, PAD + y + dy : PAD + y + dy + tile, :]

                    same = near(0, 0)
                    below, above = pltpu.roll(same, 1, 1), pltpu.roll(same, HALF - 1, 1)
                    if (colour + x) % 2 == 0:
                        beside = jnp.where(odd_row, above, below)
                    else:
                        beside = jnp.where(odd_row, below, above)
                    field = bonds[0] * near(1, 0) + bonds[1] * near(-1, 0)
                    field = field + (bonds[2] * near(0, 1) + bonds[3] * near(0, -1))
                    field = field + (bonds[4] * same + bonds[5] * beside)
                    spin = own[r, x, PAD + y : PAD + y + tile, :]
                    accept = jnp.exp2(jnp.minimum(spin * field * scale_ref[r], 0.0))
                    new = (spin * jnp.tanh(u_ref[r, x, y : y + tile, :] - 5.0 * accept)).astype(BF16)
                    wide = new.astype(F32)
                    own[r, x, PAD + y : PAD + y + tile, :] = wide
                    if last:
                        sums[i] = sums[i] + wide * field
                    else:
                        if x == 0:
                            sxlo[r, y : y + tile, :] = new
                        if x == CX - 1:
                            sxhi[r, y : y + tile, :] = new
                        if y == 0:
                            sylo[r, x : x + 1, :] = wide[:1]
                        if y == CY - tile:
                            syhi[r, x : x + 1, :] = wide[tile - 1 :]
        if last:
            for i in range(2):
                energy[pair * 2 + i] = sums[i][:8] + sums[i][8:]


def run_half_sweep(colour, last, scale, own, other, u, bonds, halos, name):
    extra = [jax.ShapeDtypeStruct((RG, 8, HALF), F32)] if last else send_shapes()
    out = pl.pallas_call(
        functools.partial(half_sweep, colour, last),
        out_shape=[state_shape()] * 2 + extra,
        in_specs=[SM] + [VM] * 8,
        out_specs=[VM] * (2 + len(extra)),
        input_output_aliases={1: 0, 2: 1},
        compiler_params=params(),
        cost_estimate=cost(10**8, 2 * 2**20),
        name=name,
    )(scale, own, other, u, bonds, *halos)
    return out[0], out[1], list(out[2:])


def mix_and_join(mix_ref, *refs):
    a0s, a1s = refs[:GROUPS], refs[GROUPS : 2 * GROUPS]
    out_ref, buf, sems = refs[2 * GROUPS :]
    matrix = join_matrix()
    odd_row = odd_rows()
    copies = []
    for g in range(GROUPS):

        @pl.loop(0, RG // 2)
        def _(pair):
            weight = mix_ref[g * (RG // 2) + pair]
            keep = 1.0 - weight
            r = pair * 2
            for x in range(CX):
                new = [[], []]
                for state in (a0s[g], a1s[g]):
                    upper = state[r, x, PAD : PAD + CY, :]
                    lower = state[r + 1, x, PAD : PAD + CY, :]
                    new[0].append(keep * upper + weight * lower)
                    new[1].append(keep * lower + weight * upper)
                for i in range(2):
                    even, odd = by_colour(*new[i], x, odd_row)
                    cells = jnp.concatenate([even.astype(BF16), odd.astype(BF16)], axis=1)
                    buf[g * RG + r + i, x] = jnp.dot(cells, matrix, preferred_element_type=F32).astype(BF16)

        copies.append(
            pltpu.make_async_copy(buf.at[pl.ds(g * RG, RG)], out_ref.at[pl.ds(g * RG, RG)], sems.at[g])
        )
        copies[-1].start()
    for copy in copies:
        copy.wait()


def run_mix_and_join(mix, a0, a1):
    return pl.pallas_call(
        mix_and_join,
        out_shape=jax.ShapeDtypeStruct((R, CX, CY, NZ), BF16),
        in_specs=[SM] + [VM] * (2 * GROUPS),
        out_specs=HB,
        scratch_shapes=[pltpu.VMEM((R, CX, CY, NZ), BF16), pltpu.SemaphoreType.DMA((GROUPS,))],
        compiler_params=params(),
        cost_estimate=cost(10**8, 2 * 2**20),
        name="mix_and_join",
    )(mix, *a0, *a1)


def shift(x, axis, by):
    count = lax.axis_size(axis)
    return lax.ppermute(x, axis, [(i, (i + by) % count) for i in range(count)])


def exchange(sends):
    xlo, xhi, ylo, yhi = sends
    return [shift(xhi, "gx", 1), shift(xlo, "gx", -1), shift(yhi, "gy", 1), shift(ylo, "gy", -1)]


def body(spins, couplings, betas, metro_uniform, swap_uniform):
    a0, a1, sends = run_split_spins(spins)
    halos = [exchange(s) for s in sends]
    u, bonds = {}, None
    u[0, 0], u[0, 1], bonds = run_split_draws(0, couplings, metro_uniform)
    u[1, 0], u[1, 1], _ = run_split_draws(1, None, metro_uniform)
    scale = (-2.0 * LOG2E) * betas
    states = [a0, a1]
    sums = [None] * GROUPS
    for sweep in range(2):
        for colour in (0, 1):
            last = sweep == 1 and colour == 1
            for g in range(GROUPS):
                own, other, rest = run_half_sweep(
                    colour,
                    last,
                    scale[g * RG : (g + 1) * RG],
                    states[colour][g],
                    states[1 - colour][g],
                    u[sweep, colour][g],
                    bonds[colour],
                    halos[g],
                    f"half_sweep_{sweep}{colour}{g}",
                )
                states[colour][g], states[1 - colour][g] = own, other
                if last:
                    sums[g] = rest[0]
                else:
                    halos[g] = exchange(rest)
    partial_sum = jnp.sum(jnp.concatenate(sums, axis=0), axis=(1, 2))
    both = ("gx", "gy")
    count = lax.axis_size(both)
    copies = jnp.broadcast_to(partial_sum[None], (count, R))
    total = jnp.sum(lax.all_to_all(copies, both, 0, 0), axis=0)
    cell_count = CX * CY * NZ * count
    energies = -total / jnp.float32(cell_count)
    delta = swap_gain * (betas[0::2] - betas[1::2]) * (energies[0::2] - energies[1::2])
    mix = jax.nn.sigmoid((jnp.minimum(delta, 0.0) - jnp.log(swap_uniform)) / swap_width)
    return run_mix_and_join(mix, *states), energies


def solution(mesh):
    return jax.shard_map(
        body,
        mesh=mesh,
        in_specs=(
            P(None, "gx", "gy", None),
            P(None, "gx", "gy", None),
            P(),
            P(None, None, "gx", "gy", None),
            P(),
        ),
        out_specs=(P(None, "gx", "gy", None), P()),
        check_vma=False,
    )
```

time: 168 us -> 137 us (0.82)
  starting transfers between devices: 25.4 us -> 77.2 us
  other arithmetic: 45.9 us -> 0.51 us
  blocking collectives: 40.5 us -> 0 us
  Pallas kernels: 0 us -> 27.8 us
  local copies, waits for them, and re-layouts: 23.3 us -> 7.61 us
  waiting for transfers between devices: 31.4 us -> 22.6 us
    ppermute x16 -> x32, starting transfers between devices: 25.4 us -> 67 us  [shift(): return lax.ppermute(x, axis, [(i, (i + by) % count) for i in range(count)])]
    psum x4 -> x0, blocking collectives: 40.5 us -> none  [one_axis_at_a_time(): return functools.reduce(lax.psum, axes, x)]
    convert_element_type x4 -> x0, other arithmetic: 30 us -> none  [the longest x3 29.8 us: body(): state = jnp.where(parity == colour, flipped, current).astype(jnp.bfloat16)]
    pallas_call x0 -> x12, Pallas kernels: none -> 27.8 us  [the longest x8 13.1 us: run_half_sweep(): pl.pallas_call(functools.partial(half_sweep, colour, last), out_shape=[st...]
    ppermute x16 -> x32, waiting for transfers between devices: 31.4 us -> 9.76 us  [shift(): return lax.ppermute(x, axis, [(i, (i + by) % count) for i in range(count)])]
    slice x16 -> x1, local copies, waits for them, and re-layouts: 17.3 us -> 0.07 us  [body(): scale[g * RG:(g + 1) * RG]]
    all_to_all x0 -> x1, waiting for transfers between devices: none -> 12.8 us  [body(): total = jnp.sum(lax.all_to_all(copies, both, 0, 0), axis=0)]
    reduce_sum x1 -> x2, other arithmetic: 11.2 us -> 0.48 us  [the longest x1 0.29 us: body(): total = jnp.sum(lax.all_to_all(copies, both, 0, 0), axis=0)]
  transfers between devices with their start and end apart: 16 -> 33, of which waited for: 10 -> 8; matrix products, arithmetic and copies ran while one was open for 10% -> 0% of each run, Pallas kernels for 0% -> 14%
where the time goes in v1:
time: 137 us
  starting transfers between devices  77.2 us (56%)
  Pallas kernels  27.8 us (20%)
  waiting for transfers between devices  22.6 us (16%)
  local copies, waits for them, and re-layouts  7.61 us (6%)
    ppermute x32, starting transfers between devices, shift(): return lax.ppermute(x, axis, [(i, (i + by) % count) for i in range(count)])  67 us
    pallas_call x8, Pallas kernels, run_half_sweep(): pl.pallas_call(functools.partial(half_sweep, colour, last), out_shape=[st...  13.1 us
    all_to_all x1, waiting for transfers between devices, body(): total = jnp.sum(lax.all_to_all(copies, both, 0, 0), axis=0)  12.8 us
    all_to_all x1, starting transfers between devices, body(): total = jnp.sum(lax.all_to_all(copies, both, 0, 0), axis=0)  10.2 us
    ppermute x32, waiting for transfers between devices, shift(): return lax.ppermute(x, axis, [(i, (i + by) % count) for i in range(count)])  9.76 us
    pallas_call x2, Pallas kernels, run_split_draws(): pl.pallas_call(functools.partial(split_draws, sweep, with_bonds), out_sha...  7.39 us
    unnamed x22, local copies, waits for them, and re-layouts  6.44 us
    pallas_call x1, Pallas kernels, run_mix_and_join(): pl.pallas_call(mix_and_join, out_shape=jax.ShapeDtypeStruct((R, CX, CY, N...  3.96 us
  transfers between devices with their start and end apart: 33, of which 8 were waited for; matrix products, arithmetic and copies ran while one was open for 0% of the time, Pallas kernels for 14%

profile of v1, /device:TPU:1, one launch (start us, length us, event | category | flops | bytes accessed | tf_op | source)
XLA Modules:
  0.0 136.8 jit_solution(7184336218857852409)
XLA Ops:
  2.2 3.3 %split_spins.1 = (f32[8,4,80,128]{3,2,1,0:T(8,128)S(1)}, f32[8,4,80,128]{3,2,1,0:T(8,128)S(1)}, f32[8,4,80,128]{3,2,1,0:T(8,128)S(1)}, f32[8,4,80,128]{3,2,1,0:T...) custom-call(bf16[16,4,64,256]{3,2,1,0:T(8,128)(2,1)S(1)} %copy-done.6), custom_call_target="tpu_custom_call" | custom-call | flops 100000000 | bytes 2097152 | tf_op jit(solution)/shard_map/split_spins/pallas_call | solution.py:114
  5.5 2.2 %collective-permute-start = (bf16[8,64,128]{2,1,0:T(8,128)(2,1)S(1)}, bf16[8,64,128]{2,1,0:T(8,128)(2,1)S(1)}, u32[]{:S(2)}, u32[]{:S(2)}) collective-permute-start(bf16[8,64,128]{2,1,0:T(8,128)(2,1)S(1)} %get-tuple-element.70), channel_id=1, source_target_pairs={{0,8},{8,16},{16,24},{24,32},{32,40},{40,48},{48,56},{56,64},{64,7... | collective-permute-start | bytes 393224 | tf_op jit(solution)/shard_map/ppermute | solution.py:325
  7.7 6.8 %collective-permute-start.1 = (bf16[8,64,128]{2,1,0:T(8,128)(2,1)S(1)}, bf16[8,64,128]{2,1,0:T(8,128)(2,1)S(1)}, u32[]{:S(2)}, u32[]{:S(2)}) collective-permute-start(bf16[8,64,128]{2,1,0:T(8,128)(2,1)S(1)} %get-tuple-element.71), channel_id=1, source_target_pairs={{0,248},{8,0},{16,8},{24,16},{32,24},{40,32},{48,40},{56,48},{64,5... | collective-permute-start | bytes 393224 | tf_op jit(solution)/shard_map/ppermute | solution.py:325
  17.5 4.0 %collective-permute-start.17 = (bf16[8,64,128]{2,1,0:T(8,128)(2,1)S(1)}, bf16[8,64,128]{2,1,0:T(8,128)(2,1)S(1)}, u32[]{:S(2)}, u32[]{:S(2)}) collective-permute-start(bf16[8,64,128]{2,1,0:T(8,128)(2,1)S(1)} %get-tuple-element.101), channel_id=1, source_target_pairs={{0,248},{8,0},{16,8},{24,16},{32,24},{40,32},{48,40},{56,48},{64,5... | collective-permute-start | bytes 393224 | tf_op jit(solution)/shard_map/ppermute | solution.py:325
  21.5 2.3 %collective-permute-start.18 = (f32[8,4,128]{2,1,0:T(4,128)S(1)}, f32[8,4,128]{2,1,0:T(4,128)S(1)}, u32[]{:S(2)}, u32[]{:S(2)}) collective-permute-start(f32[8,4,128]{2,1,0:T(4,128)S(1)} %get-tuple-element.102), channel_id=1, source_target_pairs={{0,1},{1,2},{2,3},{3,4},{4,5},{5,6},{6,7},{7,0},{8,9},{9,10},{10,1... | collective-permute-start | bytes 49160 | tf_op jit(solution)/shard_map/ppermute | solution.py:325
  23.9 2.2 %copy-done.4 = bf16[2,16,4,64,256]{4,3,2,1,0:T(8,128)(2,1)S(1)} copy-done((bf16[2,16,4,64,256]{4,3,2,1,0:T(8,128)(2,1)S(1)}, bf16[2,16,4,64,256]{4,3,2,1,0:T(8,128)(2,1)}, u32[]{:S(2)}) %copy-start.4) | copy-done | bytes 4194328
  26.0 4.1 %split_draws_0.1 = (f32[8,4,64,128]{3,2,1,0:T(8,128)S(1)}, f32[8,4,64,128]{3,2,1,0:T(8,128)S(1)}, f32[8,4,64,128]{3,2,1,0:T(8,128)S(1)}, f32[8,4,64,128]{3,2,1,0...) custom-call(s32[6,4,64,256]{3,2,1,0:T(8,128)S(1)} %copy-done.7, ...), custom_call_target="tpu_custom_call" | custom-call | flops 100000000 | bytes 2097152 | tf_op jit(solution)/shard_map/split_draws_0/pallas_call | solution.py:185
  32.0 4.8 %collective-permute-start.5 = (bf16[8,64,128]{2,1,0:T(8,128)(2,1)S(1)}, bf16[8,64,128]{2,1,0:T(8,128)(2,1)S(1)}, u32[]{:S(2)}, u32[]{:S(2)}) collective-permute-start(bf16[8,64,128]{2,1,0:T(8,128)(2,1)S(1)} %get-tuple-element.79), channel_id=1, source_target_pairs={{0,248},{8,0},{16,8},{24,16},{32,24},{40,32},{48,40},{56,48},{64,5... | collective-permute-start | bytes 393224 | tf_op jit(solution)/shard_map/ppermute | solution.py:325
  38.5 4.8 %collective-permute-start.21 = (bf16[8,64,128]{2,1,0:T(8,128)(2,1)S(1)}, bf16[8,64,128]{2,1,0:T(8,128)(2,1)S(1)}, u32[]{:S(2)}, u32[]{:S(2)}) collective-permute-start(bf16[8,64,128]{2,1,0:T(8,128)(2,1)S(1)} %get-tuple-element.108), channel_id=1, source_target_pairs={{0,248},{8,0},{16,8},{24,16},{32,24},{40,32},{48,40},{56,48},{64,5... | collective-permute-start | bytes 393224 | tf_op jit(solution)/shard_map/ppermute | solution.py:325
  43.3 2.7 %collective-permute-start.6 = (f32[8,4,128]{2,1,0:T(4,128)S(1)}, f32[8,4,128]{2,1,0:T(4,128)S(1)}, u32[]{:S(2)}, u32[]{:S(2)}) collective-permute-start(f32[8,4,128]{2,1,0:T(4,128)S(1)} %get-tuple-element.80), channel_id=1, source_target_pairs={{0,1},{1,2},{2,3},{3,4},{4,5},{5,6},{6,7},{7,0},{8,9},{9,10},{10,1... | collective-permute-start | bytes 49160 | tf_op jit(solution)/shard_map/ppermute | solution.py:325
  48.0 3.7 %collective-permute-start.7 = (f32[8,4,128]{2,1,0:T(4,128)S(1)}, f32[8,4,128]{2,1,0:T(4,128)S(1)}, u32[]{:S(2)}, u32[]{:S(2)}) collective-permute-start(f32[8,4,128]{2,1,0:T(4,128)S(1)} %get-tuple-element.81), channel_id=1, source_target_pairs={{0,7},{1,0},{2,1},{3,2},{4,3},{5,4},{6,5},{7,6},{8,15},{9,8},{10,9... | collective-permute-start | bytes 49160 | tf_op jit(solution)/shard_map/ppermute | solution.py:325
  54.9 4.8 %collective-permute-start.9 = (bf16[8,64,128]{2,1,0:T(8,128)(2,1)S(1)}, bf16[8,64,128]{2,1,0:T(8,128)(2,1)S(1)}, u32[]{:S(2)}, u32[]{:S(2)}) collective-permute-start(bf16[8,64,128]{2,1,0:T(8,128)(2,1)S(1)} %get-tuple-element.86), channel_id=1, source_target_pairs={{0,248},{8,0},{16,8},{24,16},{32,24},{40,32},{48,40},{56,48},{64,5... | collective-permute-start | bytes 393224 | tf_op jit(solution)/shard_map/ppermute | solution.py:325
  61.4 4.8 %collective-permute-start.25 = (bf16[8,64,128]{2,1,0:T(8,128)(2,1)S(1)}, bf16[8,64,128]{2,1,0:T(8,128)(2,1)S(1)}, u32[]{:S(2)}, u32[]{:S(2)}) collective-permute-start(bf16[8,64,128]{2,1,0:T(8,128)(2,1)S(1)} %get-tuple-element.115), channel_id=1, source_target_pairs={{0,248},{8,0},{16,8},{24,16},{32,24},{40,32},{48,40},{56,48},{64,5... | collective-permute-start | bytes 393224 | tf_op jit(solution)/shard_map/ppermute | solution.py:325
  66.2 2.3 %collective-permute-start.10 = (f32[8,4,128]{2,1,0:T(4,128)S(1)}, f32[8,4,128]{2,1,0:T(4,128)S(1)}, u32[]{:S(2)}, u32[]{:S(2)}) collective-permute-start(f32[8,4,128]{2,1,0:T(4,128)S(1)} %get-tuple-element.87), channel_id=1, source_target_pairs={{0,1},{1,2},{2,3},{3,4},{4,5},{5,6},{6,7},{7,0},{8,9},{9,10},{10,1... | collective-permute-start | bytes 49160 | tf_op jit(solution)/shard_map/ppermute | solution.py:325
  68.4 2.5 %collective-permute-done.10.ylo_ref = f32[8,4,128]{2,1,0:T(4,128)S(1)} collective-permute-done((f32[8,4,128]{2,1,0:T(4,128)S(1)}, f32[8,4,128]{2,1,0:T(4,128)S(1)}, u32[]{:S(2)}, u32[]{:S(2)}) %collective-permute-start.10) | collective-permute-done | bytes 16416 | tf_op jit(solution)/shard_map/ppermute | solution.py:325
  70.9 3.7 %collective-permute-start.11 = (f32[8,4,128]{2,1,0:T(4,128)S(1)}, f32[8,4,128]{2,1,0:T(4,128)S(1)}, u32[]{:S(2)}, u32[]{:S(2)}) collective-permute-start(f32[8,4,128]{2,1,0:T(4,128)S(1)} %get-tuple-element.88), channel_id=1, source_target_pairs={{0,7},{1,0},{2,1},{3,2},{4,3},{5,4},{6,5},{7,6},{8,15},{9,8},{10,9... | collective-permute-start | bytes 49160 | tf_op jit(solution)/shard_map/ppermute | solution.py:325
  74.6 3.3 %split_draws_1.1 = (f32[8,4,64,128]{3,2,1,0:T(8,128)S(1)}, f32[8,4,64,128]{3,2,1,0:T(8,128)S(1)}, f32[8,4,64,128]{3,2,1,0:T(8,128)S(1)}, f32[8,4,64,128]{3,2,1,0:T(8,128)S(1)}) custom-call(bf16[2,16,4,64,256]{4,3,2,1,0:T(8,128)(2,1)S(1)} %copy-done.5), custom_call_target="tpu_custom_call" | custom-call | flops 100000000 | bytes 2097152 | tf_op jit(solution)/shard_map/split_draws_1/pallas_call | solution.py:185
  80.4 4.8 %collective-permute-start.13 = (bf16[8,64,128]{2,1,0:T(8,128)(2,1)S(1)}, bf16[8,64,128]{2,1,0:T(8,128)(2,1)S(1)}, u32[]{:S(2)}, u32[]{:S(2)}) collective-permute-start(bf16[8,64,128]{2,1,0:T(8,128)(2,1)S(1)} %get-tuple-element.93), channel_id=1, source_target_pairs={{0,248},{8,0},{16,8},{24,16},{32,24},{40,32},{48,40},{56,48},{64,5... | collective-permute-start | bytes 393224 | tf_op jit(solution)/shard_map/ppermute | solution.py:325
  86.9 4.8 %collective-permute-start.29 = (bf16[8,64,128]{2,1,0:T(8,128)(2,1)S(1)}, bf16[8,64,128]{2,1,0:T(8,128)(2,1)S(1)}, u32[]{:S(2)}, u32[]{:S(2)}) collective-permute-start(bf16[8,64,128]{2,1,0:T(8,128)(2,1)S(1)} %get-tuple-element.122), channel_id=1, source_target_pairs={{0,248},{8,0},{16,8},{24,16},{32,24},{40,32},{48,40},{56,48},{64,5... | collective-permute-start | bytes 393224 | tf_op jit(solution)/shard_map/ppermute | solution.py:325
  91.7 2.4 %collective-permute-start.14 = (f32[8,4,128]{2,1,0:T(4,128)S(1)}, f32[8,4,128]{2,1,0:T(4,128)S(1)}, u32[]{:S(2)}, u32[]{:S(2)}) collective-permute-start(f32[8,4,128]{2,1,0:T(4,128)S(1)} %get-tuple-element.94), channel_id=1, source_target_pairs={{0,1},{1,2},{2,3},{3,4},{4,5},{5,6},{6,7},{7,0},{8,9},{9,10},{10,1... | collective-permute-start | bytes 49160 | tf_op jit(solution)/shard_map/ppermute | solution.py:325
  95.9 3.7 %collective-permute-start.15 = (f32[8,4,128]{2,1,0:T(4,128)S(1)}, f32[8,4,128]{2,1,0:T(4,128)S(1)}, u32[]{:S(2)}, u32[]{:S(2)}) collective-permute-start(f32[8,4,128]{2,1,0:T(4,128)S(1)} %get-tuple-element.95), channel_id=1, source_target_pairs={{0,7},{1,0},{2,1},{3,2},{4,3},{5,4},{6,5},{7,6},{8,15},{9,8},{10,9... | collective-permute-start | bytes 49160 | tf_op jit(solution)/shard_map/ppermute | solution.py:325
  106.3 10.2 %all-to-all-start = ((f32[256,1,16]{2,1,0:T(1,128)}), f32[256,1,16]{2,1,0:T(1,128)S(1)}, u32[]{:S(2)}, u32[]{:S(2)}) async-start(f32[256,1,16]{2,1,0:T(1,128)} %broadcast_in_dim.2), calls=%async_computation | async-start | bytes 262144 | tf_op jit(solution)/shard_map/all_to_all | solution.py:366
  116.7 12.8 %all-to-all-done = f32[256,1,16]{2,1,0:T(1,128)S(1)} async-done(((f32[256,1,16]{2,1,0:T(1,128)}), f32[256,1,16]{2,1,0:T(1,128)S(1)}, u32[]{:S(2)}, u32[]{:S(2)}) %all-to-all-start) | async-done | bytes 16416 | tf_op jit(solution)/shard_map/all_to_all | solution.py:366
  132.7 4.0 %mix_and_join.1 = bf16[16,4,64,256]{3,2,1,0:T(8,128)(2,1)} custom-call(f32[8]{0:T(128)S(1)} %add_divide_fusion.mix_ref, f32[8,4,80,128]{3,2,1,0:T(8,128)S(1)} %copy-done.1, f32[8,4,80,128]{3,2,1,0:T(8,128)S(1)} %get-tuple-element.127.refs_1_, f32[8,4,80,128]{3,2,1,0:T(8,128)S(1)} %copy-done.3, f32[8,4,80,128]{3,2,1,0:T(8,128)S(1)} %get-tuple-element.129.refs_3_), custom_call_target="tpu_custom_call" | custom-call | flops 100000000 | bytes 2097152 | tf_op jit(solution)/shard_map/mix_and_join/pallas_call | solution.py:311
  (87 shorter events, 30.9 us)
Async XLA Ops:
  5.5 24.6 %collective-permute-start = (bf16[8,64,128]{2,1,0:T(8,128)(2,1)S(1)}, bf16[8,64,128]{2,1,0:T(8,128)(2,1)S(1)}, u32[]{:S(2)}, u32[]{:S(2)}) collective-permute-start(bf16[8,64,128]{2,1,0:T(8,128)(2,1)S(1)} %get-tuple-element.70), channel_id=1, source_target_pairs={{0,8},{8,16},{16,24},{24,32},{32,40},{40,48},{48,56},{56,64},{64,7... | collective-permute-start | bytes 393224 | tf_op jit(solution)/shard_map/ppermute | solution.py:325
  7.7 22.6 %collective-permute-start.1 = (bf16[8,64,128]{2,1,0:T(8,128)(2,1)S(1)}, bf16[8,64,128]{2,1,0:T(8,128)(2,1)S(1)}, u32[]{:S(2)}, u32[]{:S(2)}) collective-permute-start(bf16[8,64,128]{2,1,0:T(8,128)(2,1)S(1)} %get-tuple-element.71), channel_id=1, source_target_pairs={{0,248},{8,0},{16,8},{24,16},{32,24},{40,32},{48,40},{56,48},{64,5... | collective-permute-start | bytes 393224 | tf_op jit(solution)/shard_map/ppermute | solution.py:325
  16.6 5.0 %collective-permute-start.3 = (f32[8,4,128]{2,1,0:T(4,128)S(1)}, f32[8,4,128]{2,1,0:T(4,128)S(1)}, u32[]{:S(2)}, u32[]{:S(2)}) collective-permute-start(f32[8,4,128]{2,1,0:T(4,128)S(1)} %get-tuple-element.73), channel_id=1, source_target_pairs={{0,7},{1,0},{2,1},{3,2},{4,3},{5,4},{6,5},{7,6},{8,15},{9,8},{10,9... | collective-permute-start | bytes 49160 | tf_op jit(solution)/shard_map/ppermute | solution.py:325
  16.6 20.2 %collective-permute-start.16 = (bf16[8,64,128]{2,1,0:T(8,128)(2,1)S(1)}, bf16[8,64,128]{2,1,0:T(8,128)(2,1)S(1)}, u32[]{:S(2)}, u32[]{:S(2)}) collective-permute-start(bf16[8,64,128]{2,1,0:T(8,128)(2,1)S(1)} %get-tuple-element.100), channel_id=1, source_target_pairs={{0,8},{8,16},{16,24},{24,32},{32,40},{40,48},{48,56},{56,64},{64,7... | collective-permute-start | bytes 393224 | tf_op jit(solution)/shard_map/ppermute | solution.py:325
  17.5 19.3 %collective-permute-start.17 = (bf16[8,64,128]{2,1,0:T(8,128)(2,1)S(1)}, bf16[8,64,128]{2,1,0:T(8,128)(2,1)S(1)}, u32[]{:S(2)}, u32[]{:S(2)}) collective-permute-start(bf16[8,64,128]{2,1,0:T(8,128)(2,1)S(1)} %get-tuple-element.101), channel_id=1, source_target_pairs={{0,248},{8,0},{16,8},{24,16},{32,24},{40,32},{48,40},{56,48},{64,5... | collective-permute-start | bytes 393224 | tf_op jit(solution)/shard_map/ppermute | solution.py:325
  21.5 10.4 %collective-permute-start.18 = (f32[8,4,128]{2,1,0:T(4,128)S(1)}, f32[8,4,128]{2,1,0:T(4,128)S(1)}, u32[]{:S(2)}, u32[]{:S(2)}) collective-permute-start(f32[8,4,128]{2,1,0:T(4,128)S(1)} %get-tuple-element.102), channel_id=1, source_target_pairs={{0,1},{1,2},{2,3},{3,4},{4,5},{5,6},{6,7},{7,0},{8,9},{9,10},{10,1... | collective-permute-start | bytes 49160 | tf_op jit(solution)/shard_map/ppermute | solution.py:325
  30.1 6.6 %collective-permute-start.19 = (f32[8,4,128]{2,1,0:T(4,128)S(1)}, f32[8,4,128]{2,1,0:T(4,128)S(1)}, u32[]{:S(2)}, u32[]{:S(2)}) collective-permute-start(f32[8,4,128]{2,1,0:T(4,128)S(1)} %get-tuple-element.103), channel_id=1, source_target_pairs={{0,7},{1,0},{2,1},{3,2},{4,3},{5,4},{6,5},{7,6},{8,15},{9,8},{10,9... | collective-permute-start | bytes 49160 | tf_op jit(solution)/shard_map/ppermute | solution.py:325
  31.9 20.7 %collective-permute-start.4 = (bf16[8,64,128]{2,1,0:T(8,128)(2,1)S(1)}, bf16[8,64,128]{2,1,0:T(8,128)(2,1)S(1)}, u32[]{:S(2)}, u32[]{:S(2)}) collective-permute-start(bf16[8,64,128]{2,1,0:T(8,128)(2,1)S(1)} %get-tuple-element.78), channel_id=1, source_target_pairs={{0,8},{8,16},{16,24},{24,32},{32,40},{40,48},{48,56},{56,64},{64,7... | collective-permute-start | bytes 393224 | tf_op jit(solution)/shard_map/ppermute | solution.py:325
  32.0 21.2 %collective-permute-start.5 = (bf16[8,64,128]{2,1,0:T(8,128)(2,1)S(1)}, bf16[8,64,128]{2,1,0:T(8,128)(2,1)S(1)}, u32[]{:S(2)}, u32[]{:S(2)}) collective-permute-start(bf16[8,64,128]{2,1,0:T(8,128)(2,1)S(1)} %get-tuple-element.79), channel_id=1, source_target_pairs={{0,248},{8,0},{16,8},{24,16},{32,24},{40,32},{48,40},{56,48},{64,5... | collective-permute-start | bytes 393224 | tf_op jit(solution)/shard_map/ppermute | solution.py:325
  38.4 21.3 %collective-permute-start.20 = (bf16[8,64,128]{2,1,0:T(8,128)(2,1)S(1)}, bf16[8,64,128]{2,1,0:T(8,128)(2,1)S(1)}, u32[]{:S(2)}, u32[]{:S(2)}) collective-permute-start(bf16[8,64,128]{2,1,0:T(8,128)(2,1)S(1)} %get-tuple-element.107), channel_id=1, source_target_pairs={{0,8},{8,16},{16,24},{24,32},{32,40},{40,48},{48,56},{56,64},{64,7... | collective-permute-start | bytes 393224 | tf_op jit(solution)/shard_map/ppermute | solution.py:325
  38.5 21.2 %collective-permute-start.21 = (bf16[8,64,128]{2,1,0:T(8,128)(2,1)S(1)}, bf16[8,64,128]{2,1,0:T(8,128)(2,1)S(1)}, u32[]{:S(2)}, u32[]{:S(2)}) collective-permute-start(bf16[8,64,128]{2,1,0:T(8,128)(2,1)S(1)} %get-tuple-element.108), channel_id=1, source_target_pairs={{0,248},{8,0},{16,8},{24,16},{32,24},{40,32},{48,40},{56,48},{64,5... | collective-permute-start | bytes 393224 | tf_op jit(solution)/shard_map/ppermute | solution.py:325
  52.5 7.1 %collective-permute-start.23 = (f32[8,4,128]{2,1,0:T(4,128)S(1)}, f32[8,4,128]{2,1,0:T(4,128)S(1)}, u32[]{:S(2)}, u32[]{:S(2)}) collective-permute-start(f32[8,4,128]{2,1,0:T(4,128)S(1)} %get-tuple-element.110), channel_id=1, source_target_pairs={{0,7},{1,0},{2,1},{3,2},{4,3},{5,4},{6,5},{7,6},{8,15},{9,8},{10,9... | collective-permute-start | bytes 49160 | tf_op jit(solution)/shard_map/ppermute | solution.py:325
  54.8 23.2 %collective-permute-start.8 = (bf16[8,64,128]{2,1,0:T(8,128)(2,1)S(1)}, bf16[8,64,128]{2,1,0:T(8,128)(2,1)S(1)}, u32[]{:S(2)}, u32[]{:S(2)}) collective-permute-start(bf16[8,64,128]{2,1,0:T(8,128)(2,1)S(1)} %get-tuple-element.85), channel_id=1, source_target_pairs={{0,8},{8,16},{16,24},{24,32},{32,40},{40,48},{48,56},{56,64},{64,7... | collective-permute-start | bytes 393224 | tf_op jit(solution)/shard_map/ppermute | solution.py:325
  54.9 23.6 %collective-permute-start.9 = (bf16[8,64,128]{2,1,0:T(8,128)(2,1)S(1)}, bf16[8,64,128]{2,1,0:T(8,128)(2,1)S(1)}, u32[]{:S(2)}, u32[]{:S(2)}) collective-permute-start(bf16[8,64,128]{2,1,0:T(8,128)(2,1)S(1)} %get-tuple-element.86), channel_id=1, source_target_pairs={{0,248},{8,0},{16,8},{24,16},{32,24},{40,32},{48,40},{56,48},{64,5... | collective-permute-start | bytes 393224 | tf_op jit(solution)/shard_map/ppermute | solution.py:325
  61.3 23.9 %collective-permute-start.24 = (bf16[8,64,128]{2,1,0:T(8,128)(2,1)S(1)}, bf16[8,64,128]{2,1,0:T(8,128)(2,1)S(1)}, u32[]{:S(2)}, u32[]{:S(2)}) collective-permute-start(bf16[8,64,128]{2,1,0:T(8,128)(2,1)S(1)} %get-tuple-element.114), channel_id=1, source_target_pairs={{0,8},{8,16},{16,24},{24,32},{32,40},{40,48},{48,56},{56,64},{64,7... | collective-permute-start | bytes 393224 | tf_op jit(solution)/shard_map/ppermute | solution.py:325
  61.4 23.8 %collective-permute-start.25 = (bf16[8,64,128]{2,1,0:T(8,128)(2,1)S(1)}, bf16[8,64,128]{2,1,0:T(8,128)(2,1)S(1)}, u32[]{:S(2)}, u32[]{:S(2)}) collective-permute-start(bf16[8,64,128]{2,1,0:T(8,128)(2,1)S(1)} %get-tuple-element.115), channel_id=1, source_target_pairs={{0,248},{8,0},{16,8},{24,16},{32,24},{40,32},{48,40},{56,48},{64,5... | collective-permute-start | bytes 393224 | tf_op jit(solution)/shard_map/ppermute | solution.py:325
  66.2 4.8 %collective-permute-start.10 = (f32[8,4,128]{2,1,0:T(4,128)S(1)}, f32[8,4,128]{2,1,0:T(4,128)S(1)}, u32[]{:S(2)}, u32[]{:S(2)}) collective-permute-start(f32[8,4,128]{2,1,0:T(4,128)S(1)} %get-tuple-element.87), channel_id=1, source_target_pairs={{0,1},{1,2},{2,3},{3,4},{4,5},{5,6},{6,7},{7,0},{8,9},{9,10},{10,1... | collective-permute-start | bytes 49160 | tf_op jit(solution)/shard_map/ppermute | solution.py:325
  70.9 7.0 %collective-permute-start.11 = (f32[8,4,128]{2,1,0:T(4,128)S(1)}, f32[8,4,128]{2,1,0:T(4,128)S(1)}, u32[]{:S(2)}, u32[]{:S(2)}) collective-permute-start(f32[8,4,128]{2,1,0:T(4,128)S(1)} %get-tuple-element.88), channel_id=1, source_target_pairs={{0,7},{1,0},{2,1},{3,2},{4,3},{5,4},{6,5},{7,6},{8,15},{9,8},{10,9... | collective-permute-start | bytes 49160 | tf_op jit(solution)/shard_map/ppermute | solution.py:325
  78.0 7.2 %collective-permute-start.27 = (f32[8,4,128]{2,1,0:T(4,128)S(1)}, f32[8,4,128]{2,1,0:T(4,128)S(1)}, u32[]{:S(2)}, u32[]{:S(2)}) collective-permute-start(f32[8,4,128]{2,1,0:T(4,128)S(1)} %get-tuple-element.117), channel_id=1, source_target_pairs={{0,7},{1,0},{2,1},{3,2},{4,3},{5,4},{6,5},{7,6},{8,15},{9,8},{10,9... | collective-permute-start | bytes 49160 | tf_op jit(solution)/shard_map/ppermute | solution.py:325
  80.1 20.3 %collective-permute-start.12 = (bf16[8,64,128]{2,1,0:T(8,128)(2,1)S(1)}, bf16[8,64,128]{2,1,0:T(8,128)(2,1)S(1)}, u32[]{:S(2)}, u32[]{:S(2)}) collective-permute-start(bf16[8,64,128]{2,1,0:T(8,128)(2,1)S(1)} %get-tuple-element.92), channel_id=1, source_target_pairs={{0,8},{8,16},{16,24},{24,32},{32,40},{40,48},{48,56},{56,64},{64,7... | collective-permute-start | bytes 393224 | tf_op jit(solution)/shard_map/ppermute | solution.py:325
  80.4 20.7 %collective-permute-start.13 = (bf16[8,64,128]{2,1,0:T(8,128)(2,1)S(1)}, bf16[8,64,128]{2,1,0:T(8,128)(2,1)S(1)}, u32[]{:S(2)}, u32[]{:S(2)}) collective-permute-start(bf16[8,64,128]{2,1,0:T(8,128)(2,1)S(1)} %get-tuple-element.93), channel_id=1, source_target_pairs={{0,248},{8,0},{16,8},{24,16},{32,24},{40,32},{48,40},{56,48},{64,5... | collective-permute-start | bytes 393224 | tf_op jit(solution)/shard_map/ppermute | solution.py:325
  86.8 16.8 %collective-permute-start.28 = (bf16[8,64,128]{2,1,0:T(8,128)(2,1)S(1)}, bf16[8,64,128]{2,1,0:T(8,128)(2,1)S(1)}, u32[]{:S(2)}, u32[]{:S(2)}) collective-permute-start(bf16[8,64,128]{2,1,0:T(8,128)(2,1)S(1)} %get-tuple-element.121), channel_id=1, source_target_pairs={{0,8},{8,16},{16,24},{24,32},{32,40},{40,48},{48,56},{56,64},{64,7... | collective-permute-start | bytes 393224 | tf_op jit(solution)/shard_map/ppermute | solution.py:325
  86.9 16.7 %collective-permute-start.29 = (bf16[8,64,128]{2,1,0:T(8,128)(2,1)S(1)}, bf16[8,64,128]{2,1,0:T(8,128)(2,1)S(1)}, u32[]{:S(2)}, u32[]{:S(2)}) collective-permute-start(bf16[8,64,128]{2,1,0:T(8,128)(2,1)S(1)} %get-tuple-element.122), channel_id=1, source_target_pairs={{0,248},{8,0},{16,8},{24,16},{32,24},{40,32},{48,40},{56,48},{64,5... | collective-permute-start | bytes 393224 | tf_op jit(solution)/shard_map/ppermute | solution.py:325
  106.3 23.2 %all-to-all-start = ((f32[256,1,16]{2,1,0:T(1,128)}), f32[256,1,16]{2,1,0:T(1,128)S(1)}, u32[]{:S(2)}, u32[]{:S(2)}) async-start(f32[256,1,16]{2,1,0:T(1,128)} %broadcast_in_dim.2), calls=%async_computation | async-start | bytes 262144 | tf_op jit(solution)/shard_map/all_to_all | solution.py:366
  (20 other events, 127.0 us)

commit v2 on v0

v2 whole, which is shorter than its diff:
```python
import functools
import math

import jax
import jax.numpy as jnp
from jax import lax
from jax.experimental import pallas as pl
from jax.experimental.pallas import tpu as pltpu
from jax.sharding import PartitionSpec as P

R = 16
CX, CY, NZ = 4, 64, 256
HALF = NZ // 2
PAD = 8
UNROLL = 4
OUTER, INNER = (0, CX - 1), (1, 2)
LOG2E = math.log2(math.e)
F32 = jnp.float32
BF16 = jnp.bfloat16
MIB = 1024 * 1024

swap_width = 0.25
swap_gain = 64.0

VM = pl.BlockSpec(memory_space=pltpu.VMEM)
SM = pl.BlockSpec(memory_space=pltpu.SMEM)
HB = pl.BlockSpec(memory_space=pltpu.HBM)


def in_hbm(x):
    return pltpu.with_memory_space_constraint(x, pltpu.HBM)


def split_matrix():
    row = lax.broadcasted_iota(jnp.int32, (NZ, NZ), 0)
    col = lax.broadcasted_iota(jnp.int32, (NZ, NZ), 1)
    wanted = jnp.where(col < HALF, 2 * col, 2 * (col - HALF) + 1)
    return (row == wanted).astype(F32).astype(BF16)


def join_matrix():
    row = lax.broadcasted_iota(jnp.int32, (NZ, NZ), 0)
    col = lax.broadcasted_iota(jnp.int32, (NZ, NZ), 1)
    wanted = jnp.where(row < HALF, 2 * row, 2 * (row - HALF) + 1)
    return (col == wanted).astype(F32).astype(BF16)


def odd_rows(rows=CY):
    return lax.broadcasted_iota(jnp.int32, (rows, HALF), 0) % 2 == 1


def by_colour(even, odd, x, odd_row):
    if x % 2 == 0:
        return jnp.where(odd_row, odd, even), jnp.where(odd_row, even, odd)
    return jnp.where(odd_row, even, odd), jnp.where(odd_row, odd, even)


def send_layers(side_ref, own, xeven, xodd):
    layer = (CX - 1) * (1 - side_ref[0])

    for r in range(R):
        xeven[r] = own[r, layer, PAD : PAD + CY, :].astype(BF16)
        xodd[r] = own[r, CX - 1 - layer, PAD : PAD + CY, :].astype(BF16)


def send_rows(side_ref, own, yeven, yodd):
    lower = side_ref[1] == 0
    for r in range(R):
        for x in range(CX):
            first = own[r, x, PAD : PAD + 1, :]
            final = own[r, x, PAD + CY - 1 : PAD + CY, :]
            yeven[r, x : x + 1, :] = jnp.where(lower, final, first)
            yodd[r, x : x + 1, :] = jnp.where(lower, first, final)


STATE = pltpu.VMEM((R, CX, CY + 2 * PAD, HALF), F32)
DRAWS = pltpu.VMEM((R, CX, CY, HALF), F32)
BONDS = pltpu.VMEM((6, CX, CY, HALF), F32)
LAYER = jax.ShapeDtypeStruct((R, CY, HALF), BF16)
ROWS = jax.ShapeDtypeStruct((R, CX, HALF), F32)


def call(kernel, name, outs, in_specs, out_specs, scratch=(), aliases={}, limit=8, flops=10**7):
    return pl.pallas_call(
        kernel,
        out_shape=outs,
        in_specs=in_specs,
        out_specs=out_specs,
        scratch_shapes=list(scratch),
        input_output_aliases=aliases,
        compiler_params=pltpu.CompilerParams(vmem_limit_bytes=limit * MIB),
        cost_estimate=pl.CostEstimate(flops=flops, bytes_accessed=2 * MIB, transcendentals=0),
        name=name,
    )


def split_outer(side_ref, spins_ref, a0, a1, xeven, xodd, yeven, yodd, layers, edge_rows, split_rows, sems):
    copies = []
    for i, x in enumerate(OUTER):
        copies.append(pltpu.make_async_copy(spins_ref.at[:, x], layers.at[i], sems.at[i]))
    for i, y in enumerate((0, CY - 8)):
        copies.append(
            pltpu.make_async_copy(
                spins_ref.at[:, pl.ds(1, 2), pl.ds(y, 8)], edge_rows.at[i], sems.at[2 + i]
            )
        )
    for copy in copies:
        copy.start()
    matrix = split_matrix()
    odd_row = odd_rows()
    for i, x in enumerate(OUTER):
        copies[i].wait()

        cells = layers[i].reshape(R * CY, NZ)
        parts = jnp.dot(cells, matrix, preferred_element_type=F32)
        for r in range(R):
            rows = parts[r * CY : (r + 1) * CY]
            c0, c1 = by_colour(rows[:, :HALF], rows[:, HALF:], x, odd_row)
            a0[r, x, PAD : PAD + CY, :] = c0
            a1[r, x, PAD : PAD + CY, :] = c1

    for i in range(2):
        copies[2 + i].wait()
        cells = edge_rows[i].reshape(R * 2 * 8, NZ)
        split_rows[i] = jnp.dot(cells, matrix, preferred_element_type=F32).reshape(R, 2, 8, NZ)
    send_layers(side_ref, a1, xeven, xodd)
    lower = side_ref[1] == 0
    for r in range(R):
        for x in range(CX):
            if x in OUTER:
                first = a1[r, x, PAD : PAD + 1, :]
                final = a1[r, x, PAD + CY - 1 : PAD + CY, :]
            else:
                at = 0 if x % 2 == 1 else HALF
                first = split_rows[0, r, x - 1, 0:1, at : at + HALF]
                at = HALF - at
                final = split_rows[1, r, x - 1, 7:8, at : at + HALF]
            yeven[r, x : x + 1, :] = jnp.where(lower, final, first)
            yodd[r, x : x + 1, :] = jnp.where(lower, first, final)


def run_split_outer(side, spins):
    return call(
        split_outer,
        "split_outer",
        [STATE] * 2 + [LAYER] * 2 + [ROWS] * 2,
        [SM, HB],
        [VM] * 6,
        [
            pltpu.VMEM((2, R, CY, NZ), BF16),
            pltpu.VMEM((2, R, 2, 8, NZ), BF16),
            pltpu.VMEM((2, R, 2, 8, NZ), F32),
            pltpu.SemaphoreType.DMA((4,)),
        ],
    )(side, in_hbm(spins))


def split_field(buf, u0, u1, matrix, odd_row):
    @pl.loop(0, R, step=4)
    def _(first):
        cells = buf[pl.ds(first, 4)].reshape(4 * CX * CY, NZ)
        parts = jnp.dot(cells, matrix, preferred_element_type=F32) * 5.0
        for k in range(4 * CX):
            rows = parts[k * CY : (k + 1) * CY]
            r, x = first + k // CX, k % CX
            c0, c1 = by_colour(rows[:, :HALF], rows[:, HALF:], x, odd_row)
            u0[r, x] = c0
            u1[r, x] = c1


def split_inner(
    spins_ref, couplings_ref, uniform_ref, a0_in, a1_in, a0, a1, u0, u1, bonds0, bonds1, layers, bond_buf, buf, sems
):
    copies = [
        pltpu.make_async_copy(spins_ref.at[:, pl.ds(1, 2)], layers, sems.at[0]),
        pltpu.make_async_copy(couplings_ref, bond_buf, sems.at[1]),
        pltpu.make_async_copy(uniform_ref.at[0], buf, sems.at[2]),
    ]
    for copy in copies:
        copy.start()
    matrix = split_matrix()
    odd_row = odd_rows()
    copies[0].wait()

    @pl.loop(0, R, step=8)
    def _(first):
        cells = layers[pl.ds(first, 8)].reshape(16 * CY, NZ)
        parts = jnp.dot(cells, matrix, preferred_element_type=F32)
        for k in range(16):
            rows = parts[k * CY : (k + 1) * CY]
            x = 1 + k % 2
            c0, c1 = by_colour(rows[:, :HALF], rows[:, HALF:], x, odd_row)
            a0[first + k // 2, x, PAD : PAD + CY, :] = c0
            a1[first + k // 2, x, PAD : PAD + CY, :] = c1

    copies[1].wait()
    for x in range(CX):
        halves = []
        for k in range(6):
            cells = bond_buf[k, x].astype(F32).astype(BF16)
            parts = jnp.dot(cells, matrix, preferred_element_type=F32)
            halves.append((parts[:, :HALF], parts[:, HALF:]))
        for place, k in enumerate((0, 3, 1, 4)):
            bonds0[place, x], bonds1[place, x] = by_colour(*halves[k], x, odd_row)
        for place, (k, m) in enumerate(((2, 5), (5, 2))):
            bonds0[4 + place, x], bonds1[4 + place, x] = by_colour(halves[k][0], halves[m][1], x, odd_row)
    copies[2].wait()
    split_field(buf, u0, u1, matrix, odd_row)


def run_split_inner(spins, couplings, uniform, a0, a1):
    return call(
        split_inner,
        "split_inner",
        [STATE] * 2 + [DRAWS] * 2 + [BONDS] * 2,
        [HB] * 3 + [VM] * 2,
        [VM] * 6,
        [
            pltpu.VMEM((R, 2, CY, NZ), BF16),
            pltpu.VMEM((6, CX, CY, NZ), jnp.int32),
            pltpu.VMEM((R, CX, CY, NZ), BF16),
            pltpu.SemaphoreType.DMA((3,)),
        ],
        {3: 0, 4: 1},
    )(in_hbm(spins), in_hbm(couplings), in_hbm(uniform), a0, a1)


def split_draws(uniform_ref, u0, u1, buf, sem):
    copy = pltpu.make_async_copy(uniform_ref.at[1], buf, sem)
    copy.start()
    matrix = split_matrix()
    odd_row = odd_rows()
    copy.wait()
    split_field(buf, u0, u1, matrix, odd_row)


def run_split_draws(uniform):
    return call(
        split_draws,
        "split_draws",
        [DRAWS] * 2,
        [HB],
        [VM] * 2,
        [pltpu.VMEM((R, CX, CY, NZ), BF16), pltpu.SemaphoreType.DMA],
    )(in_hbm(uniform))


def put_rows(side_ref, other, yeven, yodd):
    lower = side_ref[1] == 0
    for r in range(R):
        for x in range(CX):
            even, odd = yeven[r, x : x + 1, :], yodd[r, x : x + 1, :]
            other[r, x, PAD - 1 : PAD, :] = jnp.where(lower, odd, even)
            other[r, x, PAD + CY : PAD + CY + 1, :] = jnp.where(lower, even, odd)


def put_layers(side_ref, beyond, xeven, xodd):
    upper = side_ref[0]
    for r in range(R):
        beyond[1 - upper, r] = xeven[r].astype(F32)
        beyond[upper, r] = xodd[r].astype(F32)


def update(colour, layers, betas_ref, own, other, u_ref, bonds_ref, beyond, energy):
    tile = 16
    odd_row = odd_rows(tile)

    @pl.loop(0, R, step=UNROLL)
    def _(first):
        sums = [jnp.zeros((tile, HALF), F32) for _ in range(UNROLL)]
        scales = [betas_ref[first + i] * (-2.0 * LOG2E) for i in range(UNROLL)]
        for x in layers:
            for y in range(0, CY, tile):
                bonds = [bonds_ref[k, x, y : y + tile, :] for k in range(6)]
                for i in range(UNROLL):
                    r = first + i

                    def near(dx, dy):
                        at = x + dx
                        if at < 0:
                            return beyond[0, r, y : y + tile, :]
                        if at >= CX:
                            return beyond[1, r, y : y + tile, :]
                        return other[r, at, PAD + y + dy : PAD + y + dy + tile, :]

                    same = near(0, 0)
                    below, above = pltpu.roll(same, 1, 1), pltpu.roll(same, HALF - 1, 1)
                    if (colour + x) % 2 == 0:
                        beside = jnp.where(odd_row, above, below)
                    else:
                        beside = jnp.where(odd_row, below, above)
                    field = bonds[0] * near(1, 0) + bonds[1] * near(-1, 0)
                    field = field + (bonds[2] * near(0, 1) + bonds[3] * near(0, -1))
                    field = field + (bonds[4] * same + bonds[5] * beside)
                    spin = own[r, x, PAD + y : PAD + y + tile, :]
                    accept = jnp.exp2(jnp.minimum(spin * field * scales[i], 0.0))
                    new = spin * jnp.tanh(u_ref[r, x, y : y + tile, :] - 5.0 * accept)
                    wide = new.astype(BF16).astype(F32)
                    own[r, x, PAD + y : PAD + y + tile, :] = wide
                    if energy is not None:
                        sums[i] = sums[i] + wide * field
        if energy is not None:
            for i in range(UNROLL):
                energy[first + i] = sums[i][:8] + sums[i][8:]


def sweep_outer(colour, side_ref, betas_ref, own_in, other_in, u, bonds, xe, xo, ye, yo, own, other, sxe, sxo, beyond):
    put_layers(side_ref, beyond, xe, xo)
    put_rows(side_ref, other, ye, yo)
    update(colour, OUTER, betas_ref, own, other, u, bonds, beyond, None)
    send_layers(side_ref, own, sxe, sxo)


def sweep_inner(colour, side_ref, betas_ref, own_in, other_in, u, bonds, own, other, sye, syo):
    update(colour, INNER, betas_ref, own, other, u, bonds, None, None)
    send_rows(side_ref, own, sye, syo)


BEYOND = pltpu.VMEM((2, R, CY, HALF), F32)
ENERGY = jax.ShapeDtypeStruct((R, 8, HALF), F32)


def final_inner(side_ref, betas_ref, own_in, other_in, u, bonds, ye, yo, own, other, energy):
    put_rows(side_ref, other, ye, yo)
    update(1, INNER, betas_ref, own, other, u, bonds, None, energy)


def final_outer(side_ref, betas_ref, own_in, other_in, u, bonds, xe, xo, inner_energy, own, other, sums_ref, beyond, energy):
    put_layers(side_ref, beyond, xe, xo)
    update(1, OUTER, betas_ref, own, other, u, bonds, beyond, energy)
    lines = jnp.sum(energy[...] + inner_energy[...], axis=1)
    totals = jnp.sum(lines, axis=1, keepdims=True)
    diagonal = lax.broadcasted_iota(jnp.int32, (R, R), 0) == lax.broadcasted_iota(jnp.int32, (R, R), 1)
    row = jnp.sum(jnp.where(diagonal, totals, 0.0), axis=0, keepdims=True)
    sums_ref[...] = jnp.broadcast_to(row[None], sums_ref.shape)


def run_sweep_outer(colour, name, side, betas, own, other, u, bonds, xs, ys):
    return call(
        functools.partial(sweep_outer, colour),
        name,
        [STATE] * 2 + [LAYER] * 2,
        [SM, SM] + [VM] * 8,
        [VM] * 4,
        [BEYOND],
        {2: 0, 3: 1},
    )(side, betas, own, other, u, bonds, *xs, *ys)


def run_sweep_inner(colour, name, side, betas, own, other, u, bonds):
    return call(
        functools.partial(sweep_inner, colour),
        name,
        [STATE] * 2 + [ROWS] * 2,
        [SM, SM] + [VM] * 4,
        [VM] * 4,
        (),
        {2: 0, 3: 1},
    )(side, betas, own, other, u, bonds)


def run_final_inner(side, betas, own, other, u, bonds, ys):
    return call(
        final_inner,
        "final_inner",
        [STATE] * 2 + [ENERGY],
        [SM, SM] + [VM] * 6,
        [VM] * 3,
        (),
        {2: 0, 3: 1},
    )(side, betas, own, other, u, bonds, *ys)


def run_final_outer(count, side, betas, own, other, u, bonds, xs, energy):
    return call(
        final_outer,
        "final_outer",
        [STATE] * 2 + [pltpu.VMEM((count, 1, R), F32)],
        [SM, SM] + [VM] * 7,
        [VM] * 3,
        [BEYOND, pltpu.VMEM((R, 8, HALF), F32)],
        {2: 0, 3: 1},
    )(side, betas, own, other, u, bonds, *xs, energy)


def mix_and_join(cell_count, betas_ref, swap_ref, sums_ref, a0, a1, out_ref, energies_ref, weights, buf, sems):
    total = jnp.sum(sums_ref[:, 0, :], axis=0, keepdims=True)
    energies = -total / cell_count
    energies_ref[...] = energies
    place = lax.broadcasted_iota(jnp.int32, (1, R), 1)
    betas = jnp.zeros((1, R), F32)
    draws = jnp.ones((1, R), F32)
    for r in range(R):
        betas = jnp.where(place == r, betas_ref[r], betas)
    for k in range(R // 2):
        draws = jnp.where(place == 2 * k, swap_ref[k], draws)
    beta_step = betas[:, : R - 1] - betas[:, 1:]
    energy_step = energies[:, : R - 1] - energies[:, 1:]
    delta = swap_gain * beta_step * energy_step
    mix = jax.nn.sigmoid((jnp.minimum(delta, 0.0) - jnp.log(draws[:, : R - 1])) / swap_width)
    for k in range(R // 2):
        weights[k : k + 1, :] = jnp.broadcast_to(mix[:, 2 * k : 2 * k + 1], (1, HALF))
    matrix = join_matrix()
    odd_row = odd_rows()

    def out_copy(pair):
        at = pl.ds(pair * 2, 2)
        return pltpu.make_async_copy(buf.at[at], out_ref.at[at], sems.at[pair])

    @pl.loop(0, R // 2)
    def _(pair):
        weight = jnp.broadcast_to(weights[pl.ds(pair, 1), :], (CY, HALF))
        r = pair * 2
        cells = [[], []]
        for x in range(CX):
            new = [[], []]
            for state in (a0, a1):
                upper = state[r, x, PAD : PAD + CY, :]
                lower = state[r + 1, x, PAD : PAD + CY, :]
                moved = weight * (lower - upper)
                new[0].append(upper + moved)
                new[1].append(lower - moved)
            for i in range(2):
                even, odd = by_colour(*new[i], x, odd_row)
                cells[i].append(jnp.concatenate([even.astype(BF16), odd.astype(BF16)], axis=1))
        for i in range(2):
            joined = jnp.dot(jnp.concatenate(cells[i], axis=0), matrix, preferred_element_type=F32)
            buf[r + i] = joined.astype(BF16).reshape(CX, CY, NZ)
        out_copy(pair).start()

    @pl.loop(0, R // 2)
    def _(pair):
        out_copy(pair).wait()


def run_mix_and_join(cell_count, betas, swap, sums, a0, a1):
    return call(
        functools.partial(mix_and_join, cell_count),
        "mix_and_join",
        [jax.ShapeDtypeStruct((R, CX, CY, NZ), BF16), jax.ShapeDtypeStruct((1, R), F32)],
        [SM] * 2 + [VM] * 3,
        [HB, VM],
        [
            pltpu.VMEM((R // 2, HALF), F32),
            pltpu.VMEM((R, CX, CY, NZ), BF16),
            pltpu.SemaphoreType.DMA((R // 2,)),
        ],
    )(betas, swap, sums, a0, a1)


def swap_pairs(x, axis, odd):
    count = lax.axis_size(axis)
    return lax.ppermute(x, axis, [(i, (((i + odd) ^ 1) - odd) % count) for i in range(count)])


def exchange(axis, even, odd):
    return [swap_pairs(even, axis, 0), swap_pairs(odd, axis, 1)]


def body(spins, couplings, betas, metro_uniform, swap_uniform):
    side = jnp.stack([lax.axis_index("gx") % 2, lax.axis_index("gy") % 2]).astype(jnp.int32)
    a0, a1, xe, xo, ye, yo = run_split_outer(side, spins)
    xs, ys = exchange("gx", xe, xo), exchange("gy", ye, yo)
    a0, a1, u00, u01, bonds0, bonds1 = run_split_inner(spins, couplings, metro_uniform, a0, a1)
    u10, u11 = run_split_draws(metro_uniform)
    states = [a0, a1]
    for step, (u, bonds) in enumerate(((u00, bonds0), (u01, bonds1), (u10, bonds0))):
        colour = step % 2
        own, other = states[colour], states[1 - colour]
        own, other, xe, xo = run_sweep_outer(colour, f"sweep_outer_{step}", side, betas, own, other, u, bonds, xs, ys)
        xs = exchange("gx", xe, xo)
        own, other, ye, yo = run_sweep_inner(colour, f"sweep_inner_{step}", side, betas, own, other, u, bonds)
        ys = exchange("gy", ye, yo)
        states[colour], states[1 - colour] = own, other
    both = ("gx", "gy")
    count = lax.axis_size(both)
    a0, a1 = states
    a1, a0, energy = run_final_inner(side, betas, a1, a0, u11, bonds1, ys)
    a1, a0, sums = run_final_outer(count, side, betas, a1, a0, u11, bonds1, xs, energy)
    sums = lax.all_to_all(sums, both, 0, 0, tiled=True)
    cell_count = float(CX * CY * NZ * count)
    out, energies = run_mix_and_join(
        cell_count, betas, swap_uniform, sums, a0, a1
    )
    return out, energies[0]


def solution(mesh):
    return jax.shard_map(
        body,
        mesh=mesh,
        in_specs=(
            P(None, "gx", "gy", None),
            P(None, "gx", "gy", None),
            P(),
            P(None, None, "gx", "gy", None),
            P(),
        ),
        out_specs=(P(None, "gx", "gy", None), P()),
        check_vma=False,
    )
```

time: 168 us -> 85.9 us (0.51)
  other arithmetic: 45.9 us -> 0.08 us
  Pallas kernels: 0 us -> 26.8 us
  waiting for transfers between devices: 31.4 us -> 4.9 us
  local copies, waits for them, and re-layouts: 23.3 us -> 0.01 us
  blocking collectives: 40.5 us -> 21.6 us
  starting transfers between devices: 25.4 us -> 31.4 us
    psum x4 -> x0, blocking collectives: 40.5 us -> none  [one_axis_at_a_time(): return functools.reduce(lax.psum, axes, x)]
    convert_element_type x4 -> x0, other arithmetic: 30 us -> none  [the longest x3 29.8 us: body(): state = jnp.where(parity == colour, flipped, current).astype(jnp.bfloat16)]
    pallas_call x0 -> x12, Pallas kernels: none -> 26.8 us  [the longest x3 5.07 us: run_sweep_outer(): call(functools.partial(sweep_outer, colour), name, [STATE] * 2 + [LAYER]...]
    ppermute x16, waiting for transfers between devices: 31.4 us -> 4.9 us  [swap_pairs(): lax.ppermute(x, axis, [(i, ((i + odd ^ 1) - odd) % count) for i in range(...]
    all_to_all x0 -> x1, blocking collectives: none -> 21.6 us  [body(): sums = lax.all_to_all(sums, both, 0, 0, tiled=True)]
    slice x20 -> x0, local copies, waits for them, and re-layouts: 19.5 us -> none  [the longest x6 10.5 us: neighbour_field(): jnp.roll(current, -1, 3)]
    reduce_sum x1 -> x0, other arithmetic: 11.2 us -> none  [body(): jnp.sum(jnp.where(parity == 1, current * field, 0.0), axis=(1, 2, 3))]
    ppermute x16, starting transfers between devices: 25.4 us -> 31.4 us  [swap_pairs(): lax.ppermute(x, axis, [(i, ((i + odd ^ 1) - odd) % count) for i in range(...]
  transfers between devices with their start and end apart: 16 -> 16, of which waited for: 10 -> 2; matrix products, arithmetic and copies ran while one was open for 10% -> 0% of each run, Pallas kernels for 0% -> 15%
where the time goes in v2:
time: 85.9 us; the launch traced here: 85.7 us
  starting transfers between devices  31.4 us (37%)
  Pallas kernels  26.8 us (31%)
  blocking collectives  21.6 us (25%)
  waiting for transfers between devices  4.9 us (6%)
  between operations  1.02 us (1%)
    ppermute x16, starting transfers between devices, swap_pairs(): lax.ppermute(x, axis, [(i, ((i + odd ^ 1) - odd) % count) for i in range(...  31.4 us
    all_to_all x1, blocking collectives, body(): sums = lax.all_to_all(sums, both, 0, 0, tiled=True)  21.6 us
    pallas_call x3, Pallas kernels, run_sweep_outer(): call(functools.partial(sweep_outer, colour), name, [STATE] * 2 + [LAYER]...  5.07 us
    ppermute x16, waiting for transfers between devices, swap_pairs(): lax.ppermute(x, axis, [(i, ((i + odd ^ 1) - odd) % count) for i in range(...  4.9 us
    pallas_call x3, Pallas kernels, run_sweep_inner(): call(functools.partial(sweep_inner, colour), name, [STATE] * 2 + [ROWS] *...  4.67 us
    pallas_call x1, Pallas kernels, run_mix_and_join(): call(functools.partial(mix_and_join, cell_count), 'mix_and_join', [jax.Sh...  4.06 us
    pallas_call x1, Pallas kernels, run_split_inner(): call(split_inner, 'split_inner', [STATE] * 2 + [DRAWS] * 2 + [BONDS] * 2,...  3.77 us
    pallas_call x1, Pallas kernels, run_split_outer(): call(split_outer, 'split_outer', [STATE] * 2 + [LAYER] * 2 + [ROWS] * 2,...  2.95 us
  transfers between devices with their start and end apart: 16, of which 2 were waited for; matrix products, arithmetic and copies ran while one was open for 0% of the time, Pallas kernels for 15%

profile of v2, /device:TPU:1, one launch (start us, length us, event | category | flops | bytes accessed | tf_op | source)
XLA Modules:
  0.0 85.7 jit_solution(4594108619366982486)
XLA Ops:
  0.7 3.0 %split_outer.1 = (f32[16,4,80,128]{3,2,1,0:T(8,128)S(1)}, f32[16,4,80,128]{3,2,1,0:T(8,128)S(1)}, bf16[16,64,128]{2,1,0:T(8,128)(2,1)S(1)}, bf16[16,64,128]{2,1,...) custom-call(s32[2]{0:T(128)S(1)} %pad_add_fusion.side_ref, bf16[16,4,64,256]{3,2,1,0:T(8,128)(2,1)} %spins_ref.3), custom_call_target="tpu_custom_call" | custom-call | flops 10000000 | bytes 2097152 | tf_op jit(solution)/shard_map/split_outer/pallas_call | solution.py:143
  3.7 2.2 %collective-permute-start = (bf16[16,64,128]{2,1,0:T(8,128)(2,1)S(1)}, bf16[16,64,128]{2,1,0:T(8,128)(2,1)S(1)}, u32[]{:S(2)}, u32[]{:S(2)}) collective-permute-start(bf16[16,64,128]{2,1,0:T(8,128)(2,1)S(1)} %get-tuple-element.54), channel_id=1, source_target_pairs={{0,8},{8,0},{16,24},{24,16},{32,40},{40,32},{48,56},{56,48},{64,72... | collective-permute-start | bytes 786440 | tf_op jit(solution)/shard_map/ppermute | solution.py:453
  5.9 7.2 %collective-permute-start.1 = (bf16[16,64,128]{2,1,0:T(8,128)(2,1)S(1)}, bf16[16,64,128]{2,1,0:T(8,128)(2,1)S(1)}, u32[]{:S(2)}, u32[]{:S(2)}) collective-permute-start(bf16[16,64,128]{2,1,0:T(8,128)(2,1)S(1)} %get-tuple-element.55), channel_id=1, source_target_pairs={{0,248},{8,16},{16,8},{24,32},{32,24},{40,48},{48,40},{56,64},{64,... | collective-permute-start | bytes 786440 | tf_op jit(solution)/shard_map/ppermute | solution.py:453
  13.1 1.2 %collective-permute-start.2 = (f32[16,4,128]{2,1,0:T(4,128)S(1)}, f32[16,4,128]{2,1,0:T(4,128)S(1)}, u32[]{:S(2)}, u32[]{:S(2)}) collective-permute-start(f32[16,4,128]{2,1,0:T(4,128)S(1)} %get-tuple-element.56), channel_id=1, source_target_pairs={{0,1},{1,0},{2,3},{3,2},{4,5},{5,4},{6,7},{7,6},{8,9},{9,8},{10,11... | collective-permute-start | bytes 98312 | tf_op jit(solution)/shard_map/ppermute | solution.py:453
  15.4 3.8 %split_inner.1 = (f32[16,4,80,128]{3,2,1,0:T(8,128)S(1)}, f32[16,4,80,128]{3,2,1,0:T(8,128)S(1)}, f32[16,4,64,128]{3,2,1,0:T(8,128)S(1)}, f32[16,4,64,128]{3,2,1...) custom-call(bf16[16,4,64,256]{3,2,1,0:T(8,128)(2,1)} %spins_ref.3, ...), custom_call_target="tpu_custom_call", output_to_operand_aliasing={{0}: (3, {}), {1}: (4, {})} | custom-call | flops 10000000 | bytes 2097152 | tf_op jit(solution)/shard_map/split_inner/pallas_call | solution.py:212
  19.2 1.7 %sweep_outer_0.1 = (f32[16,4,80,128]{3,2,1,0:T(8,128)S(1)}, f32[16,4,80,128]{3,2,1,0:T(8,128)S(1)}, bf16[16,64,128]{2,1,0:T(8,128)(2,1)S(1)}, bf16[16,64,128]{2,1,0:T(8,128)(2,1)S(1)}) custom-call(s32[2]{0:T(128)S(1)} %pad_add_fusion.side_ref, f32[16]{0:T(128)S(1)} %copy-done, ...), custom_call_target="tpu_custom_call", output_to_operand_aliasing={{0}: (2, {}), {1}: (3, {})} | custom-call | flops 10000000 | bytes 2097152 | tf_op jit(solution)/shard_map/sweep_outer_0/pallas_call | solution.py:339
  21.0 4.1 %collective-permute-start.5 = (bf16[16,64,128]{2,1,0:T(8,128)(2,1)S(1)}, bf16[16,64,128]{2,1,0:T(8,128)(2,1)S(1)}, u32[]{:S(2)}, u32[]{:S(2)}) collective-permute-start(bf16[16,64,128]{2,1,0:T(8,128)(2,1)S(1)} %get-tuple-element.65), channel_id=1, source_target_pairs={{0,248},{8,16},{16,8},{24,32},{32,24},{40,48},{48,40},{56,64},{64,... | collective-permute-start | bytes 786440 | tf_op jit(solution)/shard_map/ppermute | solution.py:453
  25.2 1.6 %sweep_inner_0.1 = (f32[16,4,80,128]{3,2,1,0:T(8,128)S(1)}, f32[16,4,80,128]{3,2,1,0:T(8,128)S(1)}, f32[16,4,128]{2,1,0:T(4,128)S(1)}, f32[16,4,128]{2,1,0:T(4,128)S(1)}) custom-call(s32[2]{0:T(128)S(1)} %pad_add_fusion.side_ref, f32[16]{0:T(128)S(1)} %copy-done, ...), custom_call_target="tpu_custom_call", output_to_operand_aliasing={{0}: (2, {}), {1}: (3, {})} | custom-call | flops 10000000 | bytes 2097152 | tf_op jit(solution)/shard_map/sweep_inner_0/pallas_call | solution.py:351
  26.8 2.2 %collective-permute-start.6 = (f32[16,4,128]{2,1,0:T(4,128)S(1)}, f32[16,4,128]{2,1,0:T(4,128)S(1)}, u32[]{:S(2)}, u32[]{:S(2)}) collective-permute-start(f32[16,4,128]{2,1,0:T(4,128)S(1)} %get-tuple-element.66), channel_id=1, source_target_pairs={{0,1},{1,0},{2,3},{3,2},{4,5},{5,4},{6,7},{7,6},{8,9},{9,8},{10,11... | collective-permute-start | bytes 98312 | tf_op jit(solution)/shard_map/ppermute | solution.py:453
  30.2 2.4 %collective-permute-done.7.yo = f32[16,4,128]{2,1,0:T(4,128)S(1)} collective-permute-done((f32[16,4,128]{2,1,0:T(4,128)S(1)}, f32[16,4,128]{2,1,0:T(4,128)S(1)}, u32[]{:S(2)}, u32[]{:S(2)}) %collective-permute-start.7) | collective-permute-done | bytes 32800 | tf_op jit(solution)/shard_map/ppermute | solution.py:453
  32.6 1.7 %sweep_outer_1.1 = (f32[16,4,80,128]{3,2,1,0:T(8,128)S(1)}, f32[16,4,80,128]{3,2,1,0:T(8,128)S(1)}, bf16[16,64,128]{2,1,0:T(8,128)(2,1)S(1)}, bf16[16,64,128]{2,1,0:T(8,128)(2,1)S(1)}) custom-call(s32[2]{0:T(128)S(1)} %pad_add_fusion.side_ref, f32[16]{0:T(128)S(1)} %copy-done, ...), custom_call_target="tpu_custom_call", output_to_operand_aliasing={{0}: (2, {}), {1}: (3, {})} | custom-call | flops 10000000 | bytes 2097152 | tf_op jit(solution)/shard_map/sweep_outer_1/pallas_call | solution.py:339
  34.4 2.1 %collective-permute-start.9 = (bf16[16,64,128]{2,1,0:T(8,128)(2,1)S(1)}, bf16[16,64,128]{2,1,0:T(8,128)(2,1)S(1)}, u32[]{:S(2)}, u32[]{:S(2)}) collective-permute-start(bf16[16,64,128]{2,1,0:T(8,128)(2,1)S(1)} %get-tuple-element.74), channel_id=1, source_target_pairs={{0,248},{8,16},{16,8},{24,32},{32,24},{40,48},{48,40},{56,64},{64,... | collective-permute-start | bytes 786440 | tf_op jit(solution)/shard_map/ppermute | solution.py:453
  36.5 1.6 %sweep_inner_1.1 = (f32[16,4,80,128]{3,2,1,0:T(8,128)S(1)}, f32[16,4,80,128]{3,2,1,0:T(8,128)S(1)}, f32[16,4,128]{2,1,0:T(4,128)S(1)}, f32[16,4,128]{2,1,0:T(4,128)S(1)}) custom-call(s32[2]{0:T(128)S(1)} %pad_add_fusion.side_ref, f32[16]{0:T(128)S(1)} %copy-done, ...), custom_call_target="tpu_custom_call", output_to_operand_aliasing={{0}: (2, {}), {1}: (3, {})} | custom-call | flops 10000000 | bytes 2097152 | tf_op jit(solution)/shard_map/sweep_inner_1/pallas_call | solution.py:351
  38.0 3.0 %collective-permute-start.10 = (f32[16,4,128]{2,1,0:T(4,128)S(1)}, f32[16,4,128]{2,1,0:T(4,128)S(1)}, u32[]{:S(2)}, u32[]{:S(2)}) collective-permute-start(f32[16,4,128]{2,1,0:T(4,128)S(1)} %get-tuple-element.75), channel_id=1, source_target_pairs={{0,1},{1,0},{2,3},{3,2},{4,5},{5,4},{6,7},{7,6},{8,9},{9,8},{10,11... | collective-permute-start | bytes 98312 | tf_op jit(solution)/shard_map/ppermute | solution.py:453
  42.3 2.8 %split_draws.1 = (f32[16,4,64,128]{3,2,1,0:T(8,128)S(1)}, f32[16,4,64,128]{3,2,1,0:T(8,128)S(1)}) custom-call(bf16[2,16,4,64,256]{4,3,2,1,0:T(8,128)(2,1)} %uniform_ref.3), custom_call_target="tpu_custom_call" | custom-call | flops 10000000 | bytes 2097152 | tf_op jit(solution)/shard_map/split_draws/pallas_call | solution.py:238
  45.1 1.7 %sweep_outer_2.1 = (f32[16,4,80,128]{3,2,1,0:T(8,128)S(1)}, f32[16,4,80,128]{3,2,1,0:T(8,128)S(1)}, bf16[16,64,128]{2,1,0:T(8,128)(2,1)S(1)}, bf16[16,64,128]{2,1,0:T(8,128)(2,1)S(1)}) custom-call(s32[2]{0:T(128)S(1)} %pad_add_fusion.side_ref, f32[16]{0:T(128)S(1)} %copy-done, ...), custom_call_target="tpu_custom_call", output_to_operand_aliasing={{0}: (2, {}), {1}: (3, {})} | custom-call | flops 10000000 | bytes 2097152 | tf_op jit(solution)/shard_map/sweep_outer_2/pallas_call | solution.py:339
  46.9 1.3 %collective-permute-start.15 = (bf16[16,64,128]{2,1,0:T(8,128)(2,1)S(1)}, bf16[16,64,128]{2,1,0:T(8,128)(2,1)S(1)}, u32[]{:S(2)}, u32[]{:S(2)}) collective-permute-start(bf16[16,64,128]{2,1,0:T(8,128)(2,1)S(1)} %get-tuple-element.87), channel_id=1, source_target_pairs={{0,248},{8,16},{16,8},{24,32},{32,24},{40,48},{48,40},{56,64},{64,... | collective-permute-start | bytes 786440 | tf_op jit(solution)/shard_map/ppermute | solution.py:453
  48.2 1.5 %sweep_inner_2.1 = (f32[16,4,80,128]{3,2,1,0:T(8,128)S(1)}, f32[16,4,80,128]{3,2,1,0:T(8,128)S(1)}, f32[16,4,128]{2,1,0:T(4,128)S(1)}, f32[16,4,128]{2,1,0:T(4,128)S(1)}) custom-call(s32[2]{0:T(128)S(1)} %pad_add_fusion.side_ref, f32[16]{0:T(128)S(1)} %copy-done, ...), custom_call_target="tpu_custom_call", output_to_operand_aliasing={{0}: (2, {}), {1}: (3, {})} | custom-call | flops 10000000 | bytes 2097152 | tf_op jit(solution)/shard_map/sweep_inner_2/pallas_call | solution.py:351
  49.8 3.0 %collective-permute-start.12 = (f32[16,4,128]{2,1,0:T(4,128)S(1)}, f32[16,4,128]{2,1,0:T(4,128)S(1)}, u32[]{:S(2)}, u32[]{:S(2)}) collective-permute-start(f32[16,4,128]{2,1,0:T(4,128)S(1)} %get-tuple-element.82), channel_id=1, source_target_pairs={{0,1},{1,0},{2,3},{3,2},{4,5},{5,4},{6,7},{7,6},{8,9},{9,8},{10,11... | collective-permute-start | bytes 98312 | tf_op jit(solution)/shard_map/ppermute | solution.py:453
  54.0 2.4 %collective-permute-done.13.yo = f32[16,4,128]{2,1,0:T(4,128)S(1)} collective-permute-done((f32[16,4,128]{2,1,0:T(4,128)S(1)}, f32[16,4,128]{2,1,0:T(4,128)S(1)}, u32[]{:S(2)}, u32[]{:S(2)}) %collective-permute-start.13) | collective-permute-done | bytes 32800 | tf_op jit(solution)/shard_map/ppermute | solution.py:453
  56.4 1.6 %final_inner.1 = (f32[16,4,80,128]{3,2,1,0:T(8,128)S(1)}, f32[16,4,80,128]{3,2,1,0:T(8,128)S(1)}, f32[16,8,128]{2,1,0:T(8,128)S(1)}) custom-call(s32[2]{0:T(128)S(1)} %pad_add_fusion.side_ref, f32[16]{0:T(128)S(1)} %copy-done, f32[16,4,80,128]{3,2,1,0:T(8,128)S(1)} %get-tuple-element.79.own_in, ...), custom_call_target="tpu_custom_call", output_to_operand_aliasing={{0}: (2, {}), {1}: (3, {})} | custom-call | flops 10000000 | bytes 2097152 | tf_op jit(solution)/shard_map/final_inner/pallas_call | solution.py:363
  58.1 1.8 %final_outer.1 = (f32[16,4,80,128]{3,2,1,0:T(8,128)S(1)}, f32[16,4,80,128]{3,2,1,0:T(8,128)S(1)}, f32[256,1,16]{2,1,0:T(1,128)S(1)}) custom-call(s32[2]{0:T(128)S(1)} %pad_add_fusion.side_ref, f32[16]{0:T(128)S(1)} %copy-done, f32[16,4,80,128]{3,2,1,0:T(8,128)S(1)} %get-tuple-element.84.own_in, ...), custom_call_target="tpu_custom_call", output_to_operand_aliasing={{0}: (2, {}), {1}: (3, {})} | custom-call | flops 10000000 | bytes 2097152 | tf_op jit(solution)/shard_map/final_outer/pallas_call | solution.py:375
  59.9 21.6 %all_to_all.5.sums_ref = f32[256,1,16]{2,1,0:T(1,128)S(1)} all-to-all(f32[256,1,16]{2,1,0:T(1,128)S(1)} %get-tuple-element.89), channel_id=1, replica_groups=mesh['gx'=32,'gy'=8] {'gx','gy'}, dimensions={0} | all-to-all | bytes 32768 | tf_op jit(solution)/shard_map/all_to_all | solution.py:480
  81.5 4.1 %mix_and_join.1 = (bf16[16,4,64,256]{3,2,1,0:T(8,128)(2,1)}, f32[1,16]{1,0:T(1,128)}) custom-call(f32[16]{0:T(128)S(1)} %copy-done, f32[8]{0:T(128)S(1)} %copy-done.1, f32[256,1,16]{2,1,0:T(1,128)S(1)} %all_to_all.5.sums_ref, f32[16,4,80,128]{3,2,1,0:T(8,128)S(1)} %get-tuple-element.90.a0, f32[16,4,80,128]{3,2,1,0:T(8,128)S(1)} %get-tuple-element.91.a1), custom_call_target="tpu_custom_call" | custom-call | flops 10000000 | bytes 2097152 | tf_op jit(solution)/shard_map/mix_and_join/pallas_call | solution.py:437
  (26 shorter events, 5.1 us)
Async XLA Ops:
  3.7 15.5 %collective-permute-start = (bf16[16,64,128]{2,1,0:T(8,128)(2,1)S(1)}, bf16[16,64,128]{2,1,0:T(8,128)(2,1)S(1)}, u32[]{:S(2)}, u32[]{:S(2)}) collective-permute-start(bf16[16,64,128]{2,1,0:T(8,128)(2,1)S(1)} %get-tuple-element.54), channel_id=1, source_target_pairs={{0,8},{8,0},{16,24},{24,16},{32,40},{40,32},{48,56},{56,48},{64,72... | collective-permute-start | bytes 786440 | tf_op jit(solution)/shard_map/ppermute | solution.py:453
  5.9 13.3 %collective-permute-start.1 = (bf16[16,64,128]{2,1,0:T(8,128)(2,1)S(1)}, bf16[16,64,128]{2,1,0:T(8,128)(2,1)S(1)}, u32[]{:S(2)}, u32[]{:S(2)}) collective-permute-start(bf16[16,64,128]{2,1,0:T(8,128)(2,1)S(1)} %get-tuple-element.55), channel_id=1, source_target_pairs={{0,248},{8,16},{16,8},{24,32},{32,24},{40,48},{48,40},{56,64},{64,... | collective-permute-start | bytes 786440 | tf_op jit(solution)/shard_map/ppermute | solution.py:453
  13.1 6.1 %collective-permute-start.2 = (f32[16,4,128]{2,1,0:T(4,128)S(1)}, f32[16,4,128]{2,1,0:T(4,128)S(1)}, u32[]{:S(2)}, u32[]{:S(2)}) collective-permute-start(f32[16,4,128]{2,1,0:T(4,128)S(1)} %get-tuple-element.56), channel_id=1, source_target_pairs={{0,1},{1,0},{2,3},{3,2},{4,5},{5,4},{6,7},{7,6},{8,9},{9,8},{10,11... | collective-permute-start | bytes 98312 | tf_op jit(solution)/shard_map/ppermute | solution.py:453
  14.3 4.9 %collective-permute-start.3 = (f32[16,4,128]{2,1,0:T(4,128)S(1)}, f32[16,4,128]{2,1,0:T(4,128)S(1)}, u32[]{:S(2)}, u32[]{:S(2)}) collective-permute-start(f32[16,4,128]{2,1,0:T(4,128)S(1)} %get-tuple-element.57), channel_id=1, source_target_pairs={{0,7},{1,2},{2,1},{3,4},{4,3},{5,6},{6,5},{7,0},{8,15},{9,10},{10,... | collective-permute-start | bytes 98312 | tf_op jit(solution)/shard_map/ppermute | solution.py:453
  15.4 3.8 %copy-start = (f32[16]{0:T(128)S(1)}, f32[16]{0:T(128)}, u32[]{:S(2)}) copy-start(f32[16]{0:T(128)} %betas_ref.17) | copy-start | bytes 196
  20.9 11.6 %collective-permute-start.4 = (bf16[16,64,128]{2,1,0:T(8,128)(2,1)S(1)}, bf16[16,64,128]{2,1,0:T(8,128)(2,1)S(1)}, u32[]{:S(2)}, u32[]{:S(2)}) collective-permute-start(bf16[16,64,128]{2,1,0:T(8,128)(2,1)S(1)} %get-tuple-element.64), channel_id=1, source_target_pairs={{0,8},{8,0},{16,24},{24,16},{32,40},{40,32},{48,56},{56,48},{64,72... | collective-permute-start | bytes 786440 | tf_op jit(solution)/shard_map/ppermute | solution.py:453
  21.0 11.5 %collective-permute-start.5 = (bf16[16,64,128]{2,1,0:T(8,128)(2,1)S(1)}, bf16[16,64,128]{2,1,0:T(8,128)(2,1)S(1)}, u32[]{:S(2)}, u32[]{:S(2)}) collective-permute-start(bf16[16,64,128]{2,1,0:T(8,128)(2,1)S(1)} %get-tuple-element.65), channel_id=1, source_target_pairs={{0,248},{8,16},{16,8},{24,32},{32,24},{40,48},{48,40},{56,64},{64,... | collective-permute-start | bytes 786440 | tf_op jit(solution)/shard_map/ppermute | solution.py:453
  26.8 3.4 %collective-permute-start.6 = (f32[16,4,128]{2,1,0:T(4,128)S(1)}, f32[16,4,128]{2,1,0:T(4,128)S(1)}, u32[]{:S(2)}, u32[]{:S(2)}) collective-permute-start(f32[16,4,128]{2,1,0:T(4,128)S(1)} %get-tuple-element.66), channel_id=1, source_target_pairs={{0,1},{1,0},{2,3},{3,2},{4,5},{5,4},{6,7},{7,6},{8,9},{9,8},{10,11... | collective-permute-start | bytes 98312 | tf_op jit(solution)/shard_map/ppermute | solution.py:453
  29.0 3.6 %collective-permute-start.7 = (f32[16,4,128]{2,1,0:T(4,128)S(1)}, f32[16,4,128]{2,1,0:T(4,128)S(1)}, u32[]{:S(2)}, u32[]{:S(2)}) collective-permute-start(f32[16,4,128]{2,1,0:T(4,128)S(1)} %get-tuple-element.67), channel_id=1, source_target_pairs={{0,7},{1,2},{2,1},{3,4},{4,3},{5,6},{6,5},{7,0},{8,15},{9,10},{10,... | collective-permute-start | bytes 98312 | tf_op jit(solution)/shard_map/ppermute | solution.py:453
  34.3 10.8 %collective-permute-start.8 = (bf16[16,64,128]{2,1,0:T(8,128)(2,1)S(1)}, bf16[16,64,128]{2,1,0:T(8,128)(2,1)S(1)}, u32[]{:S(2)}, u32[]{:S(2)}) collective-permute-start(bf16[16,64,128]{2,1,0:T(8,128)(2,1)S(1)} %get-tuple-element.73), channel_id=1, source_target_pairs={{0,8},{8,0},{16,24},{24,16},{32,40},{40,32},{48,56},{56,48},{64,72... | collective-permute-start | bytes 786440 | tf_op jit(solution)/shard_map/ppermute | solution.py:453
  34.4 10.7 %collective-permute-start.9 = (bf16[16,64,128]{2,1,0:T(8,128)(2,1)S(1)}, bf16[16,64,128]{2,1,0:T(8,128)(2,1)S(1)}, u32[]{:S(2)}, u32[]{:S(2)}) collective-permute-start(bf16[16,64,128]{2,1,0:T(8,128)(2,1)S(1)} %get-tuple-element.74), channel_id=1, source_target_pairs={{0,248},{8,16},{16,8},{24,32},{32,24},{40,48},{48,40},{56,64},{64,... | collective-permute-start | bytes 786440 | tf_op jit(solution)/shard_map/ppermute | solution.py:453
  38.0 7.1 %collective-permute-start.10 = (f32[16,4,128]{2,1,0:T(4,128)S(1)}, f32[16,4,128]{2,1,0:T(4,128)S(1)}, u32[]{:S(2)}, u32[]{:S(2)}) collective-permute-start(f32[16,4,128]{2,1,0:T(4,128)S(1)} %get-tuple-element.75), channel_id=1, source_target_pairs={{0,1},{1,0},{2,3},{3,2},{4,5},{5,4},{6,7},{7,6},{8,9},{9,8},{10,11... | collective-permute-start | bytes 98312 | tf_op jit(solution)/shard_map/ppermute | solution.py:453
  41.1 4.0 %collective-permute-start.11 = (f32[16,4,128]{2,1,0:T(4,128)S(1)}, f32[16,4,128]{2,1,0:T(4,128)S(1)}, u32[]{:S(2)}, u32[]{:S(2)}) collective-permute-start(f32[16,4,128]{2,1,0:T(4,128)S(1)} %get-tuple-element.76), channel_id=1, source_target_pairs={{0,7},{1,2},{2,1},{3,4},{4,3},{5,6},{6,5},{7,0},{8,15},{9,10},{10,... | collective-permute-start | bytes 98312 | tf_op jit(solution)/shard_map/ppermute | solution.py:453
  46.8 11.2 %collective-permute-start.14 = (bf16[16,64,128]{2,1,0:T(8,128)(2,1)S(1)}, bf16[16,64,128]{2,1,0:T(8,128)(2,1)S(1)}, u32[]{:S(2)}, u32[]{:S(2)}) collective-permute-start(bf16[16,64,128]{2,1,0:T(8,128)(2,1)S(1)} %get-tuple-element.86), channel_id=1, source_target_pairs={{0,8},{8,0},{16,24},{24,16},{32,40},{40,32},{48,56},{56,48},{64,72... | collective-permute-start | bytes 786440 | tf_op jit(solution)/shard_map/ppermute | solution.py:453
  46.9 11.1 %collective-permute-start.15 = (bf16[16,64,128]{2,1,0:T(8,128)(2,1)S(1)}, bf16[16,64,128]{2,1,0:T(8,128)(2,1)S(1)}, u32[]{:S(2)}, u32[]{:S(2)}) collective-permute-start(bf16[16,64,128]{2,1,0:T(8,128)(2,1)S(1)} %get-tuple-element.87), channel_id=1, source_target_pairs={{0,248},{8,16},{16,8},{24,32},{32,24},{40,48},{48,40},{56,64},{64,... | collective-permute-start | bytes 786440 | tf_op jit(solution)/shard_map/ppermute | solution.py:453
  49.8 4.2 %collective-permute-start.12 = (f32[16,4,128]{2,1,0:T(4,128)S(1)}, f32[16,4,128]{2,1,0:T(4,128)S(1)}, u32[]{:S(2)}, u32[]{:S(2)}) collective-permute-start(f32[16,4,128]{2,1,0:T(4,128)S(1)} %get-tuple-element.82), channel_id=1, source_target_pairs={{0,1},{1,0},{2,3},{3,2},{4,5},{5,4},{6,7},{7,6},{8,9},{9,8},{10,11... | collective-permute-start | bytes 98312 | tf_op jit(solution)/shard_map/ppermute | solution.py:453
  52.8 3.6 %collective-permute-start.13 = (f32[16,4,128]{2,1,0:T(4,128)S(1)}, f32[16,4,128]{2,1,0:T(4,128)S(1)}, u32[]{:S(2)}, u32[]{:S(2)}) collective-permute-start(f32[16,4,128]{2,1,0:T(4,128)S(1)} %get-tuple-element.83), channel_id=1, source_target_pairs={{0,7},{1,2},{2,1},{3,4},{4,3},{5,6},{6,5},{7,0},{8,15},{9,10},{10,... | collective-permute-start | bytes 98312 | tf_op jit(solution)/shard_map/ppermute | solution.py:453
  58.1 23.4 %copy-start.1 = (f32[8]{0:T(128)S(1)}, f32[8]{0:T(128)}, u32[]{:S(2)}) copy-start(f32[8]{0:T(128)} %swap_ref.1) | copy-start | bytes 100

commit v3 on v2

v3 whole, which is shorter than its diff:
```python
import functools
import math

import jax
import jax.numpy as jnp
from jax import lax
from jax.experimental import pallas as pl
from jax.experimental.pallas import tpu as pltpu
from jax.sharding import PartitionSpec as P


R = 16
CX, CY, NZ = 4, 64, 256
HALF = NZ // 2
PAD = 8
UNROLL = 4
PAIRS = 2
FIRST, LAST, OUTER, INNER = (0,), (CX - 1,), (0, CX - 1), (1, 2)
FLIP, UPPER, BETAS, DRAWN, TABLE_ROWS = R, R + 1, R + 2, R + 3, R + 8
LOG2E = math.log2(math.e)
F32 = jnp.float32
BF16 = jnp.bfloat16
MIB = 1024 * 1024

swap_width = 0.25
swap_gain = 64.0

VM = pl.BlockSpec(memory_space=pltpu.VMEM)
SM = pl.BlockSpec(memory_space=pltpu.SMEM)
HB = pl.BlockSpec(memory_space=pltpu.HBM)


def in_hbm(x):
    return pltpu.with_memory_space_constraint(x, pltpu.HBM)


def split_matrix():
    row = lax.broadcasted_iota(jnp.int32, (NZ, NZ), 0)
    col = lax.broadcasted_iota(jnp.int32, (NZ, NZ), 1)
    wanted = jnp.where(col < HALF, 2 * col, 2 * (col - HALF) + 1)
    return (row == wanted).astype(F32).astype(BF16)


def join_matrix():
    row = lax.broadcasted_iota(jnp.int32, (NZ, NZ), 0)
    col = lax.broadcasted_iota(jnp.int32, (NZ, NZ), 1)
    wanted = jnp.where(row < HALF, 2 * row, 2 * (row - HALF) + 1)
    return (col == wanted).astype(F32).astype(BF16)


def device_side():
    return lax.axis_index("gx") % 2, lax.axis_index("gy") % 2


def fill_table(side, betas_ref, swap_ref, table):
    place = lax.broadcasted_iota(jnp.int32, (1, HALF), 1)
    betas = jnp.zeros((1, HALF), F32)
    drawn = jnp.ones((1, HALF), F32)
    for r in range(R):
        table[r : r + 1, :] = jnp.full((1, HALF), betas_ref[r] * (-2.0 * LOG2E), F32)
        betas = jnp.where(place == r, betas_ref[r], betas)
    for k in range(R // 2):
        drawn = jnp.where(place == 2 * k, swap_ref[k], drawn)
    for i in range(2):
        table[R + i : R + i + 1, :] = jnp.full((1, HALF), side[i], jnp.int32).astype(F32)
    table[BETAS : BETAS + 1, :] = betas
    table[DRAWN : DRAWN + 1, :] = drawn


def odd_rows_of(table, rows):
    place = lax.broadcasted_iota(jnp.int32, (rows, HALF), 0) % 2
    return place.astype(F32) != jnp.broadcast_to(table[FLIP : FLIP + 1, :], (rows, HALF))


def odd_rows(side, rows=CY):
    return (lax.broadcasted_iota(jnp.int32, (rows, HALF), 0) + side[0]) % 2 == 1


def layer_at(side, x):
    return jnp.where(side[0] == 0, x, CX - 1 - x)


def by_colour(even, odd, x, odd_row):
    if x % 2 == 0:
        return jnp.where(odd_row, odd, even), jnp.where(odd_row, even, odd)
    return jnp.where(odd_row, even, odd), jnp.where(odd_row, odd, even)


def send_rows(table, own, yeven, yodd):
    lower = table[UPPER : UPPER + 1, :] == 0.0
    for r in range(R):
        for x in range(CX):
            first = own[r, x, PAD : PAD + 1, :]
            final = own[r, x, PAD + CY - 1 : PAD + CY, :]
            yeven[r, x : x + 1, :] = jnp.where(lower, final, first)
            yodd[r, x : x + 1, :] = jnp.where(lower, first, final)


STATE = pltpu.VMEM((R, CX, CY + 2 * PAD, HALF), F32)
DRAWS = pltpu.VMEM((R, CX, CY, HALF), F32)
BONDS = pltpu.VMEM((6, CX, CY, HALF), F32)
LAYER = jax.ShapeDtypeStruct((R, CY, HALF), BF16)
ROWS = jax.ShapeDtypeStruct((R, CX, HALF), F32)
TABLE = jax.ShapeDtypeStruct((TABLE_ROWS, HALF), F32)


def call(kernel, outs, in_specs, out_specs, scratch=(), aliases={}, limit=8, flops=10**7):
    return pl.pallas_call(
        kernel,
        out_shape=outs,
        in_specs=in_specs,
        out_specs=out_specs,
        scratch_shapes=list(scratch),
        input_output_aliases=aliases,
        compiler_params=pltpu.CompilerParams(vmem_limit_bytes=limit * MIB),
        cost_estimate=pl.CostEstimate(flops=flops, bytes_accessed=2 * MIB, transcendentals=0),
    )


def split_outer(spins_ref, a0, a1, xeven, xodd, yeven, yodd, layers, edge_rows, split_rows, sems):
    side = device_side()
    copies = []
    for i, x in enumerate(OUTER):
        copies.append(pltpu.make_async_copy(spins_ref.at[:, layer_at(side, x)], layers.at[i], sems.at[i]))
    for i, y in enumerate((0, CY - 8)):
        copies.append(
            pltpu.make_async_copy(
                spins_ref.at[:, pl.ds(1, 2), pl.ds(y, 8)], edge_rows.at[i], sems.at[2 + i]
            )
        )
    for copy in copies:
        copy.start()
    matrix = split_matrix()
    odd_row = odd_rows(side)
    for i, x in enumerate(OUTER):
        copies[i].wait()

        cells = layers[i].reshape(R * CY, NZ)
        parts = jnp.dot(cells, matrix, preferred_element_type=F32)
        for r in range(R):
            rows = parts[r * CY : (r + 1) * CY]
            c0, c1 = by_colour(rows[:, :HALF], rows[:, HALF:], x, odd_row)
            a0[r, x, PAD : PAD + CY, :] = c0
            a1[r, x, PAD : PAD + CY, :] = c1
            (xodd if x == 0 else xeven)[r] = c1.astype(BF16)

    for i in range(2):
        copies[2 + i].wait()
        cells = edge_rows[i].reshape(R * 2 * 8, NZ)
        split_rows[i] = jnp.dot(cells, matrix, preferred_element_type=F32).reshape(R, 2, 8, NZ)
    lower = side[1] == 0
    plain = side[0] == 0
    for r in range(R):
        for x in range(CX):
            if x in OUTER:
                first = a1[r, x, PAD : PAD + 1, :]
                final = a1[r, x, PAD + CY - 1 : PAD + CY, :]
            else:
                at = x - 1
                first = jnp.where(
                    plain,
                    split_rows[0, r, at, 0:1, at * HALF : (at + 1) * HALF],
                    split_rows[0, r, 1 - at, 0:1, (1 - at) * HALF : (2 - at) * HALF],
                )
                final = jnp.where(
                    plain,
                    split_rows[1, r, at, 7:8, (1 - at) * HALF : (2 - at) * HALF],
                    split_rows[1, r, 1 - at, 7:8, at * HALF : (at + 1) * HALF],
                )
            yeven[r, x : x + 1, :] = jnp.where(lower, final, first)
            yodd[r, x : x + 1, :] = jnp.where(lower, first, final)


def run_split_outer(spins):
    return call(
        split_outer,
        [STATE] * 2 + [LAYER] * 2 + [ROWS] * 2,
        [HB],
        [VM] * 6,
        [
            pltpu.VMEM((2, R, CY, NZ), BF16),
            pltpu.VMEM((2, R, 2, 8, NZ), BF16),
            pltpu.VMEM((2, R, 2, 8, NZ), F32),
            pltpu.SemaphoreType.DMA((4,)),
        ],
    )(in_hbm(spins))


def split_field(side, buf, u0, u1, matrix, plain_row):
    @pl.loop(0, R, step=4)
    def _(first):
        cells = buf[pl.ds(first, 4)].reshape(4 * CX * CY, NZ)
        parts = jnp.dot(cells, matrix, preferred_element_type=F32) * 5.0
        for k in range(4 * CX):
            rows = parts[k * CY : (k + 1) * CY]
            r, at = first + k // CX, k % CX
            x = layer_at(side, at)
            c0, c1 = by_colour(rows[:, :HALF], rows[:, HALF:], at, plain_row)
            u0[r, x] = c0
            u1[r, x] = c1


def split_inner(betas_ref, swap_ref, spins_ref, couplings_ref, uniform_ref, a0_in, a1_in, *refs):
    side = device_side()
    a0, a1, u00, u01, u10, u11, bonds0, bonds1, table, layers, bond_buf, buf, sems = refs

    copies = [
        pltpu.make_async_copy(spins_ref.at[:, pl.ds(1, 2)], layers, sems.at[0]),
        pltpu.make_async_copy(couplings_ref, bond_buf, sems.at[1]),
        pltpu.make_async_copy(uniform_ref.at[0], buf.at[0], sems.at[2]),
        pltpu.make_async_copy(uniform_ref.at[1], buf.at[1], sems.at[3]),
    ]
    for copy in copies:
        copy.start()
    matrix = split_matrix()
    plain_row = lax.broadcasted_iota(jnp.int32, (CY, HALF), 0) % 2 == 1
    fill_table(side, betas_ref, swap_ref, table)
    copies[0].wait()

    @pl.loop(0, R, step=8)
    def _(first):
        cells = layers[pl.ds(first, 8)].reshape(16 * CY, NZ)
        parts = jnp.dot(cells, matrix, preferred_element_type=F32)
        for k in range(16):
            rows = parts[k * CY : (k + 1) * CY]
            x = layer_at(side, 1 + k % 2)
            c0, c1 = by_colour(rows[:, :HALF], rows[:, HALF:], 1 + k % 2, plain_row)
            a0[first + k // 2, x, PAD : PAD + CY, :] = c0
            a1[first + k // 2, x, PAD : PAD + CY, :] = c1

    copies[1].wait()
    flip = side[0]
    for at in range(CX):
        x = layer_at(side, at)
        halves = []
        for k in range(6):
            cells = bond_buf[k, at].astype(F32).astype(BF16)
            parts = jnp.dot(cells, matrix, preferred_element_type=F32)
            halves.append((parts[:, :HALF], parts[:, HALF:]))
        for place, k in ((flip, 0), (1 - flip, 3), (2, 1), (3, 4)):
            bonds0[place, x], bonds1[place, x] = by_colour(*halves[k], at, plain_row)
        for place, (k, m) in enumerate(((2, 5), (5, 2))):
            bonds0[4 + place, x], bonds1[4 + place, x] = by_colour(halves[k][0], halves[m][1], at, plain_row)
    copies[2].wait()
    split_field(side, buf.at[0], u00, u01, matrix, plain_row)
    copies[3].wait()
    split_field(side, buf.at[1], u10, u11, matrix, plain_row)


def run_split_inner(betas, swap, spins, couplings, uniform, a0, a1):
    return call(
        split_inner,
        [STATE] * 2 + [DRAWS] * 4 + [BONDS] * 2 + [TABLE],
        [SM] * 2 + [HB] * 3 + [VM] * 2,
        [VM] * 9,
        [
            pltpu.VMEM((R, 2, CY, NZ), BF16),
            pltpu.VMEM((6, CX, CY, NZ), jnp.int32),
            pltpu.VMEM((2, R, CX, CY, NZ), BF16),
            pltpu.SemaphoreType.DMA((4,)),
        ],
        {5: 0, 6: 1},
        limit=12,
    )(betas, swap, in_hbm(spins), in_hbm(couplings), in_hbm(uniform), a0, a1)


def put_rows(table, other, yeven, yodd):
    lower = table[UPPER : UPPER + 1, :] == 0.0
    for r in range(R):
        for x in range(CX):
            even, odd = yeven[r, x : x + 1, :], yodd[r, x : x + 1, :]
            other[r, x, PAD - 1 : PAD, :] = jnp.where(lower, odd, even)
            other[r, x, PAD + CY : PAD + CY + 1, :] = jnp.where(lower, even, odd)


def update(colour, regions, table, own, other, u_ref, bonds_ref, beyond, sent, energy):
    odd_row = odd_rows_of(table, 16)

    @pl.loop(0, R, step=UNROLL)
    def _(first):
        sums = [jnp.zeros((8, HALF), F32) for _ in range(UNROLL)]
        scales = [jnp.broadcast_to(table[pl.ds(first + i, 1), :], (16, HALF)) for i in range(UNROLL)]
        for x, y, rows in regions:
            bonds = [bonds_ref[k, x, y : y + rows, :] for k in range(6)]
            odd = odd_row[:rows]
            for i in range(UNROLL):
                r = first + i

                def near(dx, dy):
                    at = x + dx
                    if at < 0:
                        return beyond[r, y : y + rows, :].astype(F32)
                    if at >= CX:
                        return beyond[r, y : y + rows, :].astype(F32)
                    return other[r, at, PAD + y + dy : PAD + y + dy + rows, :]

                same = near(0, 0)
                below, above = pltpu.roll(same, 1, 1), pltpu.roll(same, HALF - 1, 1)
                if (colour + x) % 2 == 0:
                    beside = jnp.where(odd, above, below)
                else:
                    beside = jnp.where(odd, below, above)
                field = bonds[0] * near(1, 0) + bonds[1] * near(-1, 0)
                field = field + (bonds[2] * near(0, 1) + bonds[3] * near(0, -1))
                field = field + (bonds[4] * same + bonds[5] * beside)
                spin = own[r, x, PAD + y : PAD + y + rows, :]
                accept = jnp.exp2(jnp.minimum(spin * field * scales[i][:rows], 0.0))
                new = (spin * jnp.tanh(u_ref[r, x, y : y + rows, :] - 5.0 * accept)).astype(BF16)
                wide = new.astype(F32)
                own[r, x, PAD + y : PAD + y + rows, :] = wide
                if sent is not None and x in OUTER:
                    sent[r, y : y + rows, :] = new
                if energy is not None:
                    for part in range(0, rows, 8):
                        sums[i] = sums[i] + (wide * field)[part : part + 8]
        if energy is not None:
            for i in range(UNROLL):
                energy[first + i] = sums[i]


def rows_of(layers, start=0, stop=CY, rows=16):
    return [(x, y, rows) for x in layers for y in range(start, stop, rows)]


EDGES = rows_of(INNER, 0, 8, 8) + rows_of(INNER, CY - 8, CY, 8)
ENERGY = jax.ShapeDtypeStruct((R, 8, HALF), F32)


def sweep_first(colour, table, own_in, other_in, u, bonds, halo, yeven, yodd, own, other, sent):
    put_rows(table, other, yeven, yodd)
    update(colour, rows_of(FIRST), table, own, other, u, bonds, halo, sent, None)


def sweep_last(colour, edges, table, own_in, other_in, u, bonds, halo, own, other, sent, *rest):
    update(colour, rows_of(LAST) + (EDGES if edges else []), table, own, other, u, bonds, halo, sent, None)
    if edges:
        send_rows(table, own, *rest)


def sweep_inner(colour, edges, table, own_in, other_in, u, bonds, own, other, *rest):
    regions = rows_of(INNER, 8, CY - 8) if edges else rows_of(INNER)
    update(colour, regions, table, own, other, u, bonds, None, None, None)
    if not edges:
        send_rows(table, own, *rest)


def final_inner(table, own_in, other_in, u, bonds, yeven, yodd, own, other, energy):
    put_rows(table, other, yeven, yodd)
    update(1, rows_of(INNER), table, own, other, u, bonds, None, None, energy)


def final_last(table, own_in, other_in, u, bonds, halo, so_far, own, other, energy):
    update(1, rows_of(LAST), table, own, other, u, bonds, halo, None, energy)
    energy[...] = energy[...] + so_far[...]


def final_first(table, own_in, other_in, u, bonds, halo, so_far, own, other, sums_ref, energy):
    update(1, rows_of(FIRST), table, own, other, u, bonds, halo, None, energy)
    lines = jnp.sum(energy[...] + so_far[...], axis=1)
    totals = jnp.sum(lines, axis=1, keepdims=True)
    diagonal = lax.broadcasted_iota(jnp.int32, (R, R), 0) == lax.broadcasted_iota(jnp.int32, (R, R), 1)
    row = jnp.sum(jnp.where(diagonal, totals, 0.0), axis=0, keepdims=True)
    sums_ref[...] = jnp.broadcast_to(row[None], sums_ref.shape)


def sweep_call(kernel, more_ins, more_outs, scratch=()):
    def run(*operands):
        return call(
            kernel, [STATE] * 2 + more_outs, [VM] * (5 + more_ins), [VM] * (2 + len(more_outs)), scratch, {1: 0, 2: 1}
        )(*operands)

    return run


def mix_and_join(cell_count, table, sums_ref, a0, a1, out_ref, energies_ref, weights, buf, sems):
    total = jnp.sum(sums_ref[:, 0, :], axis=0, keepdims=True)
    energies = -total / cell_count
    energies_ref[...] = energies
    side = device_side()
    betas = table[BETAS : BETAS + 1, :R]
    drawn = table[DRAWN : DRAWN + 1, :R]
    beta_step = betas[:, : R - 1] - betas[:, 1:]
    energy_step = energies[:, : R - 1] - energies[:, 1:]
    delta = swap_gain * beta_step * energy_step
    mix = jax.nn.sigmoid((jnp.minimum(delta, 0.0) - jnp.log(drawn[:, : R - 1])) / swap_width)
    for k in range(R // 2):
        weights[k : k + 1, :] = jnp.broadcast_to(mix[:, 2 * k : 2 * k + 1], (1, HALF))
    matrix = join_matrix()
    odd_row = odd_rows(side)

    def out_copy(pair):
        at = pl.ds(pair * 2, 2)
        return pltpu.make_async_copy(buf.at[at], out_ref.at[at], sems.at[pair])

    def mix_pair(pair):
        weight = jnp.broadcast_to(weights[pl.ds(pair, 1), :], (CY, HALF))
        r = pair * 2
        cells = [[], []]
        for x in range(CX):
            new = [[], []]
            for state in (a0, a1):
                upper = state[r, x, PAD : PAD + CY, :]
                lower = state[r + 1, x, PAD : PAD + CY, :]
                moved = weight * (lower - upper)
                new[0].append(upper + moved)
                new[1].append(lower - moved)
            for i in range(2):
                even, odd = by_colour(*new[i], x, odd_row)
                cells[i].append(jnp.concatenate([even.astype(BF16), odd.astype(BF16)], axis=1))
        for i in range(2):
            joined = jnp.dot(jnp.concatenate(cells[i], axis=0), matrix, preferred_element_type=F32).astype(BF16)
            for x in range(CX):
                buf[r + i, layer_at(side, x)] = joined[x * CY : (x + 1) * CY]
        out_copy(pair).start()

    @pl.loop(0, R // 2, step=PAIRS)
    def _(first):
        for i in range(PAIRS):
            mix_pair(first + i)

    @pl.loop(0, R // 2)
    def _(pair):
        out_copy(pair).wait()


def run_mix_and_join(cell_count, table, sums, a0, a1):
    return call(
        functools.partial(mix_and_join, cell_count),
        [jax.ShapeDtypeStruct((R, CX, CY, NZ), BF16), jax.ShapeDtypeStruct((1, R), F32)],
        [VM] * 4,
        [HB, VM],
        [
            pltpu.VMEM((R // 2, HALF), F32),
            pltpu.VMEM((R, CX, CY, NZ), BF16),
            pltpu.SemaphoreType.DMA((R // 2,)),
        ],
    )(table, sums, a0, a1)


def swap_pairs(x, axis, odd):
    count = lax.axis_size(axis)
    return lax.ppermute(x, axis, [(i, (((i + odd) ^ 1) - odd) % count) for i in range(count)])


def exchange(axis, even, odd):
    near = swap_pairs(even, axis, 0)
    far = swap_pairs(odd, axis, 1)
    return [near, far]


def body(spins, couplings, betas, metro_uniform, swap_uniform):
    a0, a1, xe, xo, ye, yo = run_split_outer(spins)
    xs, ys = exchange("gx", xe, xo), exchange("gy", ye, yo)
    a0, a1, u00, u01, u10, u11, bonds0, bonds1, table = run_split_inner(
        betas, swap_uniform, spins, couplings, metro_uniform, a0, a1
    )
    states = [a0, a1]
    for step, (u, bonds) in enumerate(((u00, bonds0), (u01, bonds1), (u10, bonds0))):
        colour = step % 2
        own, other = states[colour], states[1 - colour]
        edges = step == 2
        run = sweep_call(functools.partial(sweep_first, colour), 3, [LAYER])
        own, other, xo = run(table, own, other, u, bonds, xs[1], *ys)
        run = sweep_call(functools.partial(sweep_last, colour, edges), 1, [LAYER] + ([ROWS] * 2 if edges else []))
        own, other, xe, *rows = run(table, own, other, u, bonds, xs[0])
        xs = exchange("gx", xe, xo)
        if edges:
            ys = exchange("gy", *rows)
        run = sweep_call(functools.partial(sweep_inner, colour, edges), 0, [] if edges else [ROWS] * 2)
        own, other, *rows = run(table, own, other, u, bonds)
        if not edges:
            ys = exchange("gy", *rows)
        states[colour], states[1 - colour] = own, other
    both = ("gx", "gy")
    count = lax.axis_size(both)
    a0, a1 = states
    a1, a0, energy = sweep_call(final_inner, 2, [ENERGY])(table, a1, a0, u11, bonds1, *ys)
    a1, a0, energy = sweep_call(final_last, 2, [ENERGY])(table, a1, a0, u11, bonds1, xs[0], energy)
    a1, a0, sums = sweep_call(
        final_first, 2, [pltpu.VMEM((count, 1, R), F32)], [pltpu.VMEM((R, 8, HALF), F32)]
    )(table, a1, a0, u11, bonds1, xs[1], energy)
    sums = lax.all_to_all(sums, both, 0, 0, tiled=True)
    cell_count = float(CX * CY * NZ * count)
    out, energies = run_mix_and_join(
        cell_count, table, sums, a0, a1
    )
    return out, energies[0]


def solution(mesh):
    return sharded(body, mesh)


def sharded(function, mesh):
    return jax.shard_map(
        function,
        mesh=mesh,
        in_specs=(
            P(None, "gx", "gy", None),
            P(None, "gx", "gy", None),
            P(),
            P(None, None, "gx", "gy", None),
            P(),
        ),
        out_specs=(P(None, "gx", "gy", None), P()),
        check_vma=False,
    )
```

time: 85.9 us -> 82.5 us (0.960)
  Pallas kernels: 26.8 us -> 21.7 us
  waiting for transfers between devices: 4.9 us -> 7.82 us
  starting transfers between devices: 31.4 us -> 28.6 us
  local copies, waits for them, and re-layouts: 0.01 us -> 1.31 us
    pallas_call x12 -> x15, Pallas kernels: 26.8 us -> 21.7 us  [the longest x12 10.6 us: run(): call(kernel, [STATE] * 2 + more_outs, [VM] * (5 + more_ins), [VM] * (2 +...]
    ppermute x16, waiting for transfers between devices: 4.9 us -> 7.82 us  [swap_pairs(): lax.ppermute(x, axis, [(i, ((i + odd ^ 1) - odd) % count) for i in range(...]
    ppermute x16, starting transfers between devices: 31.4 us -> 28.6 us  [swap_pairs(): lax.ppermute(x, axis, [(i, ((i + odd ^ 1) - odd) % count) for i in range(...]
    unnamed x4, local copies, waits for them, and re-layouts: 0.01 us -> 1.31 us
  transfers between devices with their start and end apart: 16 -> 16, of which waited for: 2 -> 4; matrix products, arithmetic and copies ran while one was open for 0% -> 0% of each run, Pallas kernels for 15% -> 18%
where the time goes in v3:
time: 82.5 us; the launch traced here: 82.3 us
  starting transfers between devices  28.6 us (35%)
  blocking collectives  22 us (27%)
  Pallas kernels  21.7 us (26%)
  waiting for transfers between devices  7.82 us (9%)
  local copies, waits for them, and re-layouts  1.31 us (2%)
  between operations  0.97 us (1%)
    ppermute x16, starting transfers between devices, swap_pairs(): lax.ppermute(x, axis, [(i, ((i + odd ^ 1) - odd) % count) for i in range(...  28.6 us
    all_to_all x1, blocking collectives, body(): sums = lax.all_to_all(sums, both, 0, 0, tiled=True)  22 us
    pallas_call x12, Pallas kernels, run(): call(kernel, [STATE] * 2 + more_outs, [VM] * (5 + more_ins), [VM] * (2 +...  10.6 us
    ppermute x16, waiting for transfers between devices, swap_pairs(): lax.ppermute(x, axis, [(i, ((i + odd ^ 1) - odd) % count) for i in range(...  7.82 us
    pallas_call x1, Pallas kernels, run_split_inner(): call(split_inner, [STATE] * 2 + [DRAWS] * 4 + [BONDS] * 2 + [TABLE], [SM]...  5.8 us
    pallas_call x1, Pallas kernels, run_mix_and_join(): call(functools.partial(mix_and_join, cell_count), [jax.ShapeDtypeStruct((...  2.96 us
    pallas_call x1, Pallas kernels, run_split_outer(): call(split_outer, [STATE] * 2 + [LAYER] * 2 + [ROWS] * 2, [HB], [VM] * 6,...  2.38 us
  transfers between devices with their start and end apart: 16, of which 4 were waited for; matrix products, arithmetic and copies ran while one was open for 0% of the time, Pallas kernels for 18%

profile of v3, /device:TPU:1, one launch (start us, length us, event | category | flops | bytes accessed | tf_op | source)
XLA Modules:
  0.0 82.3 jit_solution(13545478577741618277)
XLA Ops:
  0.6 2.4 %shard_map.68 = (f32[16,4,80,128]{3,2,1,0:T(8,128)S(1)}, f32[16,4,80,128]{3,2,1,0:T(8,128)S(1)}, bf16[16,64,128]{2,1,0:T(8,128)(2,1)S(1)}, bf16[16,64,128]{2,1,0...) custom-call(bf16[16,4,64,256]{3,2,1,0:T(8,128)(2,1)} %spins_ref.3), custom_call_target="tpu_custom_call" | custom-call | flops 10000000 | bytes 2097152 | tf_op jit(solution)/shard_map/pallas_call | solution.py:175
  3.0 8.9 %collective-permute-start = (bf16[16,64,128]{2,1,0:T(8,128)(2,1)S(1)}, bf16[16,64,128]{2,1,0:T(8,128)(2,1)S(1)}, u32[]{:S(2)}, u32[]{:S(2)}) collective-permute-start(bf16[16,64,128]{2,1,0:T(8,128)(2,1)S(1)} %get-tuple-element.65), channel_id=1, source_target_pairs={{0,248},{8,16},{16,8},{24,32},{32,24},{40,48},{48,40},{56,64},{64,... | collective-permute-start | bytes 786440 | tf_op jit(solution)/shard_map/ppermute | solution.py:442
  11.9 1.0 %collective-permute-start.1 = (f32[16,4,128]{2,1,0:T(4,128)S(1)}, f32[16,4,128]{2,1,0:T(4,128)S(1)}, u32[]{:S(2)}, u32[]{:S(2)}) collective-permute-start(f32[16,4,128]{2,1,0:T(4,128)S(1)} %get-tuple-element.66), channel_id=1, source_target_pairs={{0,1},{1,0},{2,3},{3,2},{4,5},{5,4},{6,7},{7,6},{8,9},{9,8},{10,11... | collective-permute-start | bytes 98312 | tf_op jit(solution)/shard_map/ppermute | solution.py:442
  12.9 1.1 %collective-permute-start.2 = (f32[16,4,128]{2,1,0:T(4,128)S(1)}, f32[16,4,128]{2,1,0:T(4,128)S(1)}, u32[]{:S(2)}, u32[]{:S(2)}) collective-permute-start(f32[16,4,128]{2,1,0:T(4,128)S(1)} %get-tuple-element.67), channel_id=1, source_target_pairs={{0,7},{1,2},{2,1},{3,4},{4,3},{5,6},{6,5},{7,0},{8,15},{9,10},{10,... | collective-permute-start | bytes 98312 | tf_op jit(solution)/shard_map/ppermute | solution.py:442
  15.3 5.8 %shard_map.69 = (f32[16,4,80,128]{3,2,1,0:T(8,128)S(1)}, f32[16,4,80,128]{3,2,1,0:T(8,128)S(1)}, f32[16,4,64,128]{3,2,1,0:T(8,128)S(1)}, f32[16,4,64,128]{3,2,1,...) custom-call(f32[16]{0:T(128)S(1)} %copy-done, ...), custom_call_target="tpu_custom_call", output_to_operand_aliasing={{0}: (5, {}), {1}: (6, {})} | custom-call | flops 10000000 | bytes 2097152 | tf_op jit(solution)/shard_map/pallas_call | solution.py:251
  21.9 1.4 %collective-permute-start.4 = (bf16[16,64,128]{2,1,0:T(8,128)(2,1)S(1)}, bf16[16,64,128]{2,1,0:T(8,128)(2,1)S(1)}, u32[]{:S(2)}, u32[]{:S(2)}) collective-permute-start(bf16[16,64,128]{2,1,0:T(8,128)(2,1)S(1)} %get-tuple-element.77), channel_id=1, source_target_pairs={{0,248},{8,16},{16,8},{24,32},{32,24},{40,48},{48,40},{56,64},{64,... | collective-permute-start | bytes 786440 | tf_op jit(solution)/shard_map/ppermute | solution.py:442
  24.5 1.1 %shard_map.72 = (f32[16,4,80,128]{3,2,1,0:T(8,128)S(1)}, f32[16,4,80,128]{3,2,1,0:T(8,128)S(1)}, f32[16,4,128]{2,1,0:T(4,128)S(1)}, f32[16,4,128]{2,1,0:T(4,128)S(1)}) custom-call(f32[24,128]{1,0:T(8,128)S(1)} %get-tuple-element.60.table, f32[16,4,80,128]{3,2,1,0:T(8,128)S(1)} %get-tuple-element.71.own_in, ...), custom_call_target="tpu_custom_call", output_to_operand_aliasing={{0}: (1, {}), {1}: (2, {})} | custom-call | flops 10000000 | bytes 2097152 | tf_op jit(solution)/shard_map/pallas_call | solution.py:368
  25.7 2.2 %collective-permute-start.5 = (f32[16,4,128]{2,1,0:T(4,128)S(1)}, f32[16,4,128]{2,1,0:T(4,128)S(1)}, u32[]{:S(2)}, u32[]{:S(2)}) collective-permute-start(f32[16,4,128]{2,1,0:T(4,128)S(1)} %get-tuple-element.78), channel_id=1, source_target_pairs={{0,1},{1,0},{2,3},{3,2},{4,5},{5,4},{6,7},{7,6},{8,9},{9,8},{10,11... | collective-permute-start | bytes 98312 | tf_op jit(solution)/shard_map/ppermute | solution.py:442
  28.7 2.8 %collective-permute-done.6.yodd = f32[16,4,128]{2,1,0:T(4,128)S(1)} collective-permute-done((f32[16,4,128]{2,1,0:T(4,128)S(1)}, f32[16,4,128]{2,1,0:T(4,128)S(1)}, u32[]{:S(2)}, u32[]{:S(2)}) %collective-permute-start.6) | collective-permute-done | bytes 32800 | tf_op jit(solution)/shard_map/ppermute | solution.py:442
  32.2 3.1 %collective-permute-start.8 = (bf16[16,64,128]{2,1,0:T(8,128)(2,1)S(1)}, bf16[16,64,128]{2,1,0:T(8,128)(2,1)S(1)}, u32[]{:S(2)}, u32[]{:S(2)}) collective-permute-start(bf16[16,64,128]{2,1,0:T(8,128)(2,1)S(1)} %get-tuple-element.88), channel_id=1, source_target_pairs={{0,248},{8,16},{16,8},{24,32},{32,24},{40,48},{48,40},{56,64},{64,... | collective-permute-start | bytes 786440 | tf_op jit(solution)/shard_map/ppermute | solution.py:442
  36.1 1.1 %shard_map.75 = (f32[16,4,80,128]{3,2,1,0:T(8,128)S(1)}, f32[16,4,80,128]{3,2,1,0:T(8,128)S(1)}, f32[16,4,128]{2,1,0:T(4,128)S(1)}, f32[16,4,128]{2,1,0:T(4,128)S(1)}) custom-call(f32[24,128]{1,0:T(8,128)S(1)} %get-tuple-element.60.table, f32[16,4,80,128]{3,2,1,0:T(8,128)S(1)} %get-tuple-element.83.own_in, ...), custom_call_target="tpu_custom_call", output_to_operand_aliasing={{0}: (1, {}), {1}: (2, {})} | custom-call | flops 10000000 | bytes 2097152 | tf_op jit(solution)/shard_map/pallas_call | solution.py:368
  37.3 1.4 %collective-permute-start.9 = (f32[16,4,128]{2,1,0:T(4,128)S(1)}, f32[16,4,128]{2,1,0:T(4,128)S(1)}, u32[]{:S(2)}, u32[]{:S(2)}) collective-permute-start(f32[16,4,128]{2,1,0:T(4,128)S(1)} %get-tuple-element.89), channel_id=1, source_target_pairs={{0,1},{1,0},{2,3},{3,2},{4,5},{5,4},{6,7},{7,6},{8,9},{9,8},{10,11... | collective-permute-start | bytes 98312 | tf_op jit(solution)/shard_map/ppermute | solution.py:442
  38.7 1.0 %collective-permute-start.10 = (f32[16,4,128]{2,1,0:T(4,128)S(1)}, f32[16,4,128]{2,1,0:T(4,128)S(1)}, u32[]{:S(2)}, u32[]{:S(2)}) collective-permute-start(f32[16,4,128]{2,1,0:T(4,128)S(1)} %get-tuple-element.90), channel_id=1, source_target_pairs={{0,7},{1,2},{2,1},{3,4},{4,3},{5,6},{6,5},{7,0},{8,15},{9,10},{10,... | collective-permute-start | bytes 98312 | tf_op jit(solution)/shard_map/ppermute | solution.py:442
  39.7 2.6 %collective-permute-done.10.yodd = f32[16,4,128]{2,1,0:T(4,128)S(1)} collective-permute-done((f32[16,4,128]{2,1,0:T(4,128)S(1)}, f32[16,4,128]{2,1,0:T(4,128)S(1)}, u32[]{:S(2)}, u32[]{:S(2)}) %collective-permute-start.10) | collective-permute-done | bytes 32800 | tf_op jit(solution)/shard_map/ppermute | solution.py:442
  43.1 0.9 %shard_map.77 = (f32[16,4,80,128]{3,2,1,0:T(8,128)S(1)}, f32[16,4,80,128]{3,2,1,0:T(8,128)S(1)}, bf16[16,64,128]{2,1,0:T(8,128)(2,1)S(1)}, f32[16,4,128]{2,1,0:T(4,128)S(1)}, f32[16,4,128]{2,1,0:T(4,128)S(1)}) custom-call(f32[24,128]{1,0:T(8,128)S(1)} %get-tuple-element.60.table, ...), custom_call_target="tpu_custom_call", output_to_operand_aliasing={{0}: (1, {}), {1}: (2, {})} | custom-call | flops 10000000 | bytes 2097152 | tf_op jit(solution)/shard_map/pallas_call | solution.py:368
  44.0 1.8 %collective-permute-start.14 = (bf16[16,64,128]{2,1,0:T(8,128)(2,1)S(1)}, bf16[16,64,128]{2,1,0:T(8,128)(2,1)S(1)}, u32[]{:S(2)}, u32[]{:S(2)}) collective-permute-start(bf16[16,64,128]{2,1,0:T(8,128)(2,1)S(1)} %get-tuple-element.103), channel_id=1, source_target_pairs={{0,8},{8,0},{16,24},{24,16},{32,40},{40,32},{48,56},{56,48},{64,72... | collective-permute-start | bytes 786440 | tf_op jit(solution)/shard_map/ppermute | solution.py:442
  45.8 3.0 %collective-permute-start.15 = (bf16[16,64,128]{2,1,0:T(8,128)(2,1)S(1)}, bf16[16,64,128]{2,1,0:T(8,128)(2,1)S(1)}, u32[]{:S(2)}, u32[]{:S(2)}) collective-permute-start(bf16[16,64,128]{2,1,0:T(8,128)(2,1)S(1)} %get-tuple-element.107), channel_id=1, source_target_pairs={{0,248},{8,16},{16,8},{24,32},{32,24},{40,48},{48,40},{56,64},{64,... | collective-permute-start | bytes 786440 | tf_op jit(solution)/shard_map/ppermute | solution.py:442
  48.9 1.9 %collective-permute-start.12 = (f32[16,4,128]{2,1,0:T(4,128)S(1)}, f32[16,4,128]{2,1,0:T(4,128)S(1)}, u32[]{:S(2)}, u32[]{:S(2)}) collective-permute-start(f32[16,4,128]{2,1,0:T(4,128)S(1)} %get-tuple-element.99), channel_id=1, source_target_pairs={{0,1},{1,0},{2,3},{3,2},{4,5},{5,4},{6,7},{7,6},{8,9},{9,8},{10,11... | collective-permute-start | bytes 98312 | tf_op jit(solution)/shard_map/ppermute | solution.py:442
  51.4 0.9 %shard_map.78 = (f32[16,4,80,128]{3,2,1,0:T(8,128)S(1)}, f32[16,4,80,128]{3,2,1,0:T(8,128)S(1)}) custom-call(f32[24,128]{1,0:T(8,128)S(1)} %get-tuple-element.60.table, f32[16,4,80,128]{3,2,1,0:T(8,128)S(1)} %get-tuple-element.94.own_in, f32[16,4,80,128]{3,2,1,0:T(8,128)S(1)} %get-tuple-element.95.other_in, ...), custom_call_target="tpu_custom_call", output_to_operand_aliasing={{0}: (1, {}), {1}: (2, {})} | custom-call | flops 10000000 | bytes 2097152 | tf_op jit(solution)/shard_map/pallas_call | solution.py:368
  52.3 2.0 %collective-permute-done.13.yodd = f32[16,4,128]{2,1,0:T(4,128)S(1)} collective-permute-done((f32[16,4,128]{2,1,0:T(4,128)S(1)}, f32[16,4,128]{2,1,0:T(4,128)S(1)}, u32[]{:S(2)}, u32[]{:S(2)}) %collective-permute-start.13) | collective-permute-done | bytes 32800 | tf_op jit(solution)/shard_map/ppermute | solution.py:442
  54.4 1.2 %shard_map.79 = (f32[16,4,80,128]{3,2,1,0:T(8,128)S(1)}, f32[16,4,80,128]{3,2,1,0:T(8,128)S(1)}, f32[16,8,128]{2,1,0:T(8,128)S(1)}) custom-call(f32[24,128]{1,0:T(8,128)S(1)} %get-tuple-element.60.table, f32[16,4,80,128]{3,2,1,0:T(8,128)S(1)} %get-tuple-element.96.own_in, ...), custom_call_target="tpu_custom_call", output_to_operand_aliasing={{0}: (1, {}), {1}: (2, {})} | custom-call | flops 10000000 | bytes 2097152 | tf_op jit(solution)/shard_map/pallas_call | solution.py:368
  56.3 0.9 %shard_map.81 = (f32[16,4,80,128]{3,2,1,0:T(8,128)S(1)}, f32[16,4,80,128]{3,2,1,0:T(8,128)S(1)}, f32[256,1,16]{2,1,0:T(1,128)S(1)}) custom-call(f32[24,128]{1,0:T(8,128)S(1)} %get-tuple-element.60.table, f32[16,4,80,128]{3,2,1,0:T(8,128)S(1)} %get-tuple-element.105.own_in, ...), custom_call_target="tpu_custom_call", output_to_operand_aliasing={{0}: (1, {}), {1}: (2, {})} | custom-call | flops 10000000 | bytes 2097152 | tf_op jit(solution)/shard_map/pallas_call | solution.py:368
  57.2 22.0 %all_to_all.5.sums_ref = f32[256,1,16]{2,1,0:T(1,128)S(1)} all-to-all(f32[256,1,16]{2,1,0:T(1,128)S(1)} %get-tuple-element.109), channel_id=1, replica_groups=mesh['gx'=32,'gy'=8] {'gx','gy'}, dimensions={0} | all-to-all | bytes 32768 | tf_op jit(solution)/shard_map/all_to_all | solution.py:482
  79.2 3.0 %shard_map.82 = (bf16[16,4,64,256]{3,2,1,0:T(8,128)(2,1)}, f32[1,16]{1,0:T(1,128)}) custom-call(f32[24,128]{1,0:T(8,128)S(1)} %get-tuple-element.60.table, f32[256,1,16]{2,1,0:T(1,128)S(1)} %all_to_all.5.sums_ref, f32[16,4,80,128]{3,2,1,0:T(8,128)S(1)} %get-tuple-element.110.a0, f32[16,4,80,128]{3,2,1,0:T(8,128)S(1)} %get-tuple-element.111.a1), custom_call_target="tpu_custom_call" | custom-call | flops 10000000 | bytes 2097152 | tf_op jit(solution)/shard_map/pallas_call | solution.py:427
  (28 shorter events, 7.9 us)
Async XLA Ops:
  3.0 18.1 %collective-permute-start = (bf16[16,64,128]{2,1,0:T(8,128)(2,1)S(1)}, bf16[16,64,128]{2,1,0:T(8,128)(2,1)S(1)}, u32[]{:S(2)}, u32[]{:S(2)}) collective-permute-start(bf16[16,64,128]{2,1,0:T(8,128)(2,1)S(1)} %get-tuple-element.65), channel_id=1, source_target_pairs={{0,248},{8,16},{16,8},{24,32},{32,24},{40,48},{48,40},{56,64},{64,... | collective-permute-start | bytes 786440 | tf_op jit(solution)/shard_map/ppermute | solution.py:442
  11.9 11.3 %collective-permute-start.3 = (bf16[16,64,128]{2,1,0:T(8,128)(2,1)S(1)}, bf16[16,64,128]{2,1,0:T(8,128)(2,1)S(1)}, u32[]{:S(2)}, u32[]{:S(2)}) collective-permute-start(bf16[16,64,128]{2,1,0:T(8,128)(2,1)S(1)} %get-tuple-element.70), channel_id=1, source_target_pairs={{0,8},{8,0},{16,24},{24,16},{32,40},{40,32},{48,56},{56,48},{64,72... | collective-permute-start | bytes 786440 | tf_op jit(solution)/shard_map/ppermute | solution.py:442
  11.9 9.2 %collective-permute-start.1 = (f32[16,4,128]{2,1,0:T(4,128)S(1)}, f32[16,4,128]{2,1,0:T(4,128)S(1)}, u32[]{:S(2)}, u32[]{:S(2)}) collective-permute-start(f32[16,4,128]{2,1,0:T(4,128)S(1)} %get-tuple-element.66), channel_id=1, source_target_pairs={{0,1},{1,0},{2,3},{3,2},{4,5},{5,4},{6,7},{7,6},{8,9},{9,8},{10,11... | collective-permute-start | bytes 98312 | tf_op jit(solution)/shard_map/ppermute | solution.py:442
  12.9 8.2 %collective-permute-start.2 = (f32[16,4,128]{2,1,0:T(4,128)S(1)}, f32[16,4,128]{2,1,0:T(4,128)S(1)}, u32[]{:S(2)}, u32[]{:S(2)}) collective-permute-start(f32[16,4,128]{2,1,0:T(4,128)S(1)} %get-tuple-element.67), channel_id=1, source_target_pairs={{0,7},{1,2},{2,1},{3,4},{4,3},{5,6},{6,5},{7,0},{8,15},{9,10},{10,... | collective-permute-start | bytes 98312 | tf_op jit(solution)/shard_map/ppermute | solution.py:442
  14.0 0.7 copy-start
  14.7 0.7 copy-start.1
  21.9 9.6 %collective-permute-start.4 = (bf16[16,64,128]{2,1,0:T(8,128)(2,1)S(1)}, bf16[16,64,128]{2,1,0:T(8,128)(2,1)S(1)}, u32[]{:S(2)}, u32[]{:S(2)}) collective-permute-start(bf16[16,64,128]{2,1,0:T(8,128)(2,1)S(1)} %get-tuple-element.77), channel_id=1, source_target_pairs={{0,248},{8,16},{16,8},{24,32},{32,24},{40,48},{48,40},{56,64},{64,... | collective-permute-start | bytes 786440 | tf_op jit(solution)/shard_map/ppermute | solution.py:442
  24.0 11.4 %collective-permute-start.7 = (bf16[16,64,128]{2,1,0:T(8,128)(2,1)S(1)}, bf16[16,64,128]{2,1,0:T(8,128)(2,1)S(1)}, u32[]{:S(2)}, u32[]{:S(2)}) collective-permute-start(bf16[16,64,128]{2,1,0:T(8,128)(2,1)S(1)} %get-tuple-element.82), channel_id=1, source_target_pairs={{0,8},{8,0},{16,24},{24,16},{32,40},{40,32},{48,56},{56,48},{64,72... | collective-permute-start | bytes 786440 | tf_op jit(solution)/shard_map/ppermute | solution.py:442
  25.7 3.0 %collective-permute-start.5 = (f32[16,4,128]{2,1,0:T(4,128)S(1)}, f32[16,4,128]{2,1,0:T(4,128)S(1)}, u32[]{:S(2)}, u32[]{:S(2)}) collective-permute-start(f32[16,4,128]{2,1,0:T(4,128)S(1)} %get-tuple-element.78), channel_id=1, source_target_pairs={{0,1},{1,0},{2,3},{3,2},{4,5},{5,4},{6,7},{7,6},{8,9},{9,8},{10,11... | collective-permute-start | bytes 98312 | tf_op jit(solution)/shard_map/ppermute | solution.py:442
  27.8 3.6 %collective-permute-start.6 = (f32[16,4,128]{2,1,0:T(4,128)S(1)}, f32[16,4,128]{2,1,0:T(4,128)S(1)}, u32[]{:S(2)}, u32[]{:S(2)}) collective-permute-start(f32[16,4,128]{2,1,0:T(4,128)S(1)} %get-tuple-element.79), channel_id=1, source_target_pairs={{0,7},{1,2},{2,1},{3,4},{4,3},{5,6},{6,5},{7,0},{8,15},{9,10},{10,... | collective-permute-start | bytes 98312 | tf_op jit(solution)/shard_map/ppermute | solution.py:442
  32.2 10.1 %collective-permute-start.8 = (bf16[16,64,128]{2,1,0:T(8,128)(2,1)S(1)}, bf16[16,64,128]{2,1,0:T(8,128)(2,1)S(1)}, u32[]{:S(2)}, u32[]{:S(2)}) collective-permute-start(bf16[16,64,128]{2,1,0:T(8,128)(2,1)S(1)} %get-tuple-element.88), channel_id=1, source_target_pairs={{0,248},{8,16},{16,8},{24,32},{32,24},{40,48},{48,40},{56,64},{64,... | collective-permute-start | bytes 786440 | tf_op jit(solution)/shard_map/ppermute | solution.py:442
  36.0 7.0 %collective-permute-start.11 = (bf16[16,64,128]{2,1,0:T(8,128)(2,1)S(1)}, bf16[16,64,128]{2,1,0:T(8,128)(2,1)S(1)}, u32[]{:S(2)}, u32[]{:S(2)}) collective-permute-start(bf16[16,64,128]{2,1,0:T(8,128)(2,1)S(1)} %get-tuple-element.93), channel_id=1, source_target_pairs={{0,8},{8,0},{16,24},{24,16},{32,40},{40,32},{48,56},{56,48},{64,72... | collective-permute-start | bytes 786440 | tf_op jit(solution)/shard_map/ppermute | solution.py:442
  37.3 2.4 %collective-permute-start.9 = (f32[16,4,128]{2,1,0:T(4,128)S(1)}, f32[16,4,128]{2,1,0:T(4,128)S(1)}, u32[]{:S(2)}, u32[]{:S(2)}) collective-permute-start(f32[16,4,128]{2,1,0:T(4,128)S(1)} %get-tuple-element.89), channel_id=1, source_target_pairs={{0,1},{1,0},{2,3},{3,2},{4,5},{5,4},{6,7},{7,6},{8,9},{9,8},{10,11... | collective-permute-start | bytes 98312 | tf_op jit(solution)/shard_map/ppermute | solution.py:442
  38.7 3.6 %collective-permute-start.10 = (f32[16,4,128]{2,1,0:T(4,128)S(1)}, f32[16,4,128]{2,1,0:T(4,128)S(1)}, u32[]{:S(2)}, u32[]{:S(2)}) collective-permute-start(f32[16,4,128]{2,1,0:T(4,128)S(1)} %get-tuple-element.90), channel_id=1, source_target_pairs={{0,7},{1,2},{2,1},{3,4},{4,3},{5,6},{6,5},{7,0},{8,15},{9,10},{10,... | collective-permute-start | bytes 98312 | tf_op jit(solution)/shard_map/ppermute | solution.py:442
  44.0 11.6 %collective-permute-start.14 = (bf16[16,64,128]{2,1,0:T(8,128)(2,1)S(1)}, bf16[16,64,128]{2,1,0:T(8,128)(2,1)S(1)}, u32[]{:S(2)}, u32[]{:S(2)}) collective-permute-start(bf16[16,64,128]{2,1,0:T(8,128)(2,1)S(1)} %get-tuple-element.103), channel_id=1, source_target_pairs={{0,8},{8,0},{16,24},{24,16},{32,40},{40,32},{48,56},{56,48},{64,72... | collective-permute-start | bytes 786440 | tf_op jit(solution)/shard_map/ppermute | solution.py:442
  45.8 10.5 %collective-permute-start.15 = (bf16[16,64,128]{2,1,0:T(8,128)(2,1)S(1)}, bf16[16,64,128]{2,1,0:T(8,128)(2,1)S(1)}, u32[]{:S(2)}, u32[]{:S(2)}) collective-permute-start(bf16[16,64,128]{2,1,0:T(8,128)(2,1)S(1)} %get-tuple-element.107), channel_id=1, source_target_pairs={{0,248},{8,16},{16,8},{24,32},{32,24},{40,48},{48,40},{56,64},{64,... | collective-permute-start | bytes 786440 | tf_op jit(solution)/shard_map/ppermute | solution.py:442
  48.9 3.4 %collective-permute-start.12 = (f32[16,4,128]{2,1,0:T(4,128)S(1)}, f32[16,4,128]{2,1,0:T(4,128)S(1)}, u32[]{:S(2)}, u32[]{:S(2)}) collective-permute-start(f32[16,4,128]{2,1,0:T(4,128)S(1)} %get-tuple-element.99), channel_id=1, source_target_pairs={{0,1},{1,0},{2,3},{3,2},{4,5},{5,4},{6,7},{7,6},{8,9},{9,8},{10,11... | collective-permute-start | bytes 98312 | tf_op jit(solution)/shard_map/ppermute | solution.py:442
  50.7 3.6 %collective-permute-start.13 = (f32[16,4,128]{2,1,0:T(4,128)S(1)}, f32[16,4,128]{2,1,0:T(4,128)S(1)}, u32[]{:S(2)}, u32[]{:S(2)}) collective-permute-start(f32[16,4,128]{2,1,0:T(4,128)S(1)} %get-tuple-element.100), channel_id=1, source_target_pairs={{0,7},{1,2},{2,1},{3,4},{4,3},{5,6},{6,5},{7,0},{8,15},{9,10},{10,... | collective-permute-start | bytes 98312 | tf_op jit(solution)/shard_map/ppermute | solution.py:442

commit v4 on v3

--- a/solution.py
+++ b/solution.py
@@ -34,11 +34,11 @@
     return pltpu.with_memory_space_constraint(x, pltpu.HBM)
 
 
-def split_matrix():
+def split_matrix(gain=1.0):
     row = lax.broadcasted_iota(jnp.int32, (NZ, NZ), 0)
     col = lax.broadcasted_iota(jnp.int32, (NZ, NZ), 1)
     wanted = jnp.where(col < HALF, 2 * col, 2 * (col - HALF) + 1)
-    return (row == wanted).astype(F32).astype(BF16)
+    return jnp.where(row == wanted, gain, 0.0).astype(BF16)
 
 
 def join_matrix():
@@ -190,7 +190,7 @@
     @pl.loop(0, R, step=4)
     def _(first):
         cells = buf[pl.ds(first, 4)].reshape(4 * CX * CY, NZ)
-        parts = jnp.dot(cells, matrix, preferred_element_type=F32) * 5.0
+        parts = jnp.dot(cells, matrix, preferred_element_type=F32)
         for k in range(4 * CX):
             rows = parts[k * CY : (k + 1) * CY]
             r, at = first + k // CX, k % CX
@@ -242,6 +242,7 @@
         for place, (k, m) in enumerate(((2, 5), (5, 2))):
             bonds0[4 + place, x], bonds1[4 + place, x] = by_colour(halves[k][0], halves[m][1], at, plain_row)
     copies[2].wait()
+    matrix = split_matrix(5.0)
     split_field(side, buf.at[0], u00, u01, matrix, plain_row)
     copies[3].wait()
     split_field(side, buf.at[1], u10, u11, matrix, plain_row)
@@ -268,9 +269,9 @@
     lower = table[UPPER : UPPER + 1, :] == 0.0
     for r in range(R):
         for x in range(CX):
-            even, odd = yeven[r, x : x + 1, :], yodd[r, x : x + 1, :]
-            other[r, x, PAD - 1 : PAD, :] = jnp.where(lower, odd, even)
-            other[r, x, PAD + CY : PAD + CY + 1, :] = jnp.where(lower, even, odd)
+            from_even, from_odd = yeven[r, x : x + 1, :], yodd[r, x : x + 1, :]
+            other[r, x, PAD - 1 : PAD, :] = jnp.where(lower, from_odd, from_even)
+            other[r, x, PAD + CY : PAD + CY + 1, :] = jnp.where(lower, from_even, from_odd)
 
 
 def update(colour, regions, table, own, other, u_ref, bonds_ref, beyond, sent, energy):
@@ -331,31 +332,31 @@
     update(colour, rows_of(FIRST), table, own, other, u, bonds, halo, sent, None)
 
 
-def sweep_last(colour, edges, table, own_in, other_in, u, bonds, halo, own, other, sent, *rest):
-    update(colour, rows_of(LAST) + (EDGES if edges else []), table, own, other, u, bonds, halo, sent, None)
-    if edges:
-        send_rows(table, own, *rest)
-
-
-def sweep_inner(colour, edges, table, own_in, other_in, u, bonds, own, other, *rest):
-    regions = rows_of(INNER, 8, CY - 8) if edges else rows_of(INNER)
-    update(colour, regions, table, own, other, u, bonds, None, None, None)
-    if not edges:
-        send_rows(table, own, *rest)
-
-
-def final_inner(table, own_in, other_in, u, bonds, yeven, yodd, own, other, energy):
+def sweep_last(colour, table, own_in, other_in, u, bonds, halo, own, other, sent):
+    update(colour, rows_of(LAST), table, own, other, u, bonds, halo, sent, None)
+
+
+def sweep_edges(colour, table, own_in, other_in, u, bonds, own, other, yeven, yodd):
+    update(colour, EDGES, table, own, other, u, bonds, None, None, None)
+    send_rows(table, own, yeven, yodd)
+
+
+def sweep_inner(colour, table, own_in, other_in, u, bonds, own, other):
+    update(colour, rows_of(INNER, 8, CY - 8), table, own, other, u, bonds, None, None, None)
+
+
+def final_inner(table, own_in, other_in, u, bonds, own, other, energy):
+    update(1, rows_of(INNER, 8, CY - 8), table, own, other, u, bonds, None, None, energy)
+
+
+def final_first(table, own_in, other_in, u, bonds, halo, yeven, yodd, so_far, own, other, energy):
     put_rows(table, other, yeven, yodd)
-    update(1, rows_of(INNER), table, own, other, u, bonds, None, None, energy)
-
-
-def final_last(table, own_in, other_in, u, bonds, halo, so_far, own, other, energy):
-    update(1, rows_of(LAST), table, own, other, u, bonds, halo, None, energy)
+    update(1, rows_of(FIRST), table, own, other, u, bonds, halo, None, energy)
     energy[...] = energy[...] + so_far[...]
 
 
-def final_first(table, own_in, other_in, u, bonds, halo, so_far, own, other, sums_ref, energy):
-    update(1, rows_of(FIRST), table, own, other, u, bonds, halo, None, energy)
+def final_last(table, own_in, other_in, u, bonds, halo, so_far, own, other, sums_ref, energy):
+    update(1, rows_of(LAST) + EDGES, table, own, other, u, bonds, halo, None, energy)
     lines = jnp.sum(energy[...] + so_far[...], axis=1)
     totals = jnp.sum(lines, axis=1, keepdims=True)
     diagonal = lax.broadcasted_iota(jnp.int32, (R, R), 0) == lax.broadcasted_iota(jnp.int32, (R, R), 1)
@@ -442,15 +443,19 @@
     return lax.ppermute(x, axis, [(i, (((i + odd) ^ 1) - odd) % count) for i in range(count)])
 
 
-def exchange(axis, even, odd):
-    near = swap_pairs(even, axis, 0)
-    far = swap_pairs(odd, axis, 1)
-    return [near, far]
+def exchange_layers(first, last):
+    first = swap_pairs(first, "gx", 1)
+    last = swap_pairs(last, "gx", 0)
+    return first, last
+
+
+def exchange_rows(even, odd):
+    return swap_pairs(even, "gy", 0), swap_pairs(odd, "gy", 1)
 
 
 def body(spins, couplings, betas, metro_uniform, swap_uniform):
     a0, a1, xe, xo, ye, yo = run_split_outer(spins)
-    xs, ys = exchange("gx", xe, xo), exchange("gy", ye, yo)
+    xs, ys = exchange_layers(xo, xe), exchange_rows(ye, yo)
     a0, a1, u00, u01, u10, u11, bonds0, bonds1, table = run_split_inner(
         betas, swap_uniform, spins, couplings, metro_uniform, a0, a1
     )
@@ -458,26 +463,24 @@
     for step, (u, bonds) in enumerate(((u00, bonds0), (u01, bonds1), (u10, bonds0))):
         colour = step % 2
         own, other = states[colour], states[1 - colour]
-        edges = step == 2
         run = sweep_call(functools.partial(sweep_first, colour), 3, [LAYER])
-        own, other, xo = run(table, own, other, u, bonds, xs[1], *ys)
-        run = sweep_call(functools.partial(sweep_last, colour, edges), 1, [LAYER] + ([ROWS] * 2 if edges else []))
-        own, other, xe, *rows = run(table, own, other, u, bonds, xs[0])
-        xs = exchange("gx", xe, xo)
-        if edges:
-            ys = exchange("gy", *rows)
-        run = sweep_call(functools.partial(sweep_inner, colour, edges), 0, [] if edges else [ROWS] * 2)
+        own, other, xo = run(table, own, other, u, bonds, xs[0], *ys)
+        run = sweep_call(functools.partial(sweep_last, colour), 1, [LAYER])
+        own, other, xe = run(table, own, other, u, bonds, xs[1])
+        xs = exchange_layers(xo, xe)
+        run = sweep_call(functools.partial(sweep_edges, colour), 0, [ROWS] * 2)
         own, other, *rows = run(table, own, other, u, bonds)
-        if not edges:
-            ys = exchange("gy", *rows)
+        ys = exchange_rows(*rows)
+        run = sweep_call(functools.partial(sweep_inner, colour), 0, [])
+        own, other = run(table, own, other, u, bonds)
         states[colour], states[1 - colour] = own, other
     both = ("gx", "gy")
     count = lax.axis_size(both)
     a0, a1 = states
-    a1, a0, energy = sweep_call(final_inner, 2, [ENERGY])(table, a1, a0, u11, bonds1, *ys)
-    a1, a0, energy = sweep_call(final_last, 2, [ENERGY])(table, a1, a0, u11, bonds1, xs[0], energy)
+    a1, a0, energy = sweep_call(final_inner, 0, [ENERGY])(table, a1, a0, u11, bonds1)
+    a1, a0, energy = sweep_call(final_first, 4, [ENERGY])(table, a1, a0, u11, bonds1, xs[0], *ys, energy)
     a1, a0, sums = sweep_call(
-        final_first, 2, [pltpu.VMEM((count, 1, R), F32)], [pltpu.VMEM((R, 8, HALF), F32)]
+        final_last, 2, [pltpu.VMEM((count, 1, R), F32)], [pltpu.VMEM((R, 8, HALF), F32)]
     )(table, a1, a0, u11, bonds1, xs[1], energy)
     sums = lax.all_to_all(sums, both, 0, 0, tiled=True)
     cell_count = float(CX * CY * NZ * count)

time: 82.5 us -> 81.2 us (0.984)
  waiting for transfers between devices: 7.82 us -> 5.3 us
  Pallas kernels: 21.7 us -> 22.6 us
    ppermute x16, waiting for transfers between devices: 7.82 us -> 5.3 us  [swap_pairs(): lax.ppermute(x, axis, [(i, ((i + odd ^ 1) - odd) % count) for i in range(...]
    pallas_call x12 -> x15, Pallas kernels: 10.6 us -> 11.4 us  [run(): call(kernel, [STATE] * 2 + more_outs, [VM] * (5 + more_ins), [VM] * (2 +...]
    all_to_all x1, blocking collectives: 22 us -> 22.8 us  [body(): sums = lax.all_to_all(sums, both, 0, 0, tiled=True)]
  transfers between devices with their start and end apart: 16 -> 16, of which waited for: 4 -> 4; matrix products, arithmetic and copies ran while one was open for 0% -> 0% of each run, Pallas kernels for 18% -> 20%
where the time goes in v4:
time: 81.2 us; the launch traced here: 81.1 us
  starting transfers between devices  28 us (34%)
  blocking collectives  22.8 us (28%)
  Pallas kernels  22.6 us (28%)
  waiting for transfers between devices  5.3 us (7%)
  local copies, waits for them, and re-layouts  1.31 us (2%)
  between operations  1 us (1%)
    ppermute x16, starting transfers between devices, swap_pairs(): lax.ppermute(x, axis, [(i, ((i + odd ^ 1) - odd) % count) for i in range(...  28 us
    all_to_all x1, blocking collectives, body(): sums = lax.all_to_all(sums, both, 0, 0, tiled=True)  22.8 us
    pallas_call x15, Pallas kernels, run(): call(kernel, [STATE] * 2 + more_outs, [VM] * (5 + more_ins), [VM] * (2 +...  11.4 us
    pallas_call x1, Pallas kernels, run_split_inner(): call(split_inner, [STATE] * 2 + [DRAWS] * 4 + [BONDS] * 2 + [TABLE], [SM]...  5.82 us
    ppermute x16, waiting for transfers between devices, swap_pairs(): lax.ppermute(x, axis, [(i, ((i + odd ^ 1) - odd) % count) for i in range(...  5.3 us
    pallas_call x1, Pallas kernels, run_mix_and_join(): call(functools.partial(mix_and_join, cell_count), [jax.ShapeDtypeStruct((...  2.95 us
    pallas_call x1, Pallas kernels, run_split_outer(): call(split_outer, [STATE] * 2 + [LAYER] * 2 + [ROWS] * 2, [HB], [VM] * 6,...  2.38 us
  transfers between devices with their start and end apart: 16, of which 4 were waited for; matrix products, arithmetic and copies ran while one was open for 0% of the time, Pallas kernels for 20%

profile of v4, /device:TPU:1, one launch (start us, length us, event | category | flops | bytes accessed | tf_op | source)
XLA Modules:
  0.0 81.1 jit_solution(6068844467289545831)
XLA Ops:
  0.6 2.4 %shard_map.68 = (f32[16,4,80,128]{3,2,1,0:T(8,128)S(1)}, f32[16,4,80,128]{3,2,1,0:T(8,128)S(1)}, bf16[16,64,128]{2,1,0:T(8,128)(2,1)S(1)}, bf16[16,64,128]{2,1,0...) custom-call(bf16[16,4,64,256]{3,2,1,0:T(8,128)(2,1)} %spins_ref.3), custom_call_target="tpu_custom_call" | custom-call | flops 10000000 | bytes 2097152 | tf_op jit(solution)/shard_map/pallas_call | solution.py:175
  3.0 8.9 %collective-permute-start = (bf16[16,64,128]{2,1,0:T(8,128)(2,1)S(1)}, bf16[16,64,128]{2,1,0:T(8,128)(2,1)S(1)}, u32[]{:S(2)}, u32[]{:S(2)}) collective-permute-start(bf16[16,64,128]{2,1,0:T(8,128)(2,1)S(1)} %get-tuple-element.71), channel_id=1, source_target_pairs={{0,248},{8,16},{16,8},{24,32},{32,24},{40,48},{48,40},{56,64},{64,... | collective-permute-start | bytes 786440 | tf_op jit(solution)/shard_map/ppermute | solution.py:443
  11.9 1.0 %collective-permute-start.1 = (f32[16,4,128]{2,1,0:T(4,128)S(1)}, f32[16,4,128]{2,1,0:T(4,128)S(1)}, u32[]{:S(2)}, u32[]{:S(2)}) collective-permute-start(f32[16,4,128]{2,1,0:T(4,128)S(1)} %get-tuple-element.72), channel_id=1, source_target_pairs={{0,1},{1,0},{2,3},{3,2},{4,5},{5,4},{6,7},{7,6},{8,9},{9,8},{10,11... | collective-permute-start | bytes 98312 | tf_op jit(solution)/shard_map/ppermute | solution.py:443
  12.9 1.1 %collective-permute-start.2 = (f32[16,4,128]{2,1,0:T(4,128)S(1)}, f32[16,4,128]{2,1,0:T(4,128)S(1)}, u32[]{:S(2)}, u32[]{:S(2)}) collective-permute-start(f32[16,4,128]{2,1,0:T(4,128)S(1)} %get-tuple-element.73), channel_id=1, source_target_pairs={{0,7},{1,2},{2,1},{3,4},{4,3},{5,6},{6,5},{7,0},{8,15},{9,10},{10,... | collective-permute-start | bytes 98312 | tf_op jit(solution)/shard_map/ppermute | solution.py:443
  15.3 5.8 %shard_map.69 = (f32[16,4,80,128]{3,2,1,0:T(8,128)S(1)}, f32[16,4,80,128]{3,2,1,0:T(8,128)S(1)}, f32[16,4,64,128]{3,2,1,0:T(8,128)S(1)}, f32[16,4,64,128]{3,2,1,...) custom-call(f32[16]{0:T(128)S(1)} %copy-done, ...), custom_call_target="tpu_custom_call", output_to_operand_aliasing={{0}: (5, {}), {1}: (6, {})} | custom-call | flops 10000000 | bytes 2097152 | tf_op jit(solution)/shard_map/pallas_call | solution.py:252
  21.9 1.4 %collective-permute-start.4 = (bf16[16,64,128]{2,1,0:T(8,128)(2,1)S(1)}, bf16[16,64,128]{2,1,0:T(8,128)(2,1)S(1)}, u32[]{:S(2)}, u32[]{:S(2)}) collective-permute-start(bf16[16,64,128]{2,1,0:T(8,128)(2,1)S(1)} %get-tuple-element.85), channel_id=1, source_target_pairs={{0,248},{8,16},{16,8},{24,32},{32,24},{40,48},{48,40},{56,64},{64,... | collective-permute-start | bytes 786440 | tf_op jit(solution)/shard_map/ppermute | solution.py:443
  25.1 2.2 %collective-permute-start.5 = (f32[16,4,128]{2,1,0:T(4,128)S(1)}, f32[16,4,128]{2,1,0:T(4,128)S(1)}, u32[]{:S(2)}, u32[]{:S(2)}) collective-permute-start(f32[16,4,128]{2,1,0:T(4,128)S(1)} %get-tuple-element.86), channel_id=1, source_target_pairs={{0,1},{1,0},{2,3},{3,2},{4,5},{5,4},{6,7},{7,6},{8,9},{9,8},{10,11... | collective-permute-start | bytes 98312 | tf_op jit(solution)/shard_map/ppermute | solution.py:443
  27.8 0.9 %shard_map.73 = (f32[16,4,80,128]{3,2,1,0:T(8,128)S(1)}, f32[16,4,80,128]{3,2,1,0:T(8,128)S(1)}) custom-call(f32[24,128]{1,0:T(8,128)S(1)} %get-tuple-element.66.table, f32[16,4,80,128]{3,2,1,0:T(8,128)S(1)} %get-tuple-element.79.own_in, f32[16,4,80,128]{3,2,1,0:T(8,128)S(1)} %get-tuple-element.80.other_in, ...), custom_call_target="tpu_custom_call", output_to_operand_aliasing={{0}: (1, {}), {1}: (2, {})} | custom-call | flops 10000000 | bytes 2097152 | tf_op jit(solution)/shard_map/pallas_call | solution.py:369
  28.7 2.3 %collective-permute-done.6.yodd = f32[16,4,128]{2,1,0:T(4,128)S(1)} collective-permute-done((f32[16,4,128]{2,1,0:T(4,128)S(1)}, f32[16,4,128]{2,1,0:T(4,128)S(1)}, u32[]{:S(2)}, u32[]{:S(2)}) %collective-permute-start.6) | collective-permute-done | bytes 32800 | tf_op jit(solution)/shard_map/ppermute | solution.py:443
  32.2 2.6 %collective-permute-start.8 = (bf16[16,64,128]{2,1,0:T(8,128)(2,1)S(1)}, bf16[16,64,128]{2,1,0:T(8,128)(2,1)S(1)}, u32[]{:S(2)}, u32[]{:S(2)}) collective-permute-start(bf16[16,64,128]{2,1,0:T(8,128)(2,1)S(1)} %get-tuple-element.98), channel_id=1, source_target_pairs={{0,248},{8,16},{16,8},{24,32},{32,24},{40,48},{48,40},{56,64},{64,... | collective-permute-start | bytes 786440 | tf_op jit(solution)/shard_map/ppermute | solution.py:443
  36.2 1.7 %collective-permute-start.9 = (f32[16,4,128]{2,1,0:T(4,128)S(1)}, f32[16,4,128]{2,1,0:T(4,128)S(1)}, u32[]{:S(2)}, u32[]{:S(2)}) collective-permute-start(f32[16,4,128]{2,1,0:T(4,128)S(1)} %get-tuple-element.99), channel_id=1, source_target_pairs={{0,1},{1,0},{2,3},{3,2},{4,5},{5,4},{6,7},{7,6},{8,9},{9,8},{10,11... | collective-permute-start | bytes 98312 | tf_op jit(solution)/shard_map/ppermute | solution.py:443
  37.9 1.2 %collective-permute-start.10 = (f32[16,4,128]{2,1,0:T(4,128)S(1)}, f32[16,4,128]{2,1,0:T(4,128)S(1)}, u32[]{:S(2)}, u32[]{:S(2)}) collective-permute-start(f32[16,4,128]{2,1,0:T(4,128)S(1)} %get-tuple-element.100), channel_id=1, source_target_pairs={{0,7},{1,2},{2,1},{3,4},{4,3},{5,6},{6,5},{7,0},{8,15},{9,10},{10,... | collective-permute-start | bytes 98312 | tf_op jit(solution)/shard_map/ppermute | solution.py:443
  39.1 0.9 %shard_map.77 = (f32[16,4,80,128]{3,2,1,0:T(8,128)S(1)}, f32[16,4,80,128]{3,2,1,0:T(8,128)S(1)}) custom-call(f32[24,128]{1,0:T(8,128)S(1)} %get-tuple-element.66.table, f32[16,4,80,128]{3,2,1,0:T(8,128)S(1)} %get-tuple-element.93.own_in, f32[16,4,80,128]{3,2,1,0:T(8,128)S(1)} %get-tuple-element.94.other_in, ...), custom_call_target="tpu_custom_call", output_to_operand_aliasing={{0}: (1, {}), {1}: (2, {})} | custom-call | flops 10000000 | bytes 2097152 | tf_op jit(solution)/shard_map/pallas_call | solution.py:369
  40.0 1.5 %collective-permute-done.10.yodd = f32[16,4,128]{2,1,0:T(4,128)S(1)} collective-permute-done((f32[16,4,128]{2,1,0:T(4,128)S(1)}, f32[16,4,128]{2,1,0:T(4,128)S(1)}, u32[]{:S(2)}, u32[]{:S(2)}) %collective-permute-start.10) | collective-permute-done | bytes 32800 | tf_op jit(solution)/shard_map/ppermute | solution.py:443
  42.3 3.6 %collective-permute-start.12 = (bf16[16,64,128]{2,1,0:T(8,128)(2,1)S(1)}, bf16[16,64,128]{2,1,0:T(8,128)(2,1)S(1)}, u32[]{:S(2)}, u32[]{:S(2)}) collective-permute-start(bf16[16,64,128]{2,1,0:T(8,128)(2,1)S(1)} %get-tuple-element.113), channel_id=1, source_target_pairs={{0,248},{8,16},{16,8},{24,32},{32,24},{40,48},{48,40},{56,64},{64,... | collective-permute-start | bytes 786440 | tf_op jit(solution)/shard_map/ppermute | solution.py:443
  47.3 2.3 %collective-permute-start.13 = (f32[16,4,128]{2,1,0:T(4,128)S(1)}, f32[16,4,128]{2,1,0:T(4,128)S(1)}, u32[]{:S(2)}, u32[]{:S(2)}) collective-permute-start(f32[16,4,128]{2,1,0:T(4,128)S(1)} %get-tuple-element.114), channel_id=1, source_target_pairs={{0,1},{1,0},{2,3},{3,2},{4,5},{5,4},{6,7},{7,6},{8,9},{9,8},{10,11... | collective-permute-start | bytes 98312 | tf_op jit(solution)/shard_map/ppermute | solution.py:443
  49.6 0.9 %collective-permute-start.14 = (f32[16,4,128]{2,1,0:T(4,128)S(1)}, f32[16,4,128]{2,1,0:T(4,128)S(1)}, u32[]{:S(2)}, u32[]{:S(2)}) collective-permute-start(f32[16,4,128]{2,1,0:T(4,128)S(1)} %get-tuple-element.115), channel_id=1, source_target_pairs={{0,7},{1,2},{2,1},{3,4},{4,3},{5,6},{6,5},{7,0},{8,15},{9,10},{10,... | collective-permute-start | bytes 98312 | tf_op jit(solution)/shard_map/ppermute | solution.py:443
  50.5 0.9 %shard_map.81 = (f32[16,4,80,128]{3,2,1,0:T(8,128)S(1)}, f32[16,4,80,128]{3,2,1,0:T(8,128)S(1)}) custom-call(f32[24,128]{1,0:T(8,128)S(1)} %get-tuple-element.66.table, f32[16,4,80,128]{3,2,1,0:T(8,128)S(1)} %get-tuple-element.106.own_in, f32[16,4,80,128]{3,2,1,0:T(8,128)S(1)} %get-tuple-element.107.other_in, ...), custom_call_target="tpu_custom_call", output_to_operand_aliasing={{0}: (1, {}), {1}: (2, {})} | custom-call | flops 10000000 | bytes 2097152 | tf_op jit(solution)/shard_map/pallas_call | solution.py:369
  51.3 0.9 %shard_map.82 = (f32[16,4,80,128]{3,2,1,0:T(8,128)S(1)}, f32[16,4,80,128]{3,2,1,0:T(8,128)S(1)}, f32[16,8,128]{2,1,0:T(8,128)S(1)}) custom-call(f32[24,128]{1,0:T(8,128)S(1)} %get-tuple-element.66.table, f32[16,4,80,128]{3,2,1,0:T(8,128)S(1)} %get-tuple-element.108.own_in, ...), custom_call_target="tpu_custom_call", output_to_operand_aliasing={{0}: (1, {}), {1}: (2, {})} | custom-call | flops 10000000 | bytes 2097152 | tf_op jit(solution)/shard_map/pallas_call | solution.py:369
  52.3 0.9 %collective-permute-done.14.yodd = f32[16,4,128]{2,1,0:T(4,128)S(1)} collective-permute-done((f32[16,4,128]{2,1,0:T(4,128)S(1)}, f32[16,4,128]{2,1,0:T(4,128)S(1)}, u32[]{:S(2)}, u32[]{:S(2)}) %collective-permute-start.14) | collective-permute-done | bytes 32800 | tf_op jit(solution)/shard_map/ppermute | solution.py:443
  53.2 0.8 shard_map.83
  54.0 1.1 %shard_map.84 = (f32[16,4,80,128]{3,2,1,0:T(8,128)S(1)}, f32[16,4,80,128]{3,2,1,0:T(8,128)S(1)}, f32[256,1,16]{2,1,0:T(1,128)S(1)}) custom-call(f32[24,128]{1,0:T(8,128)S(1)} %get-tuple-element.66.table, f32[16,4,80,128]{3,2,1,0:T(8,128)S(1)} %get-tuple-element.117.own_in, ...), custom_call_target="tpu_custom_call", output_to_operand_aliasing={{0}: (1, {}), {1}: (2, {})} | custom-call | flops 10000000 | bytes 2097152 | tf_op jit(solution)/shard_map/pallas_call | solution.py:369
  55.1 22.8 %all_to_all.5.sums_ref = f32[256,1,16]{2,1,0:T(1,128)S(1)} all-to-all(f32[256,1,16]{2,1,0:T(1,128)S(1)} %get-tuple-element.121), channel_id=1, replica_groups=mesh['gx'=32,'gy'=8] {'gx','gy'}, dimensions={0} | all-to-all | bytes 32768 | tf_op jit(solution)/shard_map/all_to_all | solution.py:485
  78.0 3.0 %shard_map.85 = (bf16[16,4,64,256]{3,2,1,0:T(8,128)(2,1)}, f32[1,16]{1,0:T(1,128)}) custom-call(f32[24,128]{1,0:T(8,128)S(1)} %get-tuple-element.66.table, f32[256,1,16]{2,1,0:T(1,128)S(1)} %all_to_all.5.sums_ref, f32[16,4,80,128]{3,2,1,0:T(8,128)S(1)} %get-tuple-element.122.a0, f32[16,4,80,128]{3,2,1,0:T(8,128)S(1)} %get-tuple-element.123.a1), custom_call_target="tpu_custom_call" | custom-call | flops 10000000 | bytes 2097152 | tf_op jit(solution)/shard_map/pallas_call | solution.py:428
  (31 shorter events, 9.1 us)
Async XLA Ops:
  3.0 18.2 %collective-permute-start = (bf16[16,64,128]{2,1,0:T(8,128)(2,1)S(1)}, bf16[16,64,128]{2,1,0:T(8,128)(2,1)S(1)}, u32[]{:S(2)}, u32[]{:S(2)}) collective-permute-start(bf16[16,64,128]{2,1,0:T(8,128)(2,1)S(1)} %get-tuple-element.71), channel_id=1, source_target_pairs={{0,248},{8,16},{16,8},{24,32},{32,24},{40,48},{48,40},{56,64},{64,... | collective-permute-start | bytes 786440 | tf_op jit(solution)/shard_map/ppermute | solution.py:443
  11.9 11.3 %collective-permute-start.3 = (bf16[16,64,128]{2,1,0:T(8,128)(2,1)S(1)}, bf16[16,64,128]{2,1,0:T(8,128)(2,1)S(1)}, u32[]{:S(2)}, u32[]{:S(2)}) collective-permute-start(bf16[16,64,128]{2,1,0:T(8,128)(2,1)S(1)} %get-tuple-element.76), channel_id=1, source_target_pairs={{0,8},{8,0},{16,24},{24,16},{32,40},{40,32},{48,56},{56,48},{64,72... | collective-permute-start | bytes 786440 | tf_op jit(solution)/shard_map/ppermute | solution.py:443
  11.9 9.2 %collective-permute-start.1 = (f32[16,4,128]{2,1,0:T(4,128)S(1)}, f32[16,4,128]{2,1,0:T(4,128)S(1)}, u32[]{:S(2)}, u32[]{:S(2)}) collective-permute-start(f32[16,4,128]{2,1,0:T(4,128)S(1)} %get-tuple-element.72), channel_id=1, source_target_pairs={{0,1},{1,0},{2,3},{3,2},{4,5},{5,4},{6,7},{7,6},{8,9},{9,8},{10,11... | collective-permute-start | bytes 98312 | tf_op jit(solution)/shard_map/ppermute | solution.py:443
  12.9 8.3 %collective-permute-start.2 = (f32[16,4,128]{2,1,0:T(4,128)S(1)}, f32[16,4,128]{2,1,0:T(4,128)S(1)}, u32[]{:S(2)}, u32[]{:S(2)}) collective-permute-start(f32[16,4,128]{2,1,0:T(4,128)S(1)} %get-tuple-element.73), channel_id=1, source_target_pairs={{0,7},{1,2},{2,1},{3,4},{4,3},{5,6},{6,5},{7,0},{8,15},{9,10},{10,... | collective-permute-start | bytes 98312 | tf_op jit(solution)/shard_map/ppermute | solution.py:443
  14.0 0.7 copy-start
  14.7 0.7 copy-start.1
  21.9 9.5 %collective-permute-start.4 = (bf16[16,64,128]{2,1,0:T(8,128)(2,1)S(1)}, bf16[16,64,128]{2,1,0:T(8,128)(2,1)S(1)}, u32[]{:S(2)}, u32[]{:S(2)}) collective-permute-start(bf16[16,64,128]{2,1,0:T(8,128)(2,1)S(1)} %get-tuple-element.85), channel_id=1, source_target_pairs={{0,248},{8,16},{16,8},{24,32},{32,24},{40,48},{48,40},{56,64},{64,... | collective-permute-start | bytes 786440 | tf_op jit(solution)/shard_map/ppermute | solution.py:443
  24.0 10.8 %collective-permute-start.7 = (bf16[16,64,128]{2,1,0:T(8,128)(2,1)S(1)}, bf16[16,64,128]{2,1,0:T(8,128)(2,1)S(1)}, u32[]{:S(2)}, u32[]{:S(2)}) collective-permute-start(bf16[16,64,128]{2,1,0:T(8,128)(2,1)S(1)} %get-tuple-element.90), channel_id=1, source_target_pairs={{0,8},{8,0},{16,24},{24,16},{32,40},{40,32},{48,56},{56,48},{64,72... | collective-permute-start | bytes 786440 | tf_op jit(solution)/shard_map/ppermute | solution.py:443
  25.1 3.5 %collective-permute-start.5 = (f32[16,4,128]{2,1,0:T(4,128)S(1)}, f32[16,4,128]{2,1,0:T(4,128)S(1)}, u32[]{:S(2)}, u32[]{:S(2)}) collective-permute-start(f32[16,4,128]{2,1,0:T(4,128)S(1)} %get-tuple-element.86), channel_id=1, source_target_pairs={{0,1},{1,0},{2,3},{3,2},{4,5},{5,4},{6,7},{7,6},{8,9},{9,8},{10,11... | collective-permute-start | bytes 98312 | tf_op jit(solution)/shard_map/ppermute | solution.py:443
  27.3 3.6 %collective-permute-start.6 = (f32[16,4,128]{2,1,0:T(4,128)S(1)}, f32[16,4,128]{2,1,0:T(4,128)S(1)}, u32[]{:S(2)}, u32[]{:S(2)}) collective-permute-start(f32[16,4,128]{2,1,0:T(4,128)S(1)} %get-tuple-element.87), channel_id=1, source_target_pairs={{0,7},{1,2},{2,1},{3,4},{4,3},{5,6},{6,5},{7,0},{8,15},{9,10},{10,... | collective-permute-start | bytes 98312 | tf_op jit(solution)/shard_map/ppermute | solution.py:443
  32.2 9.4 %collective-permute-start.8 = (bf16[16,64,128]{2,1,0:T(8,128)(2,1)S(1)}, bf16[16,64,128]{2,1,0:T(8,128)(2,1)S(1)}, u32[]{:S(2)}, u32[]{:S(2)}) collective-permute-start(bf16[16,64,128]{2,1,0:T(8,128)(2,1)S(1)} %get-tuple-element.98), channel_id=1, source_target_pairs={{0,248},{8,16},{16,8},{24,32},{32,24},{40,48},{48,40},{56,64},{64,... | collective-permute-start | bytes 786440 | tf_op jit(solution)/shard_map/ppermute | solution.py:443
  35.5 10.4 %collective-permute-start.11 = (bf16[16,64,128]{2,1,0:T(8,128)(2,1)S(1)}, bf16[16,64,128]{2,1,0:T(8,128)(2,1)S(1)}, u32[]{:S(2)}, u32[]{:S(2)}) collective-permute-start(bf16[16,64,128]{2,1,0:T(8,128)(2,1)S(1)} %get-tuple-element.103), channel_id=1, source_target_pairs={{0,8},{8,0},{16,24},{24,16},{32,40},{40,32},{48,56},{56,48},{64,72... | collective-permute-start | bytes 786440 | tf_op jit(solution)/shard_map/ppermute | solution.py:443
  36.2 3.8 %collective-permute-start.9 = (f32[16,4,128]{2,1,0:T(4,128)S(1)}, f32[16,4,128]{2,1,0:T(4,128)S(1)}, u32[]{:S(2)}, u32[]{:S(2)}) collective-permute-start(f32[16,4,128]{2,1,0:T(4,128)S(1)} %get-tuple-element.99), channel_id=1, source_target_pairs={{0,1},{1,0},{2,3},{3,2},{4,5},{5,4},{6,7},{7,6},{8,9},{9,8},{10,11... | collective-permute-start | bytes 98312 | tf_op jit(solution)/shard_map/ppermute | solution.py:443
  37.9 3.6 %collective-permute-start.10 = (f32[16,4,128]{2,1,0:T(4,128)S(1)}, f32[16,4,128]{2,1,0:T(4,128)S(1)}, u32[]{:S(2)}, u32[]{:S(2)}) collective-permute-start(f32[16,4,128]{2,1,0:T(4,128)S(1)} %get-tuple-element.100), channel_id=1, source_target_pairs={{0,7},{1,2},{2,1},{3,4},{4,3},{5,6},{6,5},{7,0},{8,15},{9,10},{10,... | collective-permute-start | bytes 98312 | tf_op jit(solution)/shard_map/ppermute | solution.py:443
  42.3 10.9 %collective-permute-start.12 = (bf16[16,64,128]{2,1,0:T(8,128)(2,1)S(1)}, bf16[16,64,128]{2,1,0:T(8,128)(2,1)S(1)}, u32[]{:S(2)}, u32[]{:S(2)}) collective-permute-start(bf16[16,64,128]{2,1,0:T(8,128)(2,1)S(1)} %get-tuple-element.113), channel_id=1, source_target_pairs={{0,248},{8,16},{16,8},{24,32},{32,24},{40,48},{48,40},{56,64},{64,... | collective-permute-start | bytes 786440 | tf_op jit(solution)/shard_map/ppermute | solution.py:443
  46.6 7.4 %collective-permute-start.15 = (bf16[16,64,128]{2,1,0:T(8,128)(2,1)S(1)}, bf16[16,64,128]{2,1,0:T(8,128)(2,1)S(1)}, u32[]{:S(2)}, u32[]{:S(2)}) collective-permute-start(bf16[16,64,128]{2,1,0:T(8,128)(2,1)S(1)} %get-tuple-element.119), channel_id=1, source_target_pairs={{0,8},{8,0},{16,24},{24,16},{32,40},{40,32},{48,56},{56,48},{64,72... | collective-permute-start | bytes 786440 | tf_op jit(solution)/shard_map/ppermute | solution.py:443
  47.3 5.0 %collective-permute-start.13 = (f32[16,4,128]{2,1,0:T(4,128)S(1)}, f32[16,4,128]{2,1,0:T(4,128)S(1)}, u32[]{:S(2)}, u32[]{:S(2)}) collective-permute-start(f32[16,4,128]{2,1,0:T(4,128)S(1)} %get-tuple-element.114), channel_id=1, source_target_pairs={{0,1},{1,0},{2,3},{3,2},{4,5},{5,4},{6,7},{7,6},{8,9},{9,8},{10,11... | collective-permute-start | bytes 98312 | tf_op jit(solution)/shard_map/ppermute | solution.py:443
  49.6 3.6 %collective-permute-start.14 = (f32[16,4,128]{2,1,0:T(4,128)S(1)}, f32[16,4,128]{2,1,0:T(4,128)S(1)}, u32[]{:S(2)}, u32[]{:S(2)}) collective-permute-start(f32[16,4,128]{2,1,0:T(4,128)S(1)} %get-tuple-element.115), channel_id=1, source_target_pairs={{0,7},{1,2},{2,1},{3,4},{4,3},{5,6},{6,5},{7,0},{8,15},{9,10},{10,... | collective-permute-start | bytes 98312 | tf_op jit(solution)/shard_map/ppermute | solution.py:443

commit v5 on v4

--- a/solution.py
+++ b/solution.py
@@ -367,7 +367,12 @@
 def sweep_call(kernel, more_ins, more_outs, scratch=()):
     def run(*operands):
         return call(
-            kernel, [STATE] * 2 + more_outs, [VM] * (5 + more_ins), [VM] * (2 + len(more_outs)), scratch, {1: 0, 2: 1}
+            kernel,
+            [STATE] * 2 + more_outs,
+            [VM] * (5 + more_ins),
+            [VM] * (2 + len(more_outs)),
+            scratch,
+            {1: 0, 2: 1},
         )(*operands)
 
     return run
@@ -450,7 +455,9 @@
 
 
 def exchange_rows(even, odd):
-    return swap_pairs(even, "gy", 0), swap_pairs(odd, "gy", 1)
+    even = swap_pairs(even, "gy", 0)
+    odd = swap_pairs(odd, "gy", 1)
+    return even, odd
 
 
 def body(spins, couplings, betas, metro_uniform, swap_uniform):

time: 81.2 us -> 81.2 us (level)
  no operation moved by 1% of the time
where the time goes in v5:
time: 81.2 us; the launch traced here: 81.1 us
  starting transfers between devices  28 us (34%)
  blocking collectives  22.8 us (28%)
  Pallas kernels  22.6 us (28%)
  waiting for transfers between devices  5.3 us (7%)
  local copies, waits for them, and re-layouts  1.31 us (2%)
  between operations  1 us (1%)
    ppermute x16, starting transfers between devices, swap_pairs(): lax.ppermute(x, axis, [(i, ((i + odd ^ 1) - odd) % count) for i in range(...  28 us
    all_to_all x1, blocking collectives, body(): sums = lax.all_to_all(sums, both, 0, 0, tiled=True)  22.8 us
    pallas_call x15, Pallas kernels, run(): call(kernel, [STATE] * 2 + more_outs, [VM] * (5 + more_ins), [VM] * (2 +...  11.4 us
    pallas_call x1, Pallas kernels, run_split_inner(): call(split_inner, [STATE] * 2 + [DRAWS] * 4 + [BONDS] * 2 + [TABLE], [SM]...  5.82 us
    ppermute x16, waiting for transfers between devices, swap_pairs(): lax.ppermute(x, axis, [(i, ((i + odd ^ 1) - odd) % count) for i in range(...  5.3 us
    pallas_call x1, Pallas kernels, run_mix_and_join(): call(functools.partial(mix_and_join, cell_count), [jax.ShapeDtypeStruct((...  2.95 us
    pallas_call x1, Pallas kernels, run_split_outer(): call(split_outer, [STATE] * 2 + [LAYER] * 2 + [ROWS] * 2, [HB], [VM] * 6,...  2.38 us
  transfers between devices with their start and end apart: 16, of which 4 were waited for; matrix products, arithmetic and copies ran while one was open for 0% of the time, Pallas kernels for 20%

profile of v5, /device:TPU:1, one launch (start us, length us, event | category | flops | bytes accessed | tf_op | source)
XLA Modules:
  0.0 81.1 jit_solution(6068844467289545831)
XLA Ops:
  0.6 2.4 %shard_map.68 = (f32[16,4,80,128]{3,2,1,0:T(8,128)S(1)}, f32[16,4,80,128]{3,2,1,0:T(8,128)S(1)}, bf16[16,64,128]{2,1,0:T(8,128)(2,1)S(1)}, bf16[16,64,128]{2,1,0...) custom-call(bf16[16,4,64,256]{3,2,1,0:T(8,128)(2,1)} %spins_ref.3), custom_call_target="tpu_custom_call" | custom-call | flops 10000000 | bytes 2097152 | tf_op jit(solution)/shard_map/pallas_call | solution.py:175
  3.0 8.9 %collective-permute-start = (bf16[16,64,128]{2,1,0:T(8,128)(2,1)S(1)}, bf16[16,64,128]{2,1,0:T(8,128)(2,1)S(1)}, u32[]{:S(2)}, u32[]{:S(2)}) collective-permute-start(bf16[16,64,128]{2,1,0:T(8,128)(2,1)S(1)} %get-tuple-element.71), channel_id=1, source_target_pairs={{0,248},{8,16},{16,8},{24,32},{32,24},{40,48},{48,40},{56,64},{64,... | collective-permute-start | bytes 786440 | tf_op jit(solution)/shard_map/ppermute | solution.py:448
  11.9 1.0 %collective-permute-start.1 = (f32[16,4,128]{2,1,0:T(4,128)S(1)}, f32[16,4,128]{2,1,0:T(4,128)S(1)}, u32[]{:S(2)}, u32[]{:S(2)}) collective-permute-start(f32[16,4,128]{2,1,0:T(4,128)S(1)} %get-tuple-element.72), channel_id=1, source_target_pairs={{0,1},{1,0},{2,3},{3,2},{4,5},{5,4},{6,7},{7,6},{8,9},{9,8},{10,11... | collective-permute-start | bytes 98312 | tf_op jit(solution)/shard_map/ppermute | solution.py:448
  12.9 1.1 %collective-permute-start.2 = (f32[16,4,128]{2,1,0:T(4,128)S(1)}, f32[16,4,128]{2,1,0:T(4,128)S(1)}, u32[]{:S(2)}, u32[]{:S(2)}) collective-permute-start(f32[16,4,128]{2,1,0:T(4,128)S(1)} %get-tuple-element.73), channel_id=1, source_target_pairs={{0,7},{1,2},{2,1},{3,4},{4,3},{5,6},{6,5},{7,0},{8,15},{9,10},{10,... | collective-permute-start | bytes 98312 | tf_op jit(solution)/shard_map/ppermute | solution.py:448
  15.3 5.8 %shard_map.69 = (f32[16,4,80,128]{3,2,1,0:T(8,128)S(1)}, f32[16,4,80,128]{3,2,1,0:T(8,128)S(1)}, f32[16,4,64,128]{3,2,1,0:T(8,128)S(1)}, f32[16,4,64,128]{3,2,1,...) custom-call(f32[16]{0:T(128)S(1)} %copy-done, ...), custom_call_target="tpu_custom_call", output_to_operand_aliasing={{0}: (5, {}), {1}: (6, {})} | custom-call | flops 10000000 | bytes 2097152 | tf_op jit(solution)/shard_map/pallas_call | solution.py:252
  21.9 1.4 %collective-permute-start.4 = (bf16[16,64,128]{2,1,0:T(8,128)(2,1)S(1)}, bf16[16,64,128]{2,1,0:T(8,128)(2,1)S(1)}, u32[]{:S(2)}, u32[]{:S(2)}) collective-permute-start(bf16[16,64,128]{2,1,0:T(8,128)(2,1)S(1)} %get-tuple-element.85), channel_id=1, source_target_pairs={{0,248},{8,16},{16,8},{24,32},{32,24},{40,48},{48,40},{56,64},{64,... | collective-permute-start | bytes 786440 | tf_op jit(solution)/shard_map/ppermute | solution.py:448
  25.1 2.2 %collective-permute-start.5 = (f32[16,4,128]{2,1,0:T(4,128)S(1)}, f32[16,4,128]{2,1,0:T(4,128)S(1)}, u32[]{:S(2)}, u32[]{:S(2)}) collective-permute-start(f32[16,4,128]{2,1,0:T(4,128)S(1)} %get-tuple-element.86), channel_id=1, source_target_pairs={{0,1},{1,0},{2,3},{3,2},{4,5},{5,4},{6,7},{7,6},{8,9},{9,8},{10,11... | collective-permute-start | bytes 98312 | tf_op jit(solution)/shard_map/ppermute | solution.py:448
  27.8 0.9 %shard_map.73 = (f32[16,4,80,128]{3,2,1,0:T(8,128)S(1)}, f32[16,4,80,128]{3,2,1,0:T(8,128)S(1)}) custom-call(f32[24,128]{1,0:T(8,128)S(1)} %get-tuple-element.66.table, f32[16,4,80,128]{3,2,1,0:T(8,128)S(1)} %get-tuple-element.79.own_in, f32[16,4,80,128]{3,2,1,0:T(8,128)S(1)} %get-tuple-element.80.other_in, ...), custom_call_target="tpu_custom_call", output_to_operand_aliasing={{0}: (1, {}), {1}: (2, {})} | custom-call | flops 10000000 | bytes 2097152 | tf_op jit(solution)/shard_map/pallas_call | solution.py:369
  28.7 2.3 %collective-permute-done.6.yodd = f32[16,4,128]{2,1,0:T(4,128)S(1)} collective-permute-done((f32[16,4,128]{2,1,0:T(4,128)S(1)}, f32[16,4,128]{2,1,0:T(4,128)S(1)}, u32[]{:S(2)}, u32[]{:S(2)}) %collective-permute-start.6) | collective-permute-done | bytes 32800 | tf_op jit(solution)/shard_map/ppermute | solution.py:448
  32.2 2.6 %collective-permute-start.8 = (bf16[16,64,128]{2,1,0:T(8,128)(2,1)S(1)}, bf16[16,64,128]{2,1,0:T(8,128)(2,1)S(1)}, u32[]{:S(2)}, u32[]{:S(2)}) collective-permute-start(bf16[16,64,128]{2,1,0:T(8,128)(2,1)S(1)} %get-tuple-element.98), channel_id=1, source_target_pairs={{0,248},{8,16},{16,8},{24,32},{32,24},{40,48},{48,40},{56,64},{64,... | collective-permute-start | bytes 786440 | tf_op jit(solution)/shard_map/ppermute | solution.py:448
  36.2 1.7 %collective-permute-start.9 = (f32[16,4,128]{2,1,0:T(4,128)S(1)}, f32[16,4,128]{2,1,0:T(4,128)S(1)}, u32[]{:S(2)}, u32[]{:S(2)}) collective-permute-start(f32[16,4,128]{2,1,0:T(4,128)S(1)} %get-tuple-element.99), channel_id=1, source_target_pairs={{0,1},{1,0},{2,3},{3,2},{4,5},{5,4},{6,7},{7,6},{8,9},{9,8},{10,11... | collective-permute-start | bytes 98312 | tf_op jit(solution)/shard_map/ppermute | solution.py:448
  37.9 1.2 %collective-permute-start.10 = (f32[16,4,128]{2,1,0:T(4,128)S(1)}, f32[16,4,128]{2,1,0:T(4,128)S(1)}, u32[]{:S(2)}, u32[]{:S(2)}) collective-permute-start(f32[16,4,128]{2,1,0:T(4,128)S(1)} %get-tuple-element.100), channel_id=1, source_target_pairs={{0,7},{1,2},{2,1},{3,4},{4,3},{5,6},{6,5},{7,0},{8,15},{9,10},{10,... | collective-permute-start | bytes 98312 | tf_op jit(solution)/shard_map/ppermute | solution.py:448
  39.1 0.9 %shard_map.77 = (f32[16,4,80,128]{3,2,1,0:T(8,128)S(1)}, f32[16,4,80,128]{3,2,1,0:T(8,128)S(1)}) custom-call(f32[24,128]{1,0:T(8,128)S(1)} %get-tuple-element.66.table, f32[16,4,80,128]{3,2,1,0:T(8,128)S(1)} %get-tuple-element.93.own_in, f32[16,4,80,128]{3,2,1,0:T(8,128)S(1)} %get-tuple-element.94.other_in, ...), custom_call_target="tpu_custom_call", output_to_operand_aliasing={{0}: (1, {}), {1}: (2, {})} | custom-call | flops 10000000 | bytes 2097152 | tf_op jit(solution)/shard_map/pallas_call | solution.py:369
  40.0 1.5 %collective-permute-done.10.yodd = f32[16,4,128]{2,1,0:T(4,128)S(1)} collective-permute-done((f32[16,4,128]{2,1,0:T(4,128)S(1)}, f32[16,4,128]{2,1,0:T(4,128)S(1)}, u32[]{:S(2)}, u32[]{:S(2)}) %collective-permute-start.10) | collective-permute-done | bytes 32800 | tf_op jit(solution)/shard_map/ppermute | solution.py:448
  42.3 3.6 %collective-permute-start.12 = (bf16[16,64,128]{2,1,0:T(8,128)(2,1)S(1)}, bf16[16,64,128]{2,1,0:T(8,128)(2,1)S(1)}, u32[]{:S(2)}, u32[]{:S(2)}) collective-permute-start(bf16[16,64,128]{2,1,0:T(8,128)(2,1)S(1)} %get-tuple-element.113), channel_id=1, source_target_pairs={{0,248},{8,16},{16,8},{24,32},{32,24},{40,48},{48,40},{56,64},{64,... | collective-permute-start | bytes 786440 | tf_op jit(solution)/shard_map/ppermute | solution.py:448
  47.3 2.3 %collective-permute-start.13 = (f32[16,4,128]{2,1,0:T(4,128)S(1)}, f32[16,4,128]{2,1,0:T(4,128)S(1)}, u32[]{:S(2)}, u32[]{:S(2)}) collective-permute-start(f32[16,4,128]{2,1,0:T(4,128)S(1)} %get-tuple-element.114), channel_id=1, source_target_pairs={{0,1},{1,0},{2,3},{3,2},{4,5},{5,4},{6,7},{7,6},{8,9},{9,8},{10,11... | collective-permute-start | bytes 98312 | tf_op jit(solution)/shard_map/ppermute | solution.py:448
  49.6 0.9 %collective-permute-start.14 = (f32[16,4,128]{2,1,0:T(4,128)S(1)}, f32[16,4,128]{2,1,0:T(4,128)S(1)}, u32[]{:S(2)}, u32[]{:S(2)}) collective-permute-start(f32[16,4,128]{2,1,0:T(4,128)S(1)} %get-tuple-element.115), channel_id=1, source_target_pairs={{0,7},{1,2},{2,1},{3,4},{4,3},{5,6},{6,5},{7,0},{8,15},{9,10},{10,... | collective-permute-start | bytes 98312 | tf_op jit(solution)/shard_map/ppermute | solution.py:448
  50.5 0.9 %shard_map.81 = (f32[16,4,80,128]{3,2,1,0:T(8,128)S(1)}, f32[16,4,80,128]{3,2,1,0:T(8,128)S(1)}) custom-call(f32[24,128]{1,0:T(8,128)S(1)} %get-tuple-element.66.table, f32[16,4,80,128]{3,2,1,0:T(8,128)S(1)} %get-tuple-element.106.own_in, f32[16,4,80,128]{3,2,1,0:T(8,128)S(1)} %get-tuple-element.107.other_in, ...), custom_call_target="tpu_custom_call", output_to_operand_aliasing={{0}: (1, {}), {1}: (2, {})} | custom-call | flops 10000000 | bytes 2097152 | tf_op jit(solution)/shard_map/pallas_call | solution.py:369
  51.3 0.9 %shard_map.82 = (f32[16,4,80,128]{3,2,1,0:T(8,128)S(1)}, f32[16,4,80,128]{3,2,1,0:T(8,128)S(1)}, f32[16,8,128]{2,1,0:T(8,128)S(1)}) custom-call(f32[24,128]{1,0:T(8,128)S(1)} %get-tuple-element.66.table, f32[16,4,80,128]{3,2,1,0:T(8,128)S(1)} %get-tuple-element.108.own_in, ...), custom_call_target="tpu_custom_call", output_to_operand_aliasing={{0}: (1, {}), {1}: (2, {})} | custom-call | flops 10000000 | bytes 2097152 | tf_op jit(solution)/shard_map/pallas_call | solution.py:369
  52.3 0.9 %collective-permute-done.14.yodd = f32[16,4,128]{2,1,0:T(4,128)S(1)} collective-permute-done((f32[16,4,128]{2,1,0:T(4,128)S(1)}, f32[16,4,128]{2,1,0:T(4,128)S(1)}, u32[]{:S(2)}, u32[]{:S(2)}) %collective-permute-start.14) | collective-permute-done | bytes 32800 | tf_op jit(solution)/shard_map/ppermute | solution.py:448
  53.2 0.8 shard_map.83
  54.0 1.1 %shard_map.84 = (f32[16,4,80,128]{3,2,1,0:T(8,128)S(1)}, f32[16,4,80,128]{3,2,1,0:T(8,128)S(1)}, f32[256,1,16]{2,1,0:T(1,128)S(1)}) custom-call(f32[24,128]{1,0:T(8,128)S(1)} %get-tuple-element.66.table, f32[16,4,80,128]{3,2,1,0:T(8,128)S(1)} %get-tuple-element.117.own_in, ...), custom_call_target="tpu_custom_call", output_to_operand_aliasing={{0}: (1, {}), {1}: (2, {})} | custom-call | flops 10000000 | bytes 2097152 | tf_op jit(solution)/shard_map/pallas_call | solution.py:369
  55.1 22.8 %all_to_all.5.sums_ref = f32[256,1,16]{2,1,0:T(1,128)S(1)} all-to-all(f32[256,1,16]{2,1,0:T(1,128)S(1)} %get-tuple-element.121), channel_id=1, replica_groups=mesh['gx'=32,'gy'=8] {'gx','gy'}, dimensions={0} | all-to-all | bytes 32768 | tf_op jit(solution)/shard_map/all_to_all | solution.py:492
  78.0 3.0 %shard_map.85 = (bf16[16,4,64,256]{3,2,1,0:T(8,128)(2,1)}, f32[1,16]{1,0:T(1,128)}) custom-call(f32[24,128]{1,0:T(8,128)S(1)} %get-tuple-element.66.table, f32[256,1,16]{2,1,0:T(1,128)S(1)} %all_to_all.5.sums_ref, f32[16,4,80,128]{3,2,1,0:T(8,128)S(1)} %get-tuple-element.122.a0, f32[16,4,80,128]{3,2,1,0:T(8,128)S(1)} %get-tuple-element.123.a1), custom_call_target="tpu_custom_call" | custom-call | flops 10000000 | bytes 2097152 | tf_op jit(solution)/shard_map/pallas_call | solution.py:433
  (31 shorter events, 9.1 us)
Async XLA Ops:
  3.0 18.2 %collective-permute-start = (bf16[16,64,128]{2,1,0:T(8,128)(2,1)S(1)}, bf16[16,64,128]{2,1,0:T(8,128)(2,1)S(1)}, u32[]{:S(2)}, u32[]{:S(2)}) collective-permute-start(bf16[16,64,128]{2,1,0:T(8,128)(2,1)S(1)} %get-tuple-element.71), channel_id=1, source_target_pairs={{0,248},{8,16},{16,8},{24,32},{32,24},{40,48},{48,40},{56,64},{64,... | collective-permute-start | bytes 786440 | tf_op jit(solution)/shard_map/ppermute | solution.py:448
  11.9 11.3 %collective-permute-start.3 = (bf16[16,64,128]{2,1,0:T(8,128)(2,1)S(1)}, bf16[16,64,128]{2,1,0:T(8,128)(2,1)S(1)}, u32[]{:S(2)}, u32[]{:S(2)}) collective-permute-start(bf16[16,64,128]{2,1,0:T(8,128)(2,1)S(1)} %get-tuple-element.76), channel_id=1, source_target_pairs={{0,8},{8,0},{16,24},{24,16},{32,40},{40,32},{48,56},{56,48},{64,72... | collective-permute-start | bytes 786440 | tf_op jit(solution)/shard_map/ppermute | solution.py:448
  11.9 9.2 %collective-permute-start.1 = (f32[16,4,128]{2,1,0:T(4,128)S(1)}, f32[16,4,128]{2,1,0:T(4,128)S(1)}, u32[]{:S(2)}, u32[]{:S(2)}) collective-permute-start(f32[16,4,128]{2,1,0:T(4,128)S(1)} %get-tuple-element.72), channel_id=1, source_target_pairs={{0,1},{1,0},{2,3},{3,2},{4,5},{5,4},{6,7},{7,6},{8,9},{9,8},{10,11... | collective-permute-start | bytes 98312 | tf_op jit(solution)/shard_map/ppermute | solution.py:448
  12.9 8.3 %collective-permute-start.2 = (f32[16,4,128]{2,1,0:T(4,128)S(1)}, f32[16,4,128]{2,1,0:T(4,128)S(1)}, u32[]{:S(2)}, u32[]{:S(2)}) collective-permute-start(f32[16,4,128]{2,1,0:T(4,128)S(1)} %get-tuple-element.73), channel_id=1, source_target_pairs={{0,7},{1,2},{2,1},{3,4},{4,3},{5,6},{6,5},{7,0},{8,15},{9,10},{10,... | collective-permute-start | bytes 98312 | tf_op jit(solution)/shard_map/ppermute | solution.py:448
  14.0 0.7 copy-start
  14.7 0.7 copy-start.1
  21.9 9.5 %collective-permute-start.4 = (bf16[16,64,128]{2,1,0:T(8,128)(2,1)S(1)}, bf16[16,64,128]{2,1,0:T(8,128)(2,1)S(1)}, u32[]{:S(2)}, u32[]{:S(2)}) collective-permute-start(bf16[16,64,128]{2,1,0:T(8,128)(2,1)S(1)} %get-tuple-element.85), channel_id=1, source_target_pairs={{0,248},{8,16},{16,8},{24,32},{32,24},{40,48},{48,40},{56,64},{64,... | collective-permute-start | bytes 786440 | tf_op jit(solution)/shard_map/ppermute | solution.py:448
  24.0 10.8 %collective-permute-start.7 = (bf16[16,64,128]{2,1,0:T(8,128)(2,1)S(1)}, bf16[16,64,128]{2,1,0:T(8,128)(2,1)S(1)}, u32[]{:S(2)}, u32[]{:S(2)}) collective-permute-start(bf16[16,64,128]{2,1,0:T(8,128)(2,1)S(1)} %get-tuple-element.90), channel_id=1, source_target_pairs={{0,8},{8,0},{16,24},{24,16},{32,40},{40,32},{48,56},{56,48},{64,72... | collective-permute-start | bytes 786440 | tf_op jit(solution)/shard_map/ppermute | solution.py:448
  25.1 3.5 %collective-permute-start.5 = (f32[16,4,128]{2,1,0:T(4,128)S(1)}, f32[16,4,128]{2,1,0:T(4,128)S(1)}, u32[]{:S(2)}, u32[]{:S(2)}) collective-permute-start(f32[16,4,128]{2,1,0:T(4,128)S(1)} %get-tuple-element.86), channel_id=1, source_target_pairs={{0,1},{1,0},{2,3},{3,2},{4,5},{5,4},{6,7},{7,6},{8,9},{9,8},{10,11... | collective-permute-start | bytes 98312 | tf_op jit(solution)/shard_map/ppermute | solution.py:448
  27.3 3.6 %collective-permute-start.6 = (f32[16,4,128]{2,1,0:T(4,128)S(1)}, f32[16,4,128]{2,1,0:T(4,128)S(1)}, u32[]{:S(2)}, u32[]{:S(2)}) collective-permute-start(f32[16,4,128]{2,1,0:T(4,128)S(1)} %get-tuple-element.87), channel_id=1, source_target_pairs={{0,7},{1,2},{2,1},{3,4},{4,3},{5,6},{6,5},{7,0},{8,15},{9,10},{10,... | collective-permute-start | bytes 98312 | tf_op jit(solution)/shard_map/ppermute | solution.py:448
  32.2 9.4 %collective-permute-start.8 = (bf16[16,64,128]{2,1,0:T(8,128)(2,1)S(1)}, bf16[16,64,128]{2,1,0:T(8,128)(2,1)S(1)}, u32[]{:S(2)}, u32[]{:S(2)}) collective-permute-start(bf16[16,64,128]{2,1,0:T(8,128)(2,1)S(1)} %get-tuple-element.98), channel_id=1, source_target_pairs={{0,248},{8,16},{16,8},{24,32},{32,24},{40,48},{48,40},{56,64},{64,... | collective-permute-start | bytes 786440 | tf_op jit(solution)/shard_map/ppermute | solution.py:448
  35.5 10.4 %collective-permute-start.11 = (bf16[16,64,128]{2,1,0:T(8,128)(2,1)S(1)}, bf16[16,64,128]{2,1,0:T(8,128)(2,1)S(1)}, u32[]{:S(2)}, u32[]{:S(2)}) collective-permute-start(bf16[16,64,128]{2,1,0:T(8,128)(2,1)S(1)} %get-tuple-element.103), channel_id=1, source_target_pairs={{0,8},{8,0},{16,24},{24,16},{32,40},{40,32},{48,56},{56,48},{64,72... | collective-permute-start | bytes 786440 | tf_op jit(solution)/shard_map/ppermute | solution.py:448
  36.2 3.8 %collective-permute-start.9 = (f32[16,4,128]{2,1,0:T(4,128)S(1)}, f32[16,4,128]{2,1,0:T(4,128)S(1)}, u32[]{:S(2)}, u32[]{:S(2)}) collective-permute-start(f32[16,4,128]{2,1,0:T(4,128)S(1)} %get-tuple-element.99), channel_id=1, source_target_pairs={{0,1},{1,0},{2,3},{3,2},{4,5},{5,4},{6,7},{7,6},{8,9},{9,8},{10,11... | collective-permute-start | bytes 98312 | tf_op jit(solution)/shard_map/ppermute | solution.py:448
  37.9 3.6 %collective-permute-start.10 = (f32[16,4,128]{2,1,0:T(4,128)S(1)}, f32[16,4,128]{2,1,0:T(4,128)S(1)}, u32[]{:S(2)}, u32[]{:S(2)}) collective-permute-start(f32[16,4,128]{2,1,0:T(4,128)S(1)} %get-tuple-element.100), channel_id=1, source_target_pairs={{0,7},{1,2},{2,1},{3,4},{4,3},{5,6},{6,5},{7,0},{8,15},{9,10},{10,... | collective-permute-start | bytes 98312 | tf_op jit(solution)/shard_map/ppermute | solution.py:448
  42.3 10.9 %collective-permute-start.12 = (bf16[16,64,128]{2,1,0:T(8,128)(2,1)S(1)}, bf16[16,64,128]{2,1,0:T(8,128)(2,1)S(1)}, u32[]{:S(2)}, u32[]{:S(2)}) collective-permute-start(bf16[16,64,128]{2,1,0:T(8,128)(2,1)S(1)} %get-tuple-element.113), channel_id=1, source_target_pairs={{0,248},{8,16},{16,8},{24,32},{32,24},{40,48},{48,40},{56,64},{64,... | collective-permute-start | bytes 786440 | tf_op jit(solution)/shard_map/ppermute | solution.py:448
  46.6 7.4 %collective-permute-start.15 = (bf16[16,64,128]{2,1,0:T(8,128)(2,1)S(1)}, bf16[16,64,128]{2,1,0:T(8,128)(2,1)S(1)}, u32[]{:S(2)}, u32[]{:S(2)}) collective-permute-start(bf16[16,64,128]{2,1,0:T(8,128)(2,1)S(1)} %get-tuple-element.119), channel_id=1, source_target_pairs={{0,8},{8,0},{16,24},{24,16},{32,40},{40,32},{48,56},{56,48},{64,72... | collective-permute-start | bytes 786440 | tf_op jit(solution)/shard_map/ppermute | solution.py:448
  47.3 5.0 %collective-permute-start.13 = (f32[16,4,128]{2,1,0:T(4,128)S(1)}, f32[16,4,128]{2,1,0:T(4,128)S(1)}, u32[]{:S(2)}, u32[]{:S(2)}) collective-permute-start(f32[16,4,128]{2,1,0:T(4,128)S(1)} %get-tuple-element.114), channel_id=1, source_target_pairs={{0,1},{1,0},{2,3},{3,2},{4,5},{5,4},{6,7},{7,6},{8,9},{9,8},{10,11... | collective-permute-start | bytes 98312 | tf_op jit(solution)/shard_map/ppermute | solution.py:448
  49.6 3.6 %collective-permute-start.14 = (f32[16,4,128]{2,1,0:T(4,128)S(1)}, f32[16,4,128]{2,1,0:T(4,128)S(1)}, u32[]{:S(2)}, u32[]{:S(2)}) collective-permute-start(f32[16,4,128]{2,1,0:T(4,128)S(1)} %get-tuple-element.115), channel_id=1, source_target_pairs={{0,7},{1,2},{2,1},{3,4},{4,3},{5,6},{6,5},{7,0},{8,15},{9,10},{10,... | collective-permute-start | bytes 98312 | tf_op jit(solution)/shard_map/ppermute | solution.py:448
